TPU v7x, 32 devices: a whole 2x2x4 slice. The times are simulated.
32 devices in a mesh: dp: 16 (over z, y, core), tp: 2 (over x).
Axes of the slice: x: 2, y: 2, z: 4, core: 2. Of those that a mesh axis runs over, the one named last changes fastest.
Arguments:
- decoder_rows: bfloat16 [16, 1024, 768], P('dp', 'tp'), may hold values from -16 to 16
- memory_rows: bfloat16 [16, 2048, 768], P('dp', 'tp'), may hold values from -6 to 6
- output_grad: bfloat16 [16, 1024, 768], P('dp', 'tp'), may hold values from -6 to 6
- token_segments: int32 [16, 1024], P('dp'), may hold values from 0 to 7, never falling along the last dimension, each value on 1 to 256 neighbouring positions
- memory_segments: int32 [16, 2048], P('dp'), may hold values from 0 to 7, never falling along the last dimension, each value on 1 to 512 neighbouring positions
- valid_mask: int32 [16, 1024], P('dp', 'tp'), may hold values from 0 to 1, as said below
- norm_gains: float32 [3, 768], replicated, may hold values from 0.5 to 1.5
- self_project: bfloat16 [3, 768, 768], P(None, None, 'tp'), may hold values from -0.21875 to 0.21875
- self_output: bfloat16 [768, 768], P('tp'), may hold values from -1.25 to 1.25
- cross_query: bfloat16 [768, 768], P(None, 'tp'), may hold values from -0.21875 to 0.21875
- cross_memory: bfloat16 [2, 768, 768], P(None, None, 'tp'), may hold values from -0.21875 to 0.21875
- cross_output: bfloat16 [768, 768], P('tp'), may hold values from -1.75 to 1.75
- gate_up: bfloat16 [2, 768, 2048], P(None, None, 'tp'), may hold values from -0.21875 to 0.21875
- down_weight: bfloat16 [2048, 768], P('tp'), may hold values from -0.125 to 0.125
Outputs:
- decoded: bfloat16 [16, 1024, 768], P('dp', 'tp')
- decoder_grad: float32 [16, 1024, 768], P('dp', 'tp')
- memory_grad: float32 [16, 2048, 768], P('dp', 'tp')
- root_squares: float32 [4], replicated
- gains_grad: float32 [3, 768], replicated
- self_project_grad: float32 [3, 768, 768], P(None, None, 'tp')
- self_output_grad: float32 [768, 768], P('tp')
- cross_query_grad: float32 [768, 768], P(None, 'tp')
- cross_memory_grad: float32 [2, 768, 768], P(None, None, 'tp')
- cross_output_grad: float32 [768, 768], P('tp')
- gate_up_grad: float32 [2, 768, 2048], P(None, None, 'tp')
- down_weight_grad: float32 [2048, 768], P('tp')
Inputs may be any that keep to these rules, and one draw needn't show every extreme that they name: `token_segments`: segment ids never fall along a row, and every id of 0 to 7 occurs in every row. `memory_segments`: segment ids never fall along a row, and every id of 0 to 7 occurs in every row. `valid_mask`: in each row the valid tokens form a prefix of one token or more.
All inputs are finite; a program needn't handle non-finite values.
Results may differ from a plain program's by a relative error of at most 0.019.
The roundings to bfloat16 on the way count: a program that leaves them out, or rounds other values in their place, can miss the bound.
Values may be sent and summed in bfloat16 or wider, within the bound.
No kernel may reach another device: no remote copies, remote signals or barrier semaphores. Data moves between devices by JAX's collectives and lax.ppermute only.
A program may use at most 320 MiB of HBM per device.

v0:
```python
import jax
import jax.numpy as jnp
from jax import lax
from jax.sharding import PartitionSpec as P

HD = 64


EPSILON = 1e-06
NEGATIVE = -1e30


def normalize(vector, factor):
    return vector * lax.rsqrt(jnp.mean(vector * vector, axis=-1, keepdims=True) + EPSILON) * factor


def gated(gate_part, up_part):
    return jax.nn.gelu(gate_part, approximate=True) * up_part


def split_heads(matrix):
    return matrix.reshape(matrix.shape[0], matrix.shape[1], -1, HD)


def join_heads(tensor):
    return tensor.reshape(tensor.shape[0], tensor.shape[1], -1)


def attend_forward(queries, key_rows, values, mask_of):
    length = queries.shape[1]
    block_rows = min(length, 512)
    score_scale = queries.shape[3] ** (-0.5)
    outputs = []
    totals = []
    for offset in range(0, length, block_rows):
        query_block = queries[:, offset : offset + block_rows]
        scores = (
            jnp.einsum("rqhe,rkhe->rhqk", query_block, key_rows, preferred_element_type=jnp.float32)
            * score_scale
        )
        scores = jnp.where(mask_of(offset, block_rows)[:, None], scores, NEGATIVE)
        row_peak = jnp.max(scores, axis=-1, keepdims=True)
        exp_scores = jnp.exp(scores - row_peak)
        row_total = jnp.sum(exp_scores, axis=-1, keepdims=True)
        attn_probs = (exp_scores / row_total).astype(jnp.bfloat16)
        outputs.append(
            jnp.einsum("rhqk,rkhe->rqhe", attn_probs, values, preferred_element_type=jnp.float32)
        )
        totals.append(row_peak + jnp.log(row_total))
    return (jnp.concatenate(outputs, axis=1), jnp.concatenate(totals, axis=2))


def attend_backward(queries, key_rows, values, out_grad, log_totals, mask_of):
    length = queries.shape[1]
    block_rows = min(length, 512)
    score_scale = queries.shape[3] ** (-0.5)
    key_grad = jnp.zeros(key_rows.shape, jnp.float32)
    value_grad = jnp.zeros(values.shape, jnp.float32)
    query_grads = []
    for offset in range(0, length, block_rows):
        query_block = queries[:, offset : offset + block_rows]
        grad_block = out_grad[:, offset : offset + block_rows]
        scores = (
            jnp.einsum("rqhe,rkhe->rhqk", query_block, key_rows, preferred_element_type=jnp.float32)
            * score_scale
        )
        scores = jnp.where(mask_of(offset, block_rows)[:, None], scores, NEGATIVE)
        attn_probs = jnp.exp(scores - log_totals[:, :, offset : offset + block_rows])
        prob_grad = jnp.einsum(
            "rqhe,rkhe->rhqk", grad_block, values, preferred_element_type=jnp.float32
        )
        inner = jnp.sum(prob_grad * attn_probs, axis=-1, keepdims=True)
        score_grad = (attn_probs * (prob_grad - inner)).astype(jnp.bfloat16)
        query_grads.append(
            jnp.einsum("rhqk,rkhe->rqhe", score_grad, key_rows, preferred_element_type=jnp.float32)
            * score_scale
        )
        key_grad = (
            key_grad
            + jnp.einsum(
                "rhqk,rqhe->rkhe", score_grad, query_block, preferred_element_type=jnp.float32
            )
            * score_scale
        )
        value_grad = value_grad + jnp.einsum(
            "rhqk,rqhe->rkhe",
            attn_probs.astype(jnp.bfloat16),
            grad_block,
            preferred_element_type=jnp.float32,
        )
    return (jnp.concatenate(query_grads, axis=1), key_grad, value_grad)


def norm_back(resid, factor, cotangent):
    unused, pull_back = jax.vjp(normalize, resid, factor)
    return pull_back(cotangent)


def spread(resid, factor):
    normed = normalize(resid, factor).astype(jnp.bfloat16)
    return lax.all_gather(normed, "tp", axis=1, tiled=True)


def collect(partial_value):
    return lax.psum_scatter(partial_value, "tp", scatter_dimension=1, tiled=True)


def spread_grad(gradient):
    return lax.all_gather(gradient.astype(jnp.bfloat16), "tp", axis=1, tiled=True)


def collect_grad(partial_value):
    return lax.psum_scatter(partial_value, "tp", scatter_dimension=1, tiled=True)


def heads_here(attended):
    return lax.all_to_all(attended, "tp", split_axis=1, concat_axis=2, tiled=True)


def shards(
    decoder_rows,
    memory_rows,
    output_grad,
    token_segments,
    memory_segments,
    valid_mask,
    norm_gains,
    self_project,
    self_output,
    cross_query,
    cross_memory,
    cross_output,
    gate_up,
    down_weight,
):
    features = decoder_rows.shape[2]
    length = token_segments.shape[1]
    positions = jnp.arange(length, dtype=jnp.int32)

    def self_mask(offset, block_rows):
        query_ids = token_segments[:, offset : offset + block_rows]
        same_table = query_ids[:, :, None] == token_segments[:, None, :]
        causal = positions[offset : offset + block_rows][:, None] >= positions[None, :]
        return same_table & causal[None]

    def cross_mask(offset, block_rows):
        return token_segments[:, offset : offset + block_rows, None] == memory_segments[:, None, :]

    self_output_all, cross_output_all, cross_query_all, cross_memory_all = (
        lax.all_gather(self_output, "tp", axis=0, tiled=True),
        lax.all_gather(cross_output, "tp", axis=0, tiled=True),
        lax.all_gather(cross_query, "tp", axis=1, tiled=True),
        lax.all_gather(cross_memory, "tp", axis=2, tiled=True),
    )
    resid0 = decoder_rows.astype(jnp.float32)
    normed_a = spread(resid0, norm_gains[0])
    proj_a = jnp.einsum(
        "rsd,cdi->crsi", normed_a, self_project, preferred_element_type=jnp.float32
    ).astype(jnp.bfloat16)
    att_a, totals_a = attend_forward(
        split_heads(proj_a[0]), split_heads(proj_a[1]), split_heads(proj_a[2]), self_mask
    )
    att_a = join_heads(att_a).astype(jnp.bfloat16)
    branch_a = jnp.einsum(
        "rsi,id->rsd", heads_here(att_a), self_output_all, preferred_element_type=jnp.float32
    )
    resid1 = resid0 + branch_a
    memory_all = lax.all_gather(memory_rows, "tp", axis=1, tiled=True)
    normed_c = spread(resid1, norm_gains[1])
    query_c = jnp.einsum(
        "rsd,di->rsi", normed_c, cross_query, preferred_element_type=jnp.float32
    ).astype(jnp.bfloat16)
    kv_c = jnp.einsum(
        "rtd,cdi->crti", memory_all, cross_memory, preferred_element_type=jnp.float32
    ).astype(jnp.bfloat16)
    att_c, totals_c = attend_forward(
        split_heads(query_c), split_heads(kv_c[0]), split_heads(kv_c[1]), cross_mask
    )
    att_c = join_heads(att_c).astype(jnp.bfloat16)
    branch_c = jnp.einsum(
        "rsi,id->rsd", heads_here(att_c), cross_output_all, preferred_element_type=jnp.float32
    )
    resid2 = resid1 + branch_c
    normed_m = spread(resid2, norm_gains[2])
    gate_values = jnp.einsum("rsd,cdf->crsf", normed_m, gate_up, preferred_element_type=jnp.float32)
    hidden = gated(gate_values[0], gate_values[1]).astype(jnp.bfloat16)
    branch_m = collect(
        jnp.einsum("rsf,fd->rsd", hidden, down_weight, preferred_element_type=jnp.float32)
    )
    result = resid2 + branch_m
    valid_rows = valid_mask.astype(jnp.float32)[..., None]
    partial_stats = jnp.stack(
        [
            jnp.sum(result * result * valid_rows),
            jnp.sum(branch_a * branch_a * valid_rows),
            jnp.sum(branch_c * branch_c * valid_rows),
            jnp.sum(branch_m * branch_m * valid_rows),
            jnp.sum(valid_rows),
        ]
    )
    stat_totals = lax.psum(partial_stats, ("dp", "tp"))
    grad_m = output_grad.astype(jnp.float32) * valid_rows
    full_m = spread_grad(grad_m)
    down_weight_grad = jnp.einsum("rsf,rsd->fd", hidden, full_m, preferred_element_type=jnp.float32)
    hidden_grad = jnp.einsum("rsd,fd->rsf", full_m, down_weight, preferred_element_type=jnp.float32)
    unused, pull_gate = jax.vjp(gated, gate_values[0], gate_values[1])
    gate_grad, up_grad = pull_gate(hidden_grad)
    gate_grads = jnp.stack([gate_grad, up_grad]).astype(jnp.bfloat16)
    gate_up_grad = jnp.einsum(
        "rsd,crsf->cdf", normed_m, gate_grads, preferred_element_type=jnp.float32
    )
    normed_m_grad = collect_grad(
        jnp.einsum("crsf,cdf->rsd", gate_grads, gate_up, preferred_element_type=jnp.float32)
    )
    resid2_grad, gain_m_grad = norm_back(resid2, norm_gains[2], normed_m_grad)
    grad_c = grad_m + resid2_grad
    full_c = spread_grad(grad_c)
    cross_output_grad = jnp.einsum("rsi,rsd->id", att_c, full_c, preferred_element_type=jnp.float32)
    att_c_grad = jnp.einsum(
        "rsd,id->rsi", full_c, cross_output, preferred_element_type=jnp.float32
    ).astype(jnp.bfloat16)
    query_part, key_part, value_part = attend_backward(
        split_heads(query_c),
        split_heads(kv_c[0]),
        split_heads(kv_c[1]),
        split_heads(att_c_grad),
        totals_c,
        cross_mask,
    )
    query_c_grad = join_heads(query_part).astype(jnp.bfloat16)
    kv_c_grad = jnp.stack([join_heads(key_part), join_heads(value_part)]).astype(jnp.bfloat16)
    cross_query_grad = jnp.einsum(
        "rsd,rsi->di", normed_c, query_c_grad, preferred_element_type=jnp.float32
    )
    cross_memory_grad = jnp.einsum(
        "rtd,crti->cdi", memory_all, kv_c_grad, preferred_element_type=jnp.float32
    )
    query_here, key_here, value_here = (
        lax.all_to_all(query_c_grad, "tp", split_axis=1, concat_axis=2, tiled=True),
        lax.all_to_all(kv_c_grad[0], "tp", split_axis=1, concat_axis=2, tiled=True),
        lax.all_to_all(kv_c_grad[1], "tp", split_axis=1, concat_axis=2, tiled=True),
    )
    memory_grad = jnp.einsum(
        "rti,di->rtd", key_here, cross_memory_all[0], preferred_element_type=jnp.float32
    ) + jnp.einsum(
        "rti,di->rtd", value_here, cross_memory_all[1], preferred_element_type=jnp.float32
    )
    normed_c_grad = jnp.einsum(
        "rsi,di->rsd", query_here, cross_query_all, preferred_element_type=jnp.float32
    )
    resid1_grad, gain_c_grad = norm_back(resid1, norm_gains[1], normed_c_grad)
    grad_a = grad_c + resid1_grad
    full_a = spread_grad(grad_a)
    self_output_grad = jnp.einsum("rsi,rsd->id", att_a, full_a, preferred_element_type=jnp.float32)
    att_a_grad = jnp.einsum(
        "rsd,id->rsi", full_a, self_output, preferred_element_type=jnp.float32
    ).astype(jnp.bfloat16)
    query_part, key_part, value_part = attend_backward(
        split_heads(proj_a[0]),
        split_heads(proj_a[1]),
        split_heads(proj_a[2]),
        split_heads(att_a_grad),
        totals_a,
        self_mask,
    )
    proj_a_grad = jnp.stack(
        [join_heads(query_part), join_heads(key_part), join_heads(value_part)]
    ).astype(jnp.bfloat16)
    self_project_grad = jnp.einsum(
        "rsd,crsi->cdi", normed_a, proj_a_grad, preferred_element_type=jnp.float32
    )
    normed_a_grad = collect_grad(
        jnp.einsum("crsi,cdi->rsd", proj_a_grad, self_project, preferred_element_type=jnp.float32)
    )
    resid0_grad, gain_a_grad = norm_back(resid0, norm_gains[0], normed_a_grad)
    decoder_grad = grad_a + resid0_grad
    (
        self_project_grad,
        self_output_grad,
        cross_query_grad,
        cross_memory_grad,
        cross_output_grad,
        gate_up_grad,
        down_weight_grad,
    ) = lax.psum(
        (
            self_project_grad,
            self_output_grad,
            cross_query_grad,
            cross_memory_grad,
            cross_output_grad,
            gate_up_grad,
            down_weight_grad,
        ),
        "dp",
    )
    gain_partial = jnp.stack([gain_a_grad, gain_c_grad, gain_m_grad])
    gains_grad = lax.psum(gain_partial, ("dp", "tp"))
    root_squares = jnp.sqrt(stat_totals[:4] / (stat_totals[4] * features))
    return (
        result.astype(jnp.bfloat16),
        decoder_grad,
        memory_grad,
        root_squares,
        gains_grad,
        self_project_grad,
        self_output_grad,
        cross_query_grad,
        cross_memory_grad,
        cross_output_grad,
        gate_up_grad,
        down_weight_grad,
    )


def solution(mesh):
    return jax.shard_map(
        shards,
        mesh=mesh,
        in_specs=(
            P("dp", "tp", None),
            P("dp", "tp", None),
            P("dp", "tp", None),
            P("dp", None),
            P("dp", None),
            P("dp", "tp"),
            P(),
            P(None, None, "tp"),
            P("tp", None),
            P(None, "tp"),
            P(None, None, "tp"),
            P("tp", None),
            P(None, None, "tp"),
            P("tp", None),
        ),
        out_specs=(
            P("dp", "tp", None),
            P("dp", "tp", None),
            P("dp", "tp", None),
            P(),
            P(),
            P(None, None, "tp"),
            P("tp", None),
            P(None, "tp"),
            P(None, None, "tp"),
            P("tp", None),
            P(None, None, "tp"),
            P("tp", None),
        ),
        check_vma=False,
    )
```

profile of v0, /device:TPU:0, one launch (start us, length us, event | category | flops | bytes accessed | tf_op | source)
XLA Modules:
  0.0 1098.0 jit_solution(16562146856251424584)
XLA Ops:
  17.3 26.5 %all-gather.12.cloned.1.call-done = bf16[1,1024,768]{2,1,0:T(8,128)(2,1)} async-done(((bf16[1,512,768]{2,1,0:T(8,128)(2,1)}), bf16[1,1024,768]{2,1,0:T(8,128)(2,1)}) %all-gather.12.cloned.1.call-update) | async-done | bytes 1572880 | tf_op jit(solution)/shard_map/all_gather | solution.py:101
  43.7 4.0 convert_bitcast_fusion
  67.2 4.9 copy.85
  72.6 7.3 reduce.44
  81.9 24.6 %all_to_all.75 = bf16[2,2,98304]{2,1,0:T(2,128)(2,1)} all-to-all(bf16[2,2,98304]{2,1,0:T(2,128)(2,1)} %reshape.1046), channel_id=1, replica_groups=mesh['dp'=16,'tp'=2] {'tp'}, dimensions={0} | all-to-all | bytes 1572864 | tf_op jit(solution)/shard_map/all_to_all | solution.py:117
  113.8 3.7 multiply_reduce_fusion.11
  123.0 4.9 fusion.49
  129.8 22.4 %all-gather.18.cloned.1.call-done = bf16[1,1024,768]{2,1,0:T(8,128)(2,1)} async-done(((bf16[1,512,768]{2,1,0:T(8,128)(2,1)}), bf16[1,1024,768]{2,1,0:T(8,128)(2,1)}) %all-gather.18.cloned.1.call-update) | async-done | bytes 1572880 | tf_op jit(solution)/shard_map/all_gather | solution.py:101
  154.8 11.1 %fusion.174 = (f32[6,512]{1,0:T(8,128)S(1)}, f32[6,512,2048]{2,1,0:T(8,128)}) fusion(bf16[2048,6,64]{0,2,1:T(8,128)(2,1)S(1)} %bitcast.353, bf16[1,1024,6,64]{1,3,2,0:T(8,128)(2,1)S(1)} %bitcast.390, pred[512,2048]{1,0:T(8,128)(4,1)S(1)} %copy-done.21), kind=kOutput, calls=%fused_computation.253 | convolution fusion | flops 824177664 | bytes 28192768 | tf_op jit(solution)/shard_map/rqhe,rkhe->rhqk/dot_general | solution.py:38
  165.9 10.8 fusion.175
  176.7 10.5 fusion.1
  187.2 10.6 fusion.126
  197.8 10.8 fusion
  208.7 10.6 fusion.127
  220.3 4.8 copy.88
  225.0 7.3 reduce.45
  234.3 15.5 %all_to_all.76 = bf16[2,2,98304]{2,1,0:T(2,128)(2,1)} all-to-all(bf16[2,2,98304]{2,1,0:T(2,128)(2,1)} %reshape.1048), channel_id=1, replica_groups=mesh['dp'=16,'tp'=2] {'tp'}, dimensions={0} | all-to-all | bytes 1572864 | tf_op jit(solution)/shard_map/all_to_all | solution.py:117
  257.0 4.0 multiply_reduce_fusion.10
  265.9 24.8 %all-gather.22.cloned.1.call-done = bf16[1,1024,768]{2,1,0:T(8,128)(2,1)} async-done(((bf16[1,512,768]{2,1,0:T(8,128)(2,1)}), bf16[1,1024,768]{2,1,0:T(8,128)(2,1)}) %all-gather.22.cloned.1.call-update) | async-done | bytes 1572880 | tf_op jit(solution)/shard_map/all_gather | solution.py:101
  290.8 4.9 convolution_bitcast_fusion
  298.9 4.0 fusion.69
  303.0 17.1 %all-gather.24.cloned.1.call-done = bf16[1,1024,768]{2,1,0:T(8,128)(2,1)} async-done(((bf16[1,512,768]{2,1,0:T(8,128)(2,1)}), bf16[1,1024,768]{2,1,0:T(8,128)(2,1)}) %all-gather.24.cloned.1.call-update) | async-done | bytes 1572880 | tf_op jit(solution)/shard_map/all_gather | solution.py:109
  320.1 8.2 fusion.68
  330.5 5.1 fusion.72
  335.7 30.6 %reduce-scatter.4.cloned.1.call-done = f32[1,512,768]{2,1,0:T(8,128)} async-done(((f32[1,1024,768]{2,1,0:T(8,128)}), f32[1,512,768]{2,1,0:T(8,128)}) %reduce-scatter.4.cloned.1.call-update) | async-done | bytes 1572880 | tf_op jit(solution)/shard_map/reduce_scatter | solution.py:105
  366.3 46.3 %reduce-scatter.6.cloned.1.call-done = f32[1,512,768]{2,1,0:T(8,128)} async-done(((f32[1,1024,768]{2,1,0:T(8,128)}), f32[1,512,768]{2,1,0:T(8,128)}) %reduce-scatter.6.cloned.1.call-update) | async-done | bytes 1572880 | tf_op jit(solution)/shard_map/reduce_scatter | solution.py:113
  412.6 4.5 multiply_reduce_fusion.5
  421.3 26.3 %all-gather.26.cloned.1.call-done = bf16[1,1024,768]{2,1,0:T(8,128)(2,1)} async-done(((bf16[1,512,768]{2,1,0:T(8,128)(2,1)}), bf16[1,1024,768]{2,1,0:T(8,128)(2,1)}) %all-gather.26.cloned.1.call-update) | async-done | bytes 1572880 | tf_op jit(solution)/shard_map/all_gather | solution.py:109
  450.0 20.0 %multiply_reduce_fusion = (f32[6,512]{1,0:T(8,128)S(1)}, f32[6,512,2048]{2,1,0:T(8,128)}) fusion(f32[6,512,2048]{2,1,0:T(8,128)} %get-tuple-element.124, f32[6,512]{1,0:T(8,128)S(1)} %log_add_fusion.2, bf16[2048,6,64]{0,2,1:T(8,128)(2,1)S(1)} %bitcast.363, bf16[1,1024,6,64]{1,3,2,0:T(8,128)(2,1)S(1)} %bitcast.394), kind=kOutput, calls=%fused_computation.1 | convolution fusion | flops 824177664 | bytes 52326400 | tf_op jit(solution)/shard_map/rqhe,rkhe->rhqk/dot_general | solution.py:69
  470.0 21.6 %multiply_convert_fusion = bf16[6,512,2048]{2,1,0:T(8,128)(2,1)} fusion(f32[6,512,2048]{2,1,0:T(8,128)} %get-tuple-element.129, f32[6,512,2048]{2,1,0:T(8,128)} %get-tuple-element.124, f32[6,512]{1,0:T(8,128)S(1)} %get-tuple-element.128, f32[6,512]{1,0:T(8,128)S(1)} %log_add_fusion.2), kind=kLoop, calls=%fused_computation | loop fusion | flops 25165824 | bytes 62939136 | tf_op jit(solution)/shard_map/convert_element_type | solution.py:73
  491.6 8.5 fusion.121
  500.1 16.4 %multiply_reduce_fusion.1 = (f32[6,512]{1,0:T(8,128)}, f32[6,512,2048]{2,1,0:T(8,128)}) fusion(f32[6,512,2048]{2,1,0:T(8,128)} %get-tuple-element.126, f32[6,512]{1,0:T(8,128)S(1)} %log_add_fusion.3, bf16[2048,6,64]{0,2,1:T(8,128)(2,1)S(1)} %bitcast.364, bf16[1,1024,6,64]{1,3,2,0:T(8,128)(2,1)} %bitcast.395), kind=kOutput, calls=%fused_computation.4 | convolution fusion | flops 824177664 | bytes 52322304 | tf_op jit(solution)/shard_map/rqhe,rkhe->rhqk/dot_general | solution.py:69
  516.5 21.8 %multiply_convert_fusion.1 = bf16[6,512,2048]{2,1,0:T(8,128)(2,1)} fusion(f32[6,512,2048]{2,1,0:T(8,128)} %get-tuple-element.131, f32[6,512,2048]{2,1,0:T(8,128)} %get-tuple-element.126, f32[6,512]{1,0:T(8,128)} %get-tuple-element.130, f32[6,512]{1,0:T(8,128)S(1)} %log_add_fusion.3), kind=kLoop, calls=%fused_computation.3 | loop fusion | flops 25165824 | bytes 62939136 | tf_op jit(solution)/shard_map/convert_element_type | solution.py:73
  538.3 8.5 fusion.120
  549.2 5.4 reduce.46
  554.9 14.2 %all_to_all.77 = bf16[2,2,98304]{2,1,0:T(2,128)(2,1)} all-to-all(bf16[2,2,98304]{2,1,0:T(2,128)(2,1)S(1)} %reshape.1050), channel_id=1, replica_groups=mesh['dp'=16,'tp'=2] {'tp'}, dimensions={0} | all-to-all | bytes 1572864 | tf_op jit(solution)/shard_map/all_to_all | solution.py:239
  583.1 8.6 fusion.60
  591.7 15.1 %all-gather.30.cloned.1.call-done = bf16[1,1024,768]{2,1,0:T(8,128)(2,1)} async-done(((bf16[1,512,768]{2,1,0:T(8,128)(2,1)}), bf16[1,1024,768]{2,1,0:T(8,128)(2,1)}) %all-gather.30.cloned.1.call-update) | async-done | bytes 1572880 | tf_op jit(solution)/shard_map/all_gather | solution.py:109
  609.1 5.9 fusion.16
  615.1 11.0 %multiply_reduce_fusion.2 = (f32[6,512]{1,0:T(8,128)}, f32[6,512,1024]{2,1,0:T(8,128)}) fusion(f32[6,512,1024]{2,1,0:T(8,128)} %copy-done.3, f32[6,512]{1,0:T(8,128)S(1)} %copy-done.63, bf16[1024,6,64]{0,2,1:T(8,128)(2,1)S(1)} %bitcast.375, bf16[1,1024,6,64]{1,3,2,0:T(8,128)(2,1)S(1)} %bitcast.409), kind=kOutput, calls=%fused_computation.19 | convolution fusion | flops 412087296 | bytes 26374144 | tf_op jit(solution)/shard_map/rqhe,rkhe->rhqk/dot_general | solution.py:69
  626.1 6.8 multiply_reduce_fusion.3
  636.4 9.8 multiply_convert_fusion.2
  650.6 6.5 multiply_convert_fusion.3
  663.5 5.1 fusion.128
  671.8 5.7 convolution_bitcast_fusion.2
  678.9 8.7 fusion.56
  691.4 6.9 fusion.141
  700.8 10.9 fusion.4
  711.8 10.7 add_convert_fusion
  722.5 6.5 fusion.75
  731.6 3.9 convolution_bitcast_fusion.1
  735.6 8.0 copy.97
  743.6 34.6 %reduce.48 = bf16[2048,384]{1,0:T(8,128)(2,1)} reduce(bf16[2048,1,384]{2,1,0:T(2,128)(2,1)S(1)} %bitcast.366, bf16[]{:T(256)} %broadcast.485), dimensions={1}, to_apply=%bitcast.282.reduce_sub_computation | reduce | bytes 3145730
  780.7 4.6 all-to-all-start.4
  785.3 8.0 copy.95
  793.3 34.4 %reduce.47 = bf16[2048,384]{1,0:T(8,128)(2,1)} reduce(bf16[2048,1,384]{2,1,0:T(2,128)(2,1)S(1)} %bitcast.365, bf16[]{:T(256)} %broadcast.485), dimensions={1}, to_apply=%bitcast.280.reduce_sub_computation | reduce | bytes 3145730
  830.4 4.8 all-to-all-start.3
  846.9 7.9 all-to-all-done.3
  860.5 4.5 fusion.130
  867.1 6.8 add_bitcast_fusion
  873.8 41.4 %all-reduce = (f32[5]{0:T(128)S(1)}, f32[3,768]{1,0:T(4,128)}) all-reduce(f32[5]{0:T(128)S(1)} %stack.63, f32[3,768]{1,0:T(4,128)S(1)} %pad_maximum_fusion.14), channel_id=1, replica_groups=mesh['dp'=16,'tp'=2] {'dp','tp'}, use_global_device_ids=true, to_apply=%region_26.27 | all-reduce | flops 2309 | bytes 18472 | tf_op jit(solution)/shard_map/psum | solution.py:201
  920.0 151.4 %all-reduce.4.cloned.1.call-done = (f32[3,768,384]{1,2,0:T(8,128)}, f32[384,768]{1,0:T(8,128)}, f32[768,384]{1,0:T(8,128)}, f32[2,768,384]{1,2,0:T(8,128)}, f32[...) async-done(((f32[3,768,384]{1,2,0:T(8,128)}, f32[384,768]{1,0:T(8,128)}, f32[768,384]{1,0:T(8,128)}, f32[2,768,384]{1,2,0:T(8,128)}, ...) | async-done | bytes 18874384 | tf_op jit(solution)/shard_map/psum | solution.py:285
  1071.4 5.3 copy.101
  1078.6 6.7 copy.103
  (347 shorter events, 158.6 us)
Async XLA Ops:
  7.2 283.6 %copy-start = (bf16[2,768,1024]{2,1,0:T(8,128)(2,1)S(1)}, bf16[2,768,1024]{2,1,0:T(8,128)(2,1)}, u32[]{:S(2)}) copy-start(bf16[2,768,1024]{2,1,0:T(8,128)(2,1)} %param.26) | copy-start | bytes 9437188
  7.2 8.1 copy-start.85
  7.2 36.5 %all-gather.12.cloned.1.call-start = ((), (), s32[]{:S(2)}) async-start(), calls=%async_computation.8 | async-start | bytes 2359296 | tf_op jit(solution)/shard_map/all_gather | solution.py:101
  10.8 107.3 %copy-start.74 = (f32[768]{0:T(1024)}, f32[768]{0:T(1024)S(1)}, u32[]{:S(2)}) copy-start(f32[768]{0:T(1024)S(1)} %get-tuple-element.84) | copy-start | bytes 9220
  13.7 100.1 %all-gather.14.cloned.1.call-start = ((), (), s32[]{:S(2)}) async-start(), calls=%async_computation.9 | async-start | bytes 1769472 | tf_op jit(solution)/shard_map/all_gather | solution.py:150
  14.4 108.6 %all-gather.16.cloned.1.call-start = ((), (), s32[]{:S(2)}) async-start(), calls=%async_computation.10 | async-start | bytes 4718592 | tf_op jit(solution)/shard_map/all_gather | solution.py:168
  15.2 137.1 %all-gather.18.cloned.1.call-start = ((), (), s32[]{:S(2)}) async-start(), calls=%async_computation.11 | async-start | bytes 2359296 | tf_op jit(solution)/shard_map/all_gather | solution.py:101
  48.0 14.8 %copy-start.22 = (bf16[1,1,1024,384]{2,3,0,1:T(8,128)(2,1)}, bf16[1,1,1024,384]{2,3,0,1:T(8,128)(2,1)S(1)}, u32[]{:S(2)}) copy-start(bf16[1,1,1024,384]{2,3,0,1:T(8,128)(2,1)S(1)} %get-tuple-element.111) | copy-start | bytes 2359300
  53.7 9.1 copy-start.2
  53.7 9.1 copy-start.65
  119.8 137.3 %all-gather.20.cloned.1.call-start = ((), (), s32[]{:S(2)}) async-start(), calls=%async_computation.12 | async-start | bytes 1769472 | tf_op jit(solution)/shard_map/all_gather | solution.py:151
  120.4 170.4 %all-gather.22.cloned.1.call-start = ((), (), s32[]{:S(2)}) async-start(), calls=%async_computation.13 | async-start | bytes 2359296 | tf_op jit(solution)/shard_map/all_gather | solution.py:101
  154.8 11.2 %copy-start.31 = (bf16[1024,384]{0,1:T(8,128)(2,1)}, bf16[1024,384]{0,1:T(8,128)(2,1)S(1)}, u32[]{:S(2)}) copy-start(bf16[1024,384]{0,1:T(8,128)(2,1)S(1)} %fusion.111) | copy-start | bytes 2359300
  154.8 11.1 %copy-start.20 = (pred[512,2048]{1,0:T(8,128)(4,1)S(1)}, pred[512,2048]{1,0:T(8,128)(4,1)}, u32[]{:S(2)}) copy-start(pred[512,2048]{1,0:T(8,128)(4,1)} %get-tuple-element.112) | copy-start | bytes 3145732
  176.7 10.5 copy-start.16
  197.8 21.4 %copy-start.55 = (bf16[6,64,512]{2,1,0:T(8,128)(2,1)}, bf16[6,64,512]{2,1,0:T(8,128)(2,1)S(1)}, u32[]{:S(2)}) copy-start(bf16[6,64,512]{2,1,0:T(8,128)(2,1)S(1)} %fusion.126) | copy-start | bytes 1179652
  263.4 56.7 %all-gather.24.cloned.1.call-start = ((), (), s32[]{:S(2)}) async-start(), calls=%async_computation.15 | async-start | bytes 2359296 | tf_op jit(solution)/shard_map/all_gather | solution.py:109
  263.5 153.7 %copy-start.72 = (f32[1,512]{1,0:T(1,128)}, f32[1,512]{1,0:T(1,128)S(1)}, u32[]{:S(2)}) copy-start(f32[1,512]{1,0:T(1,128)S(1)} %convert_element_type.215) | copy-start | bytes 6148
  265.7 100.6 %reduce-scatter.4.cloned.1.call-start = ((), (), s32[]{:S(2)}) async-start(), calls=%async_computation.14 | async-start | bytes 4718592 | tf_op jit(solution)/shard_map/reduce_scatter | solution.py:105
  290.8 8.2 copy-start.90
  303.0 109.6 %reduce-scatter.6.cloned.1.call-start = ((), (), s32[]{:S(2)}) async-start(), calls=%async_computation.16 | async-start | bytes 4718592 | tf_op jit(solution)/shard_map/reduce_scatter | solution.py:113
  335.6 77.0 %copy-start.12 = (f32[1,512,768]{2,1,0:T(8,128)S(1)}, f32[1,512,768]{2,1,0:T(8,128)}, u32[]{:S(2)}) copy-start(f32[1,512,768]{2,1,0:T(8,128)} %copy-done.11) | copy-start | bytes 4718596
  335.7 111.9 %all-gather.26.cloned.1.call-start = ((), (), s32[]{:S(2)}) async-start(), calls=%async_computation.17 | async-start | bytes 2359296 | tf_op jit(solution)/shard_map/all_gather | solution.py:109
  420.2 29.8 %copy-start.17 = (bf16[1,1,2048,384]{2,3,0,1:T(8,128)(2,1)S(1)}, bf16[1,1,2048,384]{2,3,0,1:T(8,128)(2,1)}, u32[]{:S(2)}) copy-start(bf16[1,1,2048,384]{2,3,0,1:T(8,128)(2,1)} %get-tuple-element.108) | copy-start | bytes 4718596
  420.2 154.1 %all-gather.28.cloned.1.call-start = ((), (), s32[]{:S(2)}) async-start(), calls=%async_computation.18 | async-start | bytes 1769472 | tf_op jit(solution)/shard_map/all_gather | solution.py:152
  421.0 185.8 %all-gather.30.cloned.1.call-start = ((), (), s32[]{:S(2)}) async-start(), calls=%async_computation.19 | async-start | bytes 2359296 | tf_op jit(solution)/shard_map/all_gather | solution.py:109
  421.3 48.8 %copy-start.59 = (f32[6,512]{1,0:T(8,128)}, f32[6,512]{1,0:T(8,128)S(1)}, u32[]{:S(2)}) copy-start(f32[6,512]{1,0:T(8,128)S(1)} %log_add_fusion.2) | copy-start | bytes 36868
  450.0 20.1 %copy-start.33 = (bf16[1024,384]{0,1:T(8,128)(2,1)}, bf16[1024,384]{0,1:T(8,128)(2,1)S(1)}, u32[]{:S(2)}) copy-start(bf16[1024,384]{0,1:T(8,128)(2,1)S(1)} %fusion.114) | copy-start | bytes 2359300
  470.0 21.6 %copy-start.8 = (bf16[1,1,2048,384]{2,3,0,1:T(8,128)(2,1)S(1)}, bf16[1,1,2048,384]{2,3,0,1:T(8,128)(2,1)}, u32[]{:S(2)}) copy-start(bf16[1,1,2048,384]{2,3,0,1:T(8,128)(2,1)} %get-tuple-element.107) | copy-start | bytes 4718596
  579.4 281.0 %all-gather.32.cloned.1.call-start = ((), (), s32[]{:S(2)}) async-start(), calls=%async_computation.21 | async-start | bytes 3538944 | tf_op jit(solution)/shard_map/all_gather | solution.py:153
  580.2 284.8 %reduce-scatter.8.cloned.1.call-start = ((), (), s32[]{:S(2)}) async-start(), calls=%async_computation.20 | async-start | bytes 4718592 | tf_op jit(solution)/shard_map/reduce_scatter | solution.py:113
  583.1 23.7 %copy-start.50 = (bf16[384,768]{1,0:T(8,128)(2,1)S(1)}, bf16[384,768]{1,0:T(8,128)(2,1)}, u32[]{:S(2)}) copy-start(bf16[384,768]{1,0:T(8,128)(2,1)} %param.22) | copy-start | bytes 1769476
  609.1 17.0 %slice-start = ((s8[12582912]{0:T(1024)(128)(4,1)}), s8[4194304]{0:T(1024)(128)(4,1)S(1)}, s32[]{:S(2)}) async-start(s8[12582912]{0:T(1024)(128)(4,1)} %bitcast.347), calls=%async_computation.23 | async-start | bytes 8388608
  609.1 17.0 %slice-start.1 = ((s8[12582912]{0:T(1024)(128)(4,1)}), s8[4194304]{0:T(1024)(128)(4,1)S(1)}, s32[]{:S(2)}) async-start(s8[12582912]{0:T(1024)(128)(4,1)} %bitcast.347), calls=%async_computation.24 | async-start | bytes 8388608
  615.0 11.0 %slice-start.2 = ((s8[12582912]{0:T(1024)(128)(4,1)}), s8[4194304]{0:T(1024)(128)(4,1)S(1)}, s32[]{:S(2)}) async-start(s8[12582912]{0:T(1024)(128)(4,1)} %bitcast.347), calls=%async_computation.25 | async-start | bytes 8388608
  615.1 11.0 %copy-start.61 = (f32[6,512]{1,0:T(8,128)S(1)}, f32[6,512]{1,0:T(8,128)}, u32[]{:S(2)}) copy-start(f32[6,512]{1,0:T(8,128)} %log_add_fusion.1) | copy-start | bytes 36868
  636.4 9.8 slice-start.3
  636.4 10.7 slice-start.4
  636.4 14.2 %slice-start.5 = ((s8[12582912]{0:T(1024)(128)(4,1)}), s8[4194304]{0:T(1024)(128)(4,1)S(1)}, s32[]{:S(2)}) async-start(s8[12582912]{0:T(1024)(128)(4,1)} %bitcast.349), calls=%async_computation.28 | async-start | bytes 8388608
  636.4 14.2 %copy-start.62 = (f32[6,512]{1,0:T(8,128)S(1)}, f32[6,512]{1,0:T(8,128)}, u32[]{:S(2)}) copy-start(f32[6,512]{1,0:T(8,128)} %log_add_fusion.1) | copy-start | bytes 36868
  636.4 14.2 %copy-start.66 = (f32[6,512]{1,0:T(8,128)S(1)}, f32[6,512]{1,0:T(8,128)}, u32[]{:S(2)}) copy-start(f32[6,512]{1,0:T(8,128)} %get-tuple-element.133) | copy-start | bytes 36868
  646.2 12.1 %copy-start.4 = (bf16[6,512,1024]{2,1,0:T(8,128)(2,1)}, bf16[6,512,1024]{2,1,0:T(8,128)(2,1)S(1)}, u32[]{:S(2)}) copy-start(bf16[6,512,1024]{2,1,0:T(8,128)(2,1)S(1)} %multiply_convert_fusion.2) | copy-start | bytes 18874372
  663.5 7.7 copy-start.46
  677.5 10.1 copy-start.56
  677.5 10.0 copy-start.58
  677.5 393.8 %all-reduce.4.cloned.1.call-start = ((), (), s32[]{:S(2)}) async-start(), calls=%async_computation.22 | async-start | bytes 37748736 | tf_op jit(solution)/shard_map/psum | solution.py:285
  678.9 8.7 copy-start.94
  678.9 19.4 %slice-start.6 = ((s8[12582912]{0:T(1024)(128)(4,1)}), s8[4194304]{0:T(1024)(128)(4,1)S(1)}, s32[]{:S(2)}) async-start(s8[12582912]{0:T(1024)(128)(4,1)} %bitcast.351), calls=%async_computation.29 | async-start | bytes 8388608
  678.9 19.4 %slice-start.7 = ((s8[12582912]{0:T(1024)(128)(4,1)}), s8[4194304]{0:T(1024)(128)(4,1)S(1)}, s32[]{:S(2)}) async-start(s8[12582912]{0:T(1024)(128)(4,1)} %bitcast.351), calls=%async_computation.30 | async-start | bytes 8388608
  689.4 9.0 slice-start.8
  700.8 21.7 %copy-start.25 = (bf16[6,64,2048]{2,1,0:T(8,128)(2,1)}, bf16[6,64,2048]{2,1,0:T(8,128)(2,1)S(1)}, u32[]{:S(2)}) copy-start(bf16[6,64,2048]{2,1,0:T(8,128)(2,1)S(1)} %multiply_convert_fusion.5) | copy-start | bytes 4718596
  722.5 6.6 copy-start.52
  722.5 6.6 copy-start.54
  780.7 49.7 %all-to-all-start.4 = ((bf16[2,2,196608]{2,1,0:T(2,128)(2,1)}), bf16[2,2,196608]{2,1,0:T(2,128)(2,1)}, u32[]{:S(2)}, u32[]{:S(2)}) async-start(bf16[2,2,196608]{2,1,0:T(2,128)(2,1)} %reshape.1054), calls=%async_computation.7 | async-start | bytes 3145728 | tf_op jit(solution)/shard_map/all_to_all | solution.py:241
  827.7 7.5 copy-start.88
  827.7 8.2 copy-start.26
  827.7 8.2 copy-start.27
  827.7 8.2 copy-start.73
  830.4 6.8 copy-start.84
  830.4 10.0 copy-start.89
  830.4 24.4 %all-to-all-start.3 = ((bf16[2,2,196608]{2,1,0:T(2,128)(2,1)}), bf16[2,2,196608]{2,1,0:T(2,128)(2,1)}, u32[]{:S(2)}, u32[]{:S(2)}) async-start(bf16[2,2,196608]{2,1,0:T(2,128)(2,1)} %reshape.1052), calls=%async_computation.6 | async-start | bytes 3145728 | tf_op jit(solution)/shard_map/all_to_all | solution.py:240
  867.0 49.9 %copy-start.79 = (f32[512]{0:T(512)S(1)}, f32[512]{0:T(512)}, u32[]{:S(2)}) copy-start(f32[512]{0:T(512)} %copy-done.78) | copy-start | bytes 6148
  867.0 49.9 %copy-start.28 = (f32[1,512,768]{2,1,0:T(8,128)S(1)}, f32[1,512,768]{2,1,0:T(8,128)}, u32[]{:S(2)}) copy-start(f32[1,512,768]{2,1,0:T(8,128)} %reduce-scatter.8.cloned.1.call-done) | copy-start | bytes 4718596
  1078.6 6.7 copy-start.43
  (61 other events, 188.0 us)
Sparse Core Ops, SparseCore 0:
  13.8 29.8 all-gather.11
  45.3 22.7 all-gather.13
  69.7 53.3 all-gather.15
  125.0 27.1 all-gather.17
  153.7 22.7 all-gather.19
  263.5 27.2 all-gather.21
  292.9 27.2 all-gather.23
  322.9 43.3 reduce-scatter.3
  369.2 43.3 reduce-scatter.5
  420.4 27.2 all-gather.25
  449.2 22.7 all-gather.27
  579.6 27.2 all-gather.29
  608.4 36.0 all-gather.31
  677.6 43.3 reduce-scatter.7
  735.7 335.6 all-reduce.3
where the time goes:
time: 1110 us; the launch traced here: 1100 us
  waiting for transfers between devices  372 us (34%)
  matrix products  275 us (25%)
  other arithmetic  210 us (19%)
  local copies, waits for them, and re-layouts  118 us (11%)
  blocking collectives  95.7 us (9%)
  between operations  16.1 us (1%)
    psum x1, waiting for transfers between devices, shards(): lax.psum((self_project_grad, self_output_grad, cross_query_grad, cross_me...  151 us
    unnamed x8, other arithmetic  89.1 us
    all_gather x3, waiting for transfers between devices, spread(): return lax.all_gather(normed, 'tp', axis=1, tiled=True)  73.7 us
    unnamed x239, local copies, waits for them, and re-layouts  68.6 us
    convert_element_type x4, other arithmetic, attend_backward(): score_grad = (attn_probs * (prob_grad - inner)).astype(jnp.bfloat16)  59.7 us
    all_gather x3, waiting for transfers between devices, spread_grad(): lax.all_gather(gradient.astype(jnp.bfloat16), 'tp', axis=1, tiled=True)  58.5 us
    dot_general x4, matrix products, attend_backward(): jnp.einsum('rqhe,rkhe->rhqk', grad_block, values, preferred_element_type=...  54.2 us
    reduce_scatter x2, waiting for transfers between devices, collect_grad(): lax.psum_scatter(partial_value, 'tp', scatter_dimension=1, tiled=True)  46.3 us
  transfers between devices with their start and end apart: 17, of which 11 were waited for; matrix products, arithmetic and copies ran while one was open for 49% of the time, Pallas kernels for 0%

commit v1 on v0

v1 whole, which is shorter than its diff:
```python
import functools

import jax
import jax.numpy as jnp
from jax import lax
from jax.experimental import pallas as pl
from jax.experimental.pallas import tpu as pltpu
from jax.sharding import PartitionSpec as P

HD = 64
EPSILON = 1e-06
NEGATIVE = -1e30
BQ = 128
BK = 256
F32 = jnp.float32
BF16 = jnp.bfloat16


def rows_of_two_heads(block):
    lane = lax.broadcasted_iota(jnp.int32, block.shape, 1)
    zero = jnp.zeros_like(block)
    return jnp.concatenate([jnp.where(lane < HD, block, zero), jnp.where(lane >= HD, block, zero)], axis=0)


def heads_side_by_side(wide):
    return jnp.concatenate([wide[:HD, :BQ], wide[HD:, BQ:]], axis=0).T


def twice(row):
    return jnp.concatenate([row, row], axis=1)


def block_rows(ref, start):
    return ref[0, pl.ds(pl.multiple_of(start, BQ), BQ), :]


def forward_kernel(bounds, interval_ref, q_ref, *refs, n_parts, n_blocks, q_offset):
    key_refs, (out_ref, total_ref) = refs[: 2 * n_parts], refs[2 * n_parts :]
    key_iota = lax.broadcasted_iota(jnp.int32, (BK, 2 * BQ), 0)

    def one_block(b, _):
        queries = block_rows(q_ref, q_offset + b * BQ).astype(F32) * (HD**-0.5)
        q_wide = rows_of_two_heads(queries).T.astype(BF16)
        carry = (
            jnp.full((1, 2 * BQ), NEGATIVE, F32),
            jnp.zeros((1, 2 * BQ), F32),
            jnp.zeros((2 * HD, 2 * BQ), F32),
        )
        for part in range(n_parts):
            k_ref, v_ref = key_refs[2 * part], key_refs[2 * part + 1]
            first = twice(interval_ref[2 * part, pl.ds(b, 1), :])
            last = twice(interval_ref[2 * part + 1, pl.ds(b, 1), :])
            place = (part * n_blocks + b) * 2

            def step(j, carry, k_ref=k_ref, v_ref=v_ref, first=first, last=last):
                peak, total, acc = carry
                rows = pl.ds(pl.multiple_of(j * BK, BK), BK)
                scores = jnp.dot(k_ref[0, rows, :], q_wide, preferred_element_type=F32)
                seen = (key_iota >= first - j * BK) & (key_iota < last - j * BK)
                scores = jnp.where(seen, scores, NEGATIVE)
                new_peak = jnp.maximum(peak, jnp.max(scores, axis=0, keepdims=True))
                shrink = jnp.exp(peak - new_peak)
                probs = jnp.exp(scores - new_peak)
                total = total * shrink + jnp.sum(probs, axis=0, keepdims=True)
                acc = acc * shrink + lax.dot_general(
                    v_ref[0, rows, :], probs.astype(BF16), (((0,), (0,)), ((), ())), preferred_element_type=F32
                )
                return new_peak, total, acc

            carry = lax.fori_loop(bounds[place], bounds[place + 1], step, carry)
        peak, total, acc = carry
        out = heads_side_by_side(acc / total)
        out_ref[pl.ds(pl.multiple_of(b * BQ, BQ), BQ), :] = out.astype(BF16)
        total_ref[0, pl.ds(b, 1), :] = peak + jnp.log(total)
        return 0

    lax.fori_loop(0, n_blocks, one_block, 0)


def backward_kernel(bounds, interval_ref, total_ref, q_ref, out_ref, grad_ref, *refs, n_parts, n_blocks, q_offset, fused):
    key_refs, refs = refs[: 2 * n_parts], refs[2 * n_parts :]
    if fused:
        (dall_ref, dk_acc, dv_acc) = refs
    else:
        (dq_ref, dkv_ref, dk_acc, dv_acc) = refs
    key_iota = lax.broadcasted_iota(jnp.int32, (BK, 2 * BQ), 0)
    dk_acc[...] = jnp.zeros_like(dk_acc)
    dv_acc[...] = jnp.zeros_like(dv_acc)

    def one_block(b, _):
        queries = block_rows(q_ref, q_offset + b * BQ).astype(F32) * (HD**-0.5)
        q_rows = rows_of_two_heads(queries)
        q_wide = q_rows.T.astype(BF16)
        q_rows = q_rows.astype(BF16)
        here = pl.ds(pl.multiple_of(b * BQ, BQ), BQ)
        grad = grad_ref[here, :].astype(F32)
        g_rows = rows_of_two_heads(grad)
        g_wide = g_rows.T.astype(BF16)
        g_rows = g_rows.astype(BF16)
        product = (grad * out_ref[here, :].astype(F32)).T
        inner = jnp.concatenate(
            [jnp.sum(product[:HD], axis=0, keepdims=True), jnp.sum(product[HD:], axis=0, keepdims=True)], axis=1
        )
        log_total = total_ref[0, pl.ds(b, 1), :]
        dq = jnp.zeros((2 * HD, 2 * BQ), F32)
        base = 0
        for part in range(n_parts):
            k_ref, v_ref = key_refs[2 * part], key_refs[2 * part + 1]
            first = twice(interval_ref[2 * part, pl.ds(b, 1), :])
            last = twice(interval_ref[2 * part + 1, pl.ds(b, 1), :])
            place = (part * n_blocks + b) * 2

            def step(j, dq, k_ref=k_ref, v_ref=v_ref, first=first, last=last, base=base):
                rows = pl.ds(pl.multiple_of(j * BK, BK), BK)
                sums = pl.ds(pl.multiple_of(base + j * BK, BK), BK)
                keys = k_ref[0, rows, :]
                scores = jnp.dot(keys, q_wide, preferred_element_type=F32)
                prob_grad = jnp.dot(v_ref[0, rows, :], g_wide, preferred_element_type=F32)
                seen = (key_iota >= first - j * BK) & (key_iota < last - j * BK)
                probs = jnp.exp(jnp.where(seen, scores, NEGATIVE) - log_total)
                score_grad = (probs * (prob_grad - inner)).astype(BF16)
                dv_acc[sums, :] += jnp.dot(probs.astype(BF16), g_rows, preferred_element_type=F32)
                dk_acc[sums, :] += jnp.dot(score_grad, q_rows, preferred_element_type=F32)
                return dq + lax.dot_general(keys, score_grad, (((0,), (0,)), ((), ())), preferred_element_type=F32)

            dq = lax.fori_loop(bounds[place], bounds[place + 1], step, dq)
            base += k_ref.shape[1]
        dq = (heads_side_by_side(dq) * (HD**-0.5)).astype(BF16)
        if fused:
            dall_ref[0, pl.ds(pl.multiple_of(q_offset + b * BQ, BQ), BQ), :] = dq
        else:
            dq_ref[here, :] = dq
        return 0

    lax.fori_loop(0, n_blocks, one_block, 0)
    if fused:
        if q_offset:
            dall_ref[0, :q_offset, :] = jnp.zeros((q_offset, 2 * HD), BF16)
        dall_ref[1, :, :] = dk_acc[...].astype(BF16)
        dall_ref[2, :, :] = dv_acc[...].astype(BF16)
    else:
        dkv_ref[0, :, :] = dk_acc[...].astype(BF16)
        dkv_ref[1, :, :] = dv_acc[...].astype(BF16)


def column_block(array, index=None):
    if index is None:
        return pl.BlockSpec((array.shape[0], 2 * HD), lambda g, *_: (0, g))
    return pl.BlockSpec((1, array.shape[1], 2 * HD), lambda g, *_: (index, 0, g))


def whole(array):
    return pl.BlockSpec(array.shape, lambda g, *_: (0,) * array.ndim)


PARAMS = pltpu.CompilerParams(dimension_semantics=("arbitrary",), vmem_limit_bytes=48 << 20)


def attend_forward(plan, q, parts, q_offset):
    bounds, interval = plan
    q_array, q_index = q
    n_blocks, columns = interval.shape[1], q_array.shape[2]
    length, groups = n_blocks * BQ, columns // (2 * HD)
    operands, specs = [interval, q_array], [whole(interval), column_block(q_array, q_index)]
    for array, k_index, v_index in parts:
        operands += [array, array]
        specs += [column_block(array, k_index), column_block(array, v_index)]
    n_keys = sum(array.shape[1] for array, *_ in parts)
    return pl.pallas_call(
        functools.partial(forward_kernel, n_parts=len(parts), n_blocks=n_blocks, q_offset=q_offset),
        grid_spec=pltpu.PrefetchScalarGridSpec(
            num_scalar_prefetch=1,
            grid=(groups,),
            in_specs=specs,
            out_specs=[
                pl.BlockSpec((length, 2 * HD), lambda g, *_: (0, g)),
                pl.BlockSpec((1, n_blocks, 2 * BQ), lambda g, *_: (g, 0, 0)),
            ],
        ),
        out_shape=[
            jax.ShapeDtypeStruct((length, columns), BF16),
            jax.ShapeDtypeStruct((groups, n_blocks, 2 * BQ), F32),
        ],
        compiler_params=PARAMS,
        cost_estimate=pl.CostEstimate(
            flops=2 * length * n_keys * columns, bytes_accessed=4 * n_keys * columns, transcendentals=length * n_keys
        ),
        name="attend_forward",
    )(bounds, *operands)


def attend_backward(plan, totals, q, out, out_grad, parts, q_offset, fused):
    bounds, interval = plan
    q_array, q_index = q
    n_blocks, columns = interval.shape[1], q_array.shape[2]
    length, groups = n_blocks * BQ, columns // (2 * HD)
    operands = [interval, totals, q_array, out, out_grad]
    specs = [
        whole(interval),
        pl.BlockSpec((1, n_blocks, 2 * BQ), lambda g, *_: (g, 0, 0)),
        column_block(q_array, q_index),
        column_block(out),
        column_block(out_grad),
    ]
    for array, k_index, v_index in parts:
        operands += [array, array]
        specs += [column_block(array, k_index), column_block(array, v_index)]
    n_keys = sum(array.shape[1] for array, *_ in parts)
    if fused:
        out_specs = [pl.BlockSpec((3, n_keys, 2 * HD), lambda g, *_: (0, 0, g))]
        out_shape = [jax.ShapeDtypeStruct((3, n_keys, columns), BF16)]
    else:
        out_specs = [
            pl.BlockSpec((length, 2 * HD), lambda g, *_: (0, g)),
            pl.BlockSpec((2, n_keys, 2 * HD), lambda g, *_: (0, 0, g)),
        ]
        out_shape = [
            jax.ShapeDtypeStruct((length, columns), BF16),
            jax.ShapeDtypeStruct((2, n_keys, columns), BF16),
        ]
    return pl.pallas_call(
        functools.partial(
            backward_kernel, n_parts=len(parts), n_blocks=n_blocks, q_offset=q_offset, fused=fused
        ),
        grid_spec=pltpu.PrefetchScalarGridSpec(
            num_scalar_prefetch=1,
            grid=(groups,),
            in_specs=specs,
            out_specs=out_specs,
            scratch_shapes=[pltpu.VMEM((n_keys, 2 * HD), F32), pltpu.VMEM((n_keys, 2 * HD), F32)],
        ),
        out_shape=out_shape,
        compiler_params=PARAMS,
        cost_estimate=pl.CostEstimate(
            flops=5 * length * n_keys * columns, bytes_accessed=8 * n_keys * columns, transcendentals=length * n_keys
        ),
        name="attend_backward",
    )(bounds, *operands)


def make_plan(starts, ends, bases, n_keys):
    bounds, interval = [], []
    for base in bases:
        first, last = starts - base, ends - base
        interval += [first.reshape(-1, BQ), last.reshape(-1, BQ)]
        low = jnp.clip(first[::BQ] // BK, 0, n_keys // BK)
        high = jnp.clip((last[BQ - 1 :: BQ] + BK - 1) // BK, 0, n_keys // BK)
        bounds.append(jnp.stack([low, high], axis=1).reshape(-1))
    return jnp.concatenate(bounds).astype(jnp.int32), jnp.stack(interval).astype(jnp.int32)


def inverse_rms(rows):
    return lax.rsqrt(jnp.mean(rows * rows, axis=-1, keepdims=True) + EPSILON)


def normalize(rows, gain):
    return rows * inverse_rms(rows) * gain


def normalize_back(rows, gain, cotangent):
    inverse = inverse_rms(rows)
    unit = rows * inverse
    scaled = cotangent * gain
    grad = inverse * (scaled - unit * jnp.mean(scaled * unit, axis=-1, keepdims=True))
    return grad, jnp.sum(cotangent * unit, axis=0)


def gelu_parts(u):
    c = (2.0 / jnp.pi) ** 0.5
    t = jnp.tanh(c * (u + 0.044715 * u * u * u))
    half = 0.5 * (1.0 + t)
    slope = half + 0.5 * u * (1.0 - t * t) * (c * (1.0 + 3.0 * 0.044715 * u * u))
    return u * half, slope


def mm(pattern, a, b):
    return jnp.einsum(pattern, a, b, preferred_element_type=F32)


class Links:
    def __init__(self, n_dp):
        self.n_dp = n_dp
        self.n_bits = n_dp.bit_length() - 1
        self.here = lax.axis_index("dp")

    def bit(self, k):
        return (self.here >> k) & 1

    def across_tp(self, x):
        return lax.ppermute(x, "tp", [(0, 1), (1, 0)])

    def across(self, x, k):
        return lax.ppermute(x, "dp", [(i, i ^ (1 << k)) for i in range(self.n_dp)])

    def merge(self, k, mine, theirs):
        own_first = self.bit(k) == 0
        return jnp.concatenate(
            [jnp.where(own_first, mine, theirs), jnp.where(own_first, theirs, mine)], axis=0
        )

    def part(self, x, index, size):
        return lax.dynamic_slice_in_dim(x, index * size, size, axis=0)

    def fetch(self, shard, bits):
        index = 0
        for place, k in enumerate(bits):
            index = index + (self.bit(k) << place)
        held = self.across_tp(self.part(shard, index, shard.shape[0] >> len(bits)))
        for k in bits:
            held = self.merge(k, held, self.across(held, k))
        return held

    def reduce(self, own, other):
        half = own.shape[0] // 2
        c = self.bit(0)
        sent = jnp.concatenate([self.part(own, 1 - c, half), self.part(other, 1 - c, half)], axis=0)
        got = self.across(sent, 0)
        kept_other = self.add(self.part(other, c, half), got[half:])
        kept = self.add(self.part(own, c, half), got[:half])
        kept = self.add(kept, self.across_tp(kept_other))
        for k in range(1, self.n_bits):
            half = kept.shape[0] // 2
            b = self.bit(k)
            kept = self.add(self.part(kept, b, half), self.across(self.part(kept, 1 - b, half), k))
        for k in reversed(range(self.n_bits)):
            kept = self.merge(k, kept, self.across(kept, k))
        return kept.astype(F32)

    def add(self, a, b):
        return (a.astype(F32) + b.astype(F32)).astype(BF16)

    def total(self, x):
        x = x + self.across_tp(x)
        for k in range(self.n_bits):
            x = x + self.across(x, k)
        return x


def flat(x):
    return x.reshape(-1, x.shape[-1])


def shards(
    n_dp,
    decoder_rows,
    memory_rows,
    output_grad,
    token_segments,
    memory_segments,
    valid_mask,
    norm_gains,
    self_project,
    self_output,
    cross_query,
    cross_memory,
    cross_output,
    gate_up,
    down_weight,
):
    links = Links(n_dp)
    side = lax.axis_index("tp")
    decoder, memory, out_grad = decoder_rows[0], memory_rows[0], output_grad[0]
    tokens, patches, valid = token_segments[0], memory_segments[0], valid_mask[0]
    own_len, features = decoder.shape
    mem_len = memory.shape[0]
    halo = tokens.shape[0] // 4

    halo_rows = lax.ppermute(decoder[-halo:], "tp", [(0, 1)])
    two, three = (1, 0), (2, 1, 0)
    project = (self_project, links.fetch(flat(self_project), two).reshape(self_project.shape))
    out_a = (self_output, links.fetch(self_output, two))
    query_w = (cross_query, links.fetch(cross_query, two))
    memory_w = (cross_memory, links.fetch(flat(cross_memory), two).reshape(cross_memory.shape))
    memory_other = links.across_tp(memory)
    out_c = (cross_output, links.fetch(cross_output, two))
    gate_w = (gate_up, links.fetch(flat(gate_up), three).reshape(gate_up.shape))
    down_w = (down_weight, links.fetch(down_weight, three))
    both = (0, 1)

    own_tokens = lax.dynamic_slice_in_dim(tokens, side * own_len, own_len)
    first_own = side * own_len - halo
    place = jnp.arange(own_len, dtype=jnp.int32)
    starts_a = jnp.sum((tokens[None, :] < own_tokens[:, None]).astype(jnp.int32), axis=1) - first_own
    plan_a = make_plan(starts_a, place + (halo + 1), (0,), own_len + halo)
    starts_c = jnp.sum((patches[None, :] < own_tokens[:, None]).astype(jnp.int32), axis=1)
    ends_c = jnp.sum((patches[None, :] <= own_tokens[:, None]).astype(jnp.int32), axis=1)
    plan_c = make_plan(starts_c, ends_c, (side * mem_len, (1 - side) * mem_len), mem_len)

    resid0 = decoder.astype(F32)
    normed_a = normalize(jnp.concatenate([halo_rows, decoder], axis=0).astype(F32), norm_gains[0]).astype(BF16)
    proj_a = [mm("sd,cdi->csi", normed_a, project[h]).astype(BF16) for h in both]
    att_a, totals_a = zip(
        *[attend_forward(plan_a, (proj_a[h], 0), ((proj_a[h], 1, 2),), halo) for h in both]
    )
    branch_a = mm("si,id->sd", att_a[0], out_a[0]) + mm("si,id->sd", att_a[1], out_a[1])
    resid1 = resid0 + branch_a

    normed_c = normalize(resid1, norm_gains[1]).astype(BF16)
    query_c = [mm("sd,di->si", normed_c, query_w[h]).astype(BF16)[None] for h in both]
    kv_own = [mm("td,cdi->cti", memory, memory_w[h]).astype(BF16) for h in both]
    kv_other = [mm("td,cdi->cti", memory_other, memory_w[h]).astype(BF16) for h in both]
    keys_c = [((kv_own[h], 0, 1), (kv_other[h], 0, 1)) for h in both]
    att_c, totals_c = zip(*[attend_forward(plan_c, (query_c[h], 0), keys_c[h], 0) for h in both])
    branch_c = mm("si,id->sd", att_c[0], out_c[0]) + mm("si,id->sd", att_c[1], out_c[1])
    resid2 = resid1 + branch_c

    normed_m = normalize(resid2, norm_gains[2]).astype(BF16)
    gates = [mm("sd,cdf->csf", normed_m, gate_w[h]) for h in both]
    acts = [gelu_parts(gates[h][0]) for h in both]
    hidden = [(acts[h][0] * gates[h][1]).astype(BF16) for h in both]
    branch_m = mm("sf,fd->sd", hidden[0], down_w[0]) + mm("sf,fd->sd", hidden[1], down_w[1])
    result = resid2 + branch_m

    valid_rows = valid.astype(F32)[:, None]
    grad_m = out_grad.astype(F32) * valid_rows
    full_m = grad_m.astype(BF16)
    hidden_grad = [mm("sd,fd->sf", full_m, down_w[h]) for h in both]
    gate_grads = [
        jnp.stack([hidden_grad[h] * gates[h][1] * acts[h][1], hidden_grad[h] * acts[h][0]]).astype(BF16)
        for h in both
    ]
    ffn_sums = links.reduce(
        *[
            jnp.concatenate(
                [
                    flat(mm("sd,csf->cdf", normed_m, gate_grads[h]).astype(BF16)),
                    mm("sd,sf->df", full_m, hidden[h]).astype(BF16),
                ],
                axis=0,
            )
            for h in both
        ]
    )
    normed_m_grad = mm("csf,cdf->sd", gate_grads[0], gate_w[0]) + mm("csf,cdf->sd", gate_grads[1], gate_w[1])
    resid2_grad, gain_m_grad = normalize_back(resid2, norm_gains[2], normed_m_grad)
    grad_c = grad_m + resid2_grad
    full_c = grad_c.astype(BF16)

    att_c_grad = [mm("sd,id->si", full_c, out_c[h]).astype(BF16) for h in both]
    query_grad, kv_grad = zip(
        *[
            attend_backward(
                plan_c, totals_c[h], (query_c[h], 0), att_c[h], att_c_grad[h], keys_c[h], 0, False
            )
            for h in both
        ]
    )
    memory_partial = mm("cti,cdi->td", kv_grad[0][:, mem_len:], memory_w[0]) + mm(
        "cti,cdi->td", kv_grad[1][:, mem_len:], memory_w[1]
    )
    memory_got = links.across_tp(memory_partial.astype(BF16))
    normed_c_grad = mm("si,di->sd", query_grad[0], query_w[0]) + mm("si,di->sd", query_grad[1], query_w[1])
    memory_all = jnp.concatenate([memory, memory_other], axis=0)
    cross_sums = links.reduce(
        *[
            jnp.concatenate(
                [
                    mm("sd,si->di", full_c, att_c[h]).astype(BF16),
                    mm("sd,si->di", normed_c, query_grad[h]).astype(BF16),
                    flat(mm("td,cti->cdi", memory_all, kv_grad[h]).astype(BF16)),
                ],
                axis=0,
            )
            for h in both
        ]
    )
    resid1_grad, gain_c_grad = normalize_back(resid1, norm_gains[1], normed_c_grad)
    grad_a = grad_c + resid1_grad
    full_a = grad_a.astype(BF16)

    att_a_grad = [mm("sd,id->si", full_a, out_a[h]).astype(BF16) for h in both]
    proj_grad = [
        attend_backward(
            plan_a, totals_a[h], (proj_a[h], 0), att_a[h], att_a_grad[h], ((proj_a[h], 1, 2),), halo, True
        )[0]
        for h in both
    ]
    normed_a_grad = mm("csi,cdi->sd", proj_grad[0], project[0]) + mm("csi,cdi->sd", proj_grad[1], project[1])
    halo_got = lax.ppermute(normed_a_grad[:halo].astype(BF16), "tp", [(1, 0)])
    self_sums = links.reduce(
        *[
            jnp.concatenate(
                [
                    flat(mm("sd,csi->cdi", normed_a, proj_grad[h]).astype(BF16)),
                    mm("sd,si->di", full_a, att_a[h]).astype(BF16),
                ],
                axis=0,
            )
            for h in both
        ]
    )
    normed_a_grad = normed_a_grad[halo:]
    normed_a_grad = jnp.concatenate(
        [normed_a_grad[:-halo], normed_a_grad[-halo:] + halo_got.astype(F32)], axis=0
    )
    resid0_grad, gain_a_grad = normalize_back(resid0, norm_gains[0], normed_a_grad)
    decoder_grad = grad_a + resid0_grad
    memory_grad = (
        mm("cti,cdi->td", kv_grad[0][:, :mem_len], memory_w[0])
        + mm("cti,cdi->td", kv_grad[1][:, :mem_len], memory_w[1])
        + memory_got.astype(F32)
    )

    sums = [jnp.sum(v * v * valid_rows) for v in (result, branch_a, branch_c, branch_m)] + [jnp.sum(valid_rows)]
    stats = jnp.zeros((8, features), F32)
    for row, value in enumerate(sums):
        stats = stats.at[row].set(value)
    stats = links.total(stats.at[5].set(gain_m_grad).at[6].set(gain_c_grad))
    gain_a = links.total(jnp.broadcast_to(gain_a_grad, (8, features)))
    gains_grad = jnp.stack([gain_a[0], stats[6], stats[5]])
    root_squares = jnp.sqrt(stats[:4, 0] / (stats[4, 0] * features))

    d = features
    return (
        result.astype(BF16)[None],
        decoder_grad[None],
        memory_grad[None],
        root_squares,
        gains_grad,
        self_sums[: 3 * d].reshape(self_project.shape),
        self_sums[3 * d :].T,
        cross_sums[d : 2 * d],
        cross_sums[2 * d :].reshape(cross_memory.shape),
        cross_sums[:d].T,
        ffn_sums[: 2 * d].reshape(gate_up.shape),
        ffn_sums[2 * d :].T,
    )


def solution(mesh):
    assert mesh.shape["tp"] == 2
    return jax.shard_map(
        functools.partial(shards, mesh.shape["dp"]),
        mesh=mesh,
        in_specs=(
            P("dp", "tp", None),
            P("dp", "tp", None),
            P("dp", "tp", None),
            P("dp", None),
            P("dp", None),
            P("dp", "tp"),
            P(),
            P(None, None, "tp"),
            P("tp", None),
            P(None, "tp"),
            P(None, None, "tp"),
            P("tp", None),
            P(None, None, "tp"),
            P("tp", None),
        ),
        out_specs=(
            P("dp", "tp", None),
            P("dp", "tp", None),
            P("dp", "tp", None),
            P(),
            P(),
            P(None, None, "tp"),
            P("tp", None),
            P(None, "tp"),
            P(None, None, "tp"),
            P("tp", None),
            P(None, None, "tp"),
            P("tp", None),
        ),
        check_vma=False,
    )
```

time: 1110 us -> 728 us (0.66)
  matrix products: 275 us -> 99.1 us
  Pallas kernels: 0 us -> 134 us
  other arithmetic: 210 us -> 78.2 us
  blocking collectives: 95.7 us -> 0 us
  waiting for transfers between devices: 372 us -> 283 us
  local copies, waits for them, and re-layouts: 118 us -> 63.3 us
  starting transfers between devices: 10.9 us -> 54.8 us
  between operations: 16.1 us -> 3.77 us
    ppermute x0 -> x64, waiting for transfers between devices: none -> 283 us  [the longest x48 143 us: across(): return lax.ppermute(x, 'dp', [(i, i ^ 1 << k) for i in range(self.n_dp)])]
    dot_general x46, matrix products: 275 us -> 99.1 us  [mm(): return jnp.einsum(pattern, a, b, preferred_element_type=F32)]
    psum x1 -> x0, waiting for transfers between devices: 151 us -> none  [shards(): lax.psum((self_project_grad, self_output_grad, cross_query_grad, cross_me...]
    pallas_call x0 -> x8, Pallas kernels: none -> 134 us  [the longest x4 68.2 us: attend_backward(): pl.pallas_call(functools.partial(backward_kernel, n_parts=len(parts), n_b...]
    all_gather x11 -> x0, waiting for transfers between devices: 132 us -> none  [the longest x3 73.7 us: spread(): return lax.all_gather(normed, 'tp', axis=1, tiled=True)]
    unnamed x8 -> x0, other arithmetic: 89.1 us -> none
    reduce_scatter x3 -> x0, waiting for transfers between devices: 76.9 us -> none  [the longest x2 46.3 us: collect_grad(): lax.psum_scatter(partial_value, 'tp', scatter_dimension=1, tiled=True)]
    ppermute x0 -> x64, starting transfers between devices: none -> 54.8 us  [the longest x48 29.9 us: across(): return lax.ppermute(x, 'dp', [(i, i ^ 1 << k) for i in range(self.n_dp)])]
  transfers between devices with their start and end apart: 17 -> 64, of which waited for: 11 -> 27; matrix products, arithmetic and copies ran while one was open for 49% -> 25% of each run, Pallas kernels for 0% -> 9%
where the time goes in v1:
time: 728 us; the launch traced here: 717 us
  waiting for transfers between devices  283 us (39%)
  Pallas kernels  134 us (18%)
  matrix products  99.1 us (14%)
  other arithmetic  78.2 us (11%)
  local copies, waits for them, and re-layouts  63.3 us (9%)
  starting transfers between devices  54.8 us (8%)
    ppermute x48, waiting for transfers between devices, across(): return lax.ppermute(x, 'dp', [(i, i ^ 1 << k) for i in range(self.n_dp)])  143 us
    ppermute x14, waiting for transfers between devices, across_tp(): return lax.ppermute(x, 'tp', [(0, 1), (1, 0)])  141 us
    dot_general x46, matrix products, mm(): return jnp.einsum(pattern, a, b, preferred_element_type=F32)  99.1 us
    pallas_call x4, Pallas kernels, attend_backward(): pl.pallas_call(functools.partial(backward_kernel, n_parts=len(parts), n_b...  68.2 us
    pallas_call x4, Pallas kernels, attend_forward(): pl.pallas_call(functools.partial(forward_kernel, n_parts=len(parts), n_bl...  66.3 us
    ppermute x48, starting transfers between devices, across(): return lax.ppermute(x, 'dp', [(i, i ^ 1 << k) for i in range(self.n_dp)])  29.9 us
    unnamed x211, local copies, waits for them, and re-layouts  19.4 us
    convert_element_type x15, other arithmetic, add(): return (a.astype(F32) + b.astype(F32)).astype(BF16)  18.7 us
  transfers between devices with their start and end apart: 64, of which 27 were waited for; matrix products, arithmetic and copies ran while one was open for 25% of the time, Pallas kernels for 9%

profile of v1, /device:TPU:0, one launch (start us, length us, event | category | flops | bytes accessed | tf_op | source)
XLA Modules:
  0.0 716.9 jit_solution(13774546064445806103)
XLA Ops:
  2.6 5.6 collective-permute-start
  21.1 4.3 fusion.72.refs_0_.refs_1_
  35.4 2.7 collective-permute-start.7
  42.8 2.7 collective-permute-done.9
  48.0 33.9 %collective-permute-done.21 = bf16[128,768]{1,0:T(8,128)(2,1)S(1)} collective-permute-done((bf16[128,768]{1,0:T(8,128)(2,1)}, bf16[128,768]{1,0:T(8,128)(2,1)S(1)}, u32[]{:S(2)}, u32[]{:S(2)}) %collective-permute-start.21) | collective-permute-done | bytes 196640 | tf_op jit(solution)/shard_map/ppermute | solution.py:290
  86.5 2.8 convert_bitcast_fusion.5.q_ref.refs_0_.refs_1_
  89.3 10.1 %attend_forward.4 = (bf16[512,384]{1,0:T(8,128)(2,1)S(1)}, f32[3,4,256]{2,1,0:T(4,128)S(1)}) custom-call(s32[8]{0:T(128)S(1)} %reshape.389.bounds, s32[2,4,128]{2,1,0:T(4,128)S(1)} %pad_add_fusion.1.interval_ref, bf16[3,768,384]{2,1,0:T(8,128)(2,1)S(1)} %convert_bitcast_fusion.5.q_ref.refs_0_.refs_1_, ...), custom_call_target="tpu_custom_call" | custom-call | flops 301989888 | bytes 1179648 | tf_op jit(solution)/shard_map/attend_forward/pallas_call | solution.py:169
  102.1 7.4 %collective-permute-done.12 = bf16[384,384]{1,0:T(8,128)(2,1)S(1)} collective-permute-done((bf16[384,384]{1,0:T(8,128)(2,1)S(1)}, bf16[384,384]{1,0:T(8,128)(2,1)S(1)}, u32[]{:S(2)}, u32[]{:S(2)}) %collective-permute-start.12) | collective-permute-done | bytes 294944 | tf_op jit(solution)/shard_map/ppermute | solution.py:293
  114.3 8.2 %collective-permute-done.18 = bf16[192,1024]{1,0:T(8,128)(2,1)S(1)} collective-permute-done((bf16[192,1024]{1,0:T(8,128)(2,1)S(1)}, bf16[192,1024]{1,0:T(8,128)(2,1)S(1)}, u32[]{:S(2)}, u32[]{:S(2)}) %collective-permute-start.18) | collective-permute-done | bytes 393248 | tf_op jit(solution)/shard_map/ppermute | solution.py:293
  123.4 7.6 %collective-permute-done.2 = bf16[576,384]{1,0:T(8,128)(2,1)S(1)} collective-permute-done((bf16[576,384]{1,0:T(8,128)(2,1)}, bf16[576,384]{1,0:T(8,128)(2,1)S(1)}, u32[]{:S(2)}, u32[]{:S(2)}) %collective-permute-start.2) | collective-permute-done | bytes 442400 | tf_op jit(solution)/shard_map/ppermute | solution.py:293
  135.1 12.5 %collective-permute-done.19 = bf16[384,1024]{1,0:T(8,128)(2,1)S(1)} collective-permute-done((bf16[384,1024]{1,0:T(8,128)(2,1)S(1)}, bf16[384,1024]{1,0:T(8,128)(2,1)S(1)}, u32[]{:S(2)}, u32[]{:S(2)}) %collective-permute-start.19) | collective-permute-done | bytes 786464 | tf_op jit(solution)/shard_map/ppermute | solution.py:293
  150.8 4.0 fusion.75.refs_2_.refs_3_
  154.7 2.8 fusion.81.refs_2_.refs_3_
  159.3 2.8 convert_bitcast_fusion.4.q_ref.refs_0_.refs_1_
  162.1 9.9 %attend_forward.5 = (bf16[512,384]{1,0:T(8,128)(2,1)S(1)}, f32[3,4,256]{2,1,0:T(4,128)S(1)}) custom-call(s32[8]{0:T(128)S(1)} %reshape.389.bounds, s32[2,4,128]{2,1,0:T(4,128)S(1)} %pad_add_fusion.1.interval_ref, bf16[3,768,384]{2,1,0:T(8,128)(2,1)S(1)} %convert_bitcast_fusion.4.q_ref.refs_0_.refs_1_, ...), custom_call_target="tpu_custom_call" | custom-call | flops 301989888 | bytes 1179648 | tf_op jit(solution)/shard_map/attend_forward/pallas_call | solution.py:169
  176.8 23.3 %attend_forward.6 = (bf16[512,384]{1,0:T(8,128)(2,1)S(1)}, f32[3,4,256]{2,1,0:T(4,128)S(1)}) custom-call(s32[16]{0:T(128)S(1)} %pad_add_fusion.5.bounds, s32[4,4,128]{2,1,0:T(4,128)S(1)} %pad_add_fusion.interval_ref, bf16[1,512,384]{2,1,0:T(8,128)(2,1)S(1)} %fusion.87.q_ref, bf16[2,1024,384]{2,1,0:T(8,128)(2,1)S(1)} %copy-done.2, ...), custom_call_target="tpu_custom_call" | custom-call | flops 805306368 | bytes 3145728 | tf_op jit(solution)/shard_map/attend_forward/pallas_call | solution.py:169
  200.2 2.9 fusion.167
  203.7 22.9 %attend_forward.7 = (bf16[512,384]{1,0:T(8,128)(2,1)S(1)}, f32[3,4,256]{2,1,0:T(4,128)S(1)}) custom-call(s32[16]{0:T(128)S(1)} %copy-done.9, s32[4,4,128]{2,1,0:T(4,128)S(1)} %pad_add_fusion.interval_ref, bf16[1,512,384]{2,1,0:T(8,128)(2,1)S(1)} %fusion.88.q_ref, bf16[2,1024,384]{2,1,0:T(8,128)(2,1)S(1)} %fusion.78.refs_0_.refs_1_, ...), custom_call_target="tpu_custom_call" | custom-call | flops 805306368 | bytes 3145728 | tf_op jit(solution)/shard_map/attend_forward/pallas_call | solution.py:169
  226.6 2.8 multiply_reduce_fusion.8
  237.7 4.2 fusion.8
  254.2 3.9 multiply_reduce_fusion.2
  260.3 23.4 %attend_backward.4 = (bf16[512,384]{1,0:T(8,128)(2,1)S(1)}, bf16[2,2048,384]{2,1,0:T(8,128)(2,1)}) custom-call(s32[16]{0:T(128)S(1)} %copy-done.9, s32[4,4,128]{2,1,0:T(4,128)S(1)} %pad_add_fusion.interval_ref, f32[3,4,256]{2,1,0:T(4,128)S(1)} %get-tuple-element.112.total_ref, bf16[1,512,384]{2,1,0:T(8,128)(2,1)S(1)} %fusion.87.q_ref, ...), custom_call_target="tpu_custom_call" | custom-call | flops 2013265920 | bytes 6291456 | tf_op jit(solution)/shard_map/attend_backward/pallas_call | solution.py:221
  284.4 23.8 %attend_backward.5 = (bf16[512,384]{1,0:T(8,128)(2,1)S(1)}, bf16[2,2048,384]{2,1,0:T(8,128)(2,1)}) custom-call(s32[16]{0:T(128)S(1)} %copy-done.9, s32[4,4,128]{2,1,0:T(4,128)S(1)} %pad_add_fusion.interval_ref, f32[3,4,256]{2,1,0:T(4,128)S(1)} %get-tuple-element.114.total_ref, bf16[1,512,384]{2,1,0:T(8,128)(2,1)S(1)} %fusion.88.q_ref, ...), custom_call_target="tpu_custom_call" | custom-call | flops 2013265920 | bytes 6291456 | tf_op jit(solution)/shard_map/attend_backward/pallas_call | solution.py:221
  319.3 3.6 convolution_convert_fusion
  325.4 10.5 %attend_backward.6 = bf16[3,768,384]{2,1,0:T(8,128)(2,1)S(1)} custom-call(s32[8]{0:T(128)S(1)} %reshape.389.bounds, s32[2,4,128]{2,1,0:T(4,128)S(1)} %pad_add_fusion.1.interval_ref, f32[3,4,256]{2,1,0:T(4,128)S(1)} %get-tuple-element.116.total_ref, bf16[3,768,384]{2,1,0:T(8,128)(2,1)S(1)} %convert_bitcast_fusion.5.q_ref.refs_0_.refs_1_, ...), custom_call_target="tpu_custom_call" | custom-call | flops 754974720 | bytes 2359296 | tf_op jit(solution)/shard_map/attend_backward/pallas_call | solution.py:221
  337.6 10.5 %attend_backward.7 = bf16[3,768,384]{2,1,0:T(8,128)(2,1)S(1)} custom-call(s32[8]{0:T(128)S(1)} %reshape.389.bounds, s32[2,4,128]{2,1,0:T(4,128)S(1)} %pad_add_fusion.1.interval_ref, f32[3,4,256]{2,1,0:T(4,128)S(1)} %get-tuple-element.117.total_ref, bf16[3,768,384]{2,1,0:T(8,128)(2,1)S(1)} %convert_bitcast_fusion.4.q_ref.refs_0_.refs_1_, ...), custom_call_target="tpu_custom_call" | custom-call | flops 754974720 | bytes 2359296 | tf_op jit(solution)/shard_map/attend_backward/pallas_call | solution.py:221
  352.1 3.1 fusion.65
  367.1 3.4 collective-permute-start.27
  370.5 4.1 convert_bitcast_fusion.2
  374.6 2.8 copy.104
  377.4 4.1 convert_bitcast_fusion.3
  381.5 2.9 copy.102
  391.6 2.6 fusion.7
  394.3 2.9 pad_maximum_fusion
  399.2 2.6 fusion
  401.8 5.3 fusion.84
  407.1 5.7 fusion.85
  424.0 3.7 collective-permute-done.29
  428.2 3.5 collective-permute-done.30
  439.8 3.2 collective-permute-done.34
  443.0 3.8 collective-permute-done.35
  446.8 2.8 collective-permute-start.36
  449.6 3.3 add_convert_fusion.8
  455.5 4.7 add_convert_fusion.1
  462.6 36.5 %collective-permute-done.38 = bf16[1536,384]{1,0:T(8,128)(2,1)S(1)} collective-permute-done((bf16[1536,384]{1,0:T(8,128)(2,1)S(1)}, bf16[1536,384]{1,0:T(8,128)(2,1)S(1)}, u32[]{:S(2)}, u32[]{:S(2)}) %collective-permute-start.38) | collective-permute-done | bytes 1179680 | tf_op jit(solution)/shard_map/ppermute | solution.py:290
  499.0 3.4 add_convert_fusion.7
  502.6 21.7 %collective-permute-done.47 = bf16[1536,384]{1,0:T(8,128)(2,1)S(1)} collective-permute-done((bf16[1536,384]{1,0:T(8,128)(2,1)S(1)}, bf16[1536,384]{1,0:T(8,128)(2,1)S(1)}, u32[]{:S(2)}, u32[]{:S(2)}) %collective-permute-start.47) | collective-permute-done | bytes 1179680 | tf_op jit(solution)/shard_map/ppermute | solution.py:290
  525.3 45.8 %collective-permute-done.56 = bf16[1152,1024]{1,0:T(8,128)(2,1)S(1)} collective-permute-done((bf16[1152,1024]{1,0:T(8,128)(2,1)S(1)}, bf16[1152,1024]{1,0:T(8,128)(2,1)S(1)}, u32[]{:S(2)}, u32[]{:S(2)}) %collective-permute-start.56) | collective-permute-done | bytes 2359328 | tf_op jit(solution)/shard_map/ppermute | solution.py:290
  571.1 5.1 add_convert_fusion
  580.2 5.4 collective-permute-done.49
  588.9 11.6 %collective-permute-done.57 = bf16[576,1024]{1,0:T(8,128)(2,1)S(1)} collective-permute-done((bf16[576,1024]{1,0:T(8,128)(2,1)S(1)}, bf16[576,1024]{1,0:T(8,128)(2,1)S(1)}, u32[]{:S(2)}, u32[]{:S(2)}) %collective-permute-start.57) | collective-permute-done | bytes 1179680 | tf_op jit(solution)/shard_map/ppermute | solution.py:293
  603.5 2.9 collective-permute-start.51
  606.6 16.3 %collective-permute-done.58 = bf16[288,1024]{1,0:T(8,128)(2,1)S(1)} collective-permute-done((bf16[288,1024]{1,0:T(8,128)(2,1)S(1)}, bf16[288,1024]{1,0:T(8,128)(2,1)S(1)}, u32[]{:S(2)}, u32[]{:S(2)}) %collective-permute-start.58) | collective-permute-done | bytes 589856 | tf_op jit(solution)/shard_map/ppermute | solution.py:293
  624.7 15.1 %collective-permute-done.59 = bf16[144,1024]{1,0:T(8,128)(2,1)S(1)} collective-permute-done((bf16[144,1024]{1,0:T(8,128)(2,1)S(1)}, bf16[144,1024]{1,0:T(8,128)(2,1)S(1)}, u32[]{:S(2)}, u32[]{:S(2)}) %collective-permute-start.59) | collective-permute-done | bytes 294944 | tf_op jit(solution)/shard_map/ppermute | solution.py:293
  640.3 7.9 %collective-permute-done.60 = bf16[144,1024]{1,0:T(8,128)(2,1)S(1)} collective-permute-done((bf16[144,1024]{1,0:T(8,128)(2,1)S(1)}, bf16[144,1024]{1,0:T(8,128)(2,1)S(1)}, u32[]{:S(2)}, u32[]{:S(2)}) %collective-permute-start.60) | collective-permute-done | bytes 294944 | tf_op jit(solution)/shard_map/ppermute | solution.py:293
  649.2 6.7 collective-permute-done.44
  656.1 2.7 collective-permute-done.61
  661.3 3.1 fusion.2
  664.5 4.0 collective-permute-done.53
  669.9 18.2 %collective-permute-done.62 = bf16[576,1024]{1,0:T(8,128)(2,1)S(1)} collective-permute-done((bf16[576,1024]{1,0:T(8,128)(2,1)S(1)}, bf16[576,1024]{1,0:T(8,128)(2,1)S(1)}, u32[]{:S(2)}, u32[]{:S(2)}) %collective-permute-start.62) | collective-permute-done | bytes 1179680 | tf_op jit(solution)/shard_map/ppermute | solution.py:293
  694.4 2.7 copy.111
  703.2 3.0 broadcast_select_fusion.1
  709.6 3.5 slice.293
  713.1 3.5 copy.113
  (512 shorter events, 180.6 us)
Async XLA Ops:
  2.6 81.0 %collective-permute-start = (bf16[256,768]{1,0:T(8,128)(2,1)}, bf16[256,768]{1,0:T(8,128)(2,1)}, u32[]{:S(2)}, u32[]{:S(2)}) collective-permute-start(bf16[256,768]{1,0:T(8,128)(2,1)} %slice_bitcast_fusion), channel_id=1, source_target_pairs={{0,1},{2,3},{4,5},{6,7},{8,9},{10,11},{12,13},{14,15},{16,17},{18,... | collective-permute-start | bytes 1179656 | tf_op jit(solution)/shard_map/ppermute | solution.py:368
  10.0 101.2 %collective-permute-start.1 = (bf16[576,384]{1,0:T(8,128)(2,1)}, bf16[576,384]{1,0:T(8,128)(2,1)}, u32[]{:S(2)}, u32[]{:S(2)}) collective-permute-start(bf16[576,384]{1,0:T(8,128)(2,1)} %constant_dynamic-slice_fusion.17), channel_id=1, source_target_pairs={{0,1},{1,0},{2,3},{3,2},{4,5},{5,4},{6,7},{7,6},{8,9},{9,8},{10,11... | collective-permute-start | bytes 1327112 | tf_op jit(solution)/shard_map/ppermute | solution.py:290
  11.6 18.3 %collective-permute-start.14 = (bf16[96,768]{1,0:T(8,128)(2,1)}, bf16[96,768]{1,0:T(8,128)(2,1)}, u32[]{:S(2)}, u32[]{:S(2)}) collective-permute-start(bf16[96,768]{1,0:T(8,128)(2,1)} %constant_dynamic-slice_fusion.13), channel_id=1, source_target_pairs={{0,1},{1,0},{2,3},{3,2},{4,5},{5,4},{6,7},{7,6},{8,9},{9,8},{10,11... | collective-permute-start | bytes 442376 | tf_op jit(solution)/shard_map/ppermute | solution.py:290
  14.6 18.4 %collective-permute-start.4 = (bf16[96,768]{1,0:T(8,128)(2,1)S(1)}, bf16[96,768]{1,0:T(8,128)(2,1)}, u32[]{:S(2)}, u32[]{:S(2)}) collective-permute-start(bf16[96,768]{1,0:T(8,128)(2,1)S(1)} %constant_dynamic-slice_fusion.16), channel_id=1, source_target_pairs={{0,1},{1,0},{2,3},{3,2},{4,5},{5,4},{6,7},{7,6},{8,9},{9,8},{10,11... | collective-permute-start | bytes 442376 | tf_op jit(solution)/shard_map/ppermute | solution.py:290
  15.6 19.8 %collective-permute-start.8 = (bf16[192,384]{1,0:T(8,128)(2,1)S(1)}, bf16[192,384]{1,0:T(8,128)(2,1)}, u32[]{:S(2)}, u32[]{:S(2)}) collective-permute-start(bf16[192,384]{1,0:T(8,128)(2,1)S(1)} %constant_dynamic-slice_fusion.15), channel_id=1, source_target_pairs={{0,1},{1,0},{2,3},{3,2},{4,5},{5,4},{6,7},{7,6},{8,9},{9,8},{10,11... | collective-permute-start | bytes 442376 | tf_op jit(solution)/shard_map/ppermute | solution.py:290
  29.9 8.1 %collective-permute-start.15 = (bf16[96,768]{1,0:T(8,128)(2,1)}, bf16[96,768]{1,0:T(8,128)(2,1)}, u32[]{:S(2)}, u32[]{:S(2)}) collective-permute-start(bf16[96,768]{1,0:T(8,128)(2,1)} %collective-permute-done.14), channel_id=1, source_target_pairs={{0,4},{2,6},{4,0},{6,2},{8,12},{10,14},{12,8},{14,10},{16,20},{18,... | collective-permute-start | bytes 442376 | tf_op jit(solution)/shard_map/ppermute | solution.py:293
  33.0 6.5 collective-permute-start.5
  35.4 115.4 %collective-permute-start.7 = (bf16[1024,768]{1,0:T(8,128)(2,1)}, bf16[1024,768]{1,0:T(8,128)(2,1)}, u32[]{:S(2)}, u32[]{:S(2)}) collective-permute-start(bf16[1024,768]{1,0:T(8,128)(2,1)} %bitcast.352), channel_id=1, source_target_pairs={{0,1},{1,0},{2,3},{3,2},{4,5},{5,4},{6,7},{7,6},{8,9},{9,8},{10,11... | collective-permute-start | bytes 4718600 | tf_op jit(solution)/shard_map/ppermute | solution.py:290
  38.1 62.0 %collective-permute-start.11 = (bf16[384,384]{1,0:T(8,128)(2,1)}, bf16[384,384]{1,0:T(8,128)(2,1)S(1)}, u32[]{:S(2)}, u32[]{:S(2)}) collective-permute-start(bf16[384,384]{1,0:T(8,128)(2,1)} %constant_dynamic-slice_fusion.14), channel_id=1, source_target_pairs={{0,1},{1,0},{2,3},{3,2},{4,5},{5,4},{6,7},{7,6},{8,9},{9,8},{10,11... | collective-permute-start | bytes 884744 | tf_op jit(solution)/shard_map/ppermute | solution.py:290
  40.1 5.4 collective-permute-start.9
  45.5 36.4 %collective-permute-start.21 = (bf16[128,768]{1,0:T(8,128)(2,1)}, bf16[128,768]{1,0:T(8,128)(2,1)S(1)}, u32[]{:S(2)}, u32[]{:S(2)}) collective-permute-start(bf16[128,768]{1,0:T(8,128)(2,1)} %constant_dynamic-slice_fusion.11), channel_id=1, source_target_pairs={{0,1},{1,0},{2,3},{3,2},{4,5},{5,4},{6,7},{7,6},{8,9},{9,8},{10,11... | collective-permute-start | bytes 589832 | tf_op jit(solution)/shard_map/ppermute | solution.py:290
  81.8 27.8 %collective-permute-start.17 = (bf16[192,1024]{1,0:T(8,128)(2,1)S(1)}, bf16[192,1024]{1,0:T(8,128)(2,1)S(1)}, u32[]{:S(2)}, u32[]{:S(2)}) collective-permute-start(bf16[192,1024]{1,0:T(8,128)(2,1)S(1)} %constant_dynamic-slice_fusion.12), channel_id=1, source_target_pairs={{0,1},{1,0},{2,3},{3,2},{4,5},{5,4},{6,7},{7,6},{8,9},{9,8},{10,11... | collective-permute-start | bytes 1179656 | tf_op jit(solution)/shard_map/ppermute | solution.py:290
  83.6 16.5 %collective-permute-start.22 = (bf16[128,768]{1,0:T(8,128)(2,1)S(1)}, bf16[128,768]{1,0:T(8,128)(2,1)S(1)}, u32[]{:S(2)}, u32[]{:S(2)}) collective-permute-start(bf16[128,768]{1,0:T(8,128)(2,1)S(1)} %collective-permute-done.21), channel_id=1, source_target_pairs={{0,8},{2,10},{4,12},{6,14},{8,0},{10,2},{12,4},{14,6},{16,24},{18,... | collective-permute-start | bytes 589832 | tf_op jit(solution)/shard_map/ppermute | solution.py:293
  100.0 1.7 collective-permute-start.6
  100.1 9.4 %collective-permute-start.12 = (bf16[384,384]{1,0:T(8,128)(2,1)S(1)}, bf16[384,384]{1,0:T(8,128)(2,1)S(1)}, u32[]{:S(2)}, u32[]{:S(2)}) collective-permute-start(bf16[384,384]{1,0:T(8,128)(2,1)S(1)} %collective-permute-done.11), channel_id=1, source_target_pairs={{0,4},{2,6},{4,0},{6,2},{8,12},{10,14},{12,8},{14,10},{16,20},{18,... | collective-permute-start | bytes 884744 | tf_op jit(solution)/shard_map/ppermute | solution.py:293
  101.8 9.4 %collective-permute-start.10 = (bf16[384,384]{1,0:T(8,128)(2,1)S(1)}, bf16[384,384]{1,0:T(8,128)(2,1)S(1)}, u32[]{:S(2)}, u32[]{:S(2)}) collective-permute-start(bf16[384,384]{1,0:T(8,128)(2,1)S(1)} %pad_maximum_fusion.42), channel_id=1, source_target_pairs={{0,2},{2,0},{4,6},{6,4},{8,10},{10,8},{12,14},{14,12},{16,18},{18,... | collective-permute-start | bytes 884744 | tf_op jit(solution)/shard_map/ppermute | solution.py:293
  109.5 3.7 collective-permute-start.16
  109.6 13.5 %collective-permute-start.23 = (bf16[256,768]{1,0:T(8,128)(2,1)S(1)}, bf16[256,768]{1,0:T(8,128)(2,1)S(1)}, u32[]{:S(2)}, u32[]{:S(2)}) collective-permute-start(bf16[256,768]{1,0:T(8,128)(2,1)S(1)} %pad_maximum_fusion.34), channel_id=1, source_target_pairs={{0,4},{2,6},{4,0},{6,2},{8,12},{10,14},{12,8},{14,10},{16,20},{18,... | collective-permute-start | bytes 1179656 | tf_op jit(solution)/shard_map/ppermute | solution.py:293
  111.2 11.2 %collective-permute-start.18 = (bf16[192,1024]{1,0:T(8,128)(2,1)S(1)}, bf16[192,1024]{1,0:T(8,128)(2,1)S(1)}, u32[]{:S(2)}, u32[]{:S(2)}) collective-permute-start(bf16[192,1024]{1,0:T(8,128)(2,1)S(1)} %collective-permute-done.17), channel_id=1, source_target_pairs={{0,8},{2,10},{4,12},{6,14},{8,0},{10,2},{12,4},{14,6},{16,24},{18,... | collective-permute-start | bytes 1179656 | tf_op jit(solution)/shard_map/ppermute | solution.py:293
  111.2 19.9 %collective-permute-start.2 = (bf16[576,384]{1,0:T(8,128)(2,1)}, bf16[576,384]{1,0:T(8,128)(2,1)S(1)}, u32[]{:S(2)}, u32[]{:S(2)}) collective-permute-start(bf16[576,384]{1,0:T(8,128)(2,1)} %collective-permute-done.1), channel_id=1, source_target_pairs={{0,4},{2,6},{4,0},{6,2},{8,12},{10,14},{12,8},{14,10},{16,20},{18,... | collective-permute-start | bytes 1327112 | tf_op jit(solution)/shard_map/ppermute | solution.py:293
  113.2 19.1 %collective-permute-start.13 = (bf16[768,384]{1,0:T(8,128)(2,1)S(1)}, bf16[768,384]{1,0:T(8,128)(2,1)S(1)}, u32[]{:S(2)}, u32[]{:S(2)}) collective-permute-start(bf16[768,384]{1,0:T(8,128)(2,1)S(1)} %pad_maximum_fusion.29), channel_id=1, source_target_pairs={{0,2},{2,0},{4,6},{6,4},{8,10},{10,8},{12,14},{14,12},{16,18},{18,... | collective-permute-start | bytes 1769480 | tf_op jit(solution)/shard_map/ppermute | solution.py:293
  122.6 25.0 %collective-permute-start.19 = (bf16[384,1024]{1,0:T(8,128)(2,1)S(1)}, bf16[384,1024]{1,0:T(8,128)(2,1)S(1)}, u32[]{:S(2)}, u32[]{:S(2)}) collective-permute-start(bf16[384,1024]{1,0:T(8,128)(2,1)S(1)} %pad_maximum_fusion.25), channel_id=1, source_target_pairs={{0,4},{2,6},{4,0},{6,2},{8,12},{10,14},{12,8},{14,10},{16,20},{18,... | collective-permute-start | bytes 2359304 | tf_op jit(solution)/shard_map/ppermute | solution.py:293
  123.3 26.0 %collective-permute-start.24 = (bf16[512,768]{1,0:T(8,128)(2,1)S(1)}, bf16[512,768]{1,0:T(8,128)(2,1)S(1)}, u32[]{:S(2)}, u32[]{:S(2)}) collective-permute-start(bf16[512,768]{1,0:T(8,128)(2,1)S(1)} %pad_maximum_fusion.26), channel_id=1, source_target_pairs={{0,2},{2,0},{4,6},{6,4},{8,10},{10,8},{12,14},{14,12},{16,18},{18,... | collective-permute-start | bytes 2359304 | tf_op jit(solution)/shard_map/ppermute | solution.py:293
  132.3 25.3 %collective-permute-start.3 = (bf16[1152,384]{1,0:T(8,128)(2,1)S(1)}, bf16[1152,384]{1,0:T(8,128)(2,1)S(1)}, u32[]{:S(2)}, u32[]{:S(2)}) collective-permute-start(bf16[1152,384]{1,0:T(8,128)(2,1)S(1)} %pad_maximum_fusion.24), channel_id=1, source_target_pairs={{0,2},{2,0},{4,6},{6,4},{8,10},{10,8},{12,14},{14,12},{16,18},{18,... | collective-permute-start | bytes 2654216 | tf_op jit(solution)/shard_map/ppermute | solution.py:293
  149.3 95.8 %collective-permute-start.20 = (bf16[768,1024]{1,0:T(8,128)(2,1)}, bf16[768,1024]{1,0:T(8,128)(2,1)}, u32[]{:S(2)}, u32[]{:S(2)}) collective-permute-start(bf16[768,1024]{1,0:T(8,128)(2,1)} %pad_maximum_fusion.10), channel_id=1, source_target_pairs={{0,2},{2,0},{4,6},{6,4},{8,10},{10,8},{12,14},{14,12},{16,18},{18,... | collective-permute-start | bytes 4718600 | tf_op jit(solution)/shard_map/ppermute | solution.py:293
  350.8 80.9 %collective-permute-start.25 = (bf16[256,768]{1,0:T(8,128)(2,1)}, bf16[256,768]{1,0:T(8,128)(2,1)}, u32[]{:S(2)}, u32[]{:S(2)}) collective-permute-start(bf16[256,768]{1,0:T(8,128)(2,1)} %slice.375), channel_id=1, source_target_pairs={{1,0},{3,2},{5,4},{7,6},{9,8},{11,10},{13,12},{15,14},{17,16},{19,... | collective-permute-start | bytes 1179656 | tf_op jit(solution)/shard_map/ppermute | solution.py:479
  367.1 54.3 %collective-permute-start.27 = (f32[8,768]{1,0:T(8,128)}, f32[8,768]{1,0:T(8,128)}, u32[]{:S(2)}, u32[]{:S(2)}) collective-permute-start(f32[8,768]{1,0:T(8,128)} %scatter.44), channel_id=1, source_target_pairs={{0,1},{1,0},{2,3},{3,2},{4,5},{5,4},{6,7},{7,6},{8,9},{9,8},{10,11... | collective-permute-start | bytes 73736 | tf_op jit(solution)/shard_map/ppermute | solution.py:290
  390.1 59.6 %collective-permute-start.37 = (bf16[3072,384]{1,0:T(8,128)(2,1)}, bf16[3072,384]{1,0:T(8,128)(2,1)}, u32[]{:S(2)}, u32[]{:S(2)}) collective-permute-start(bf16[3072,384]{1,0:T(8,128)(2,1)} %pad_maximum_fusion.2), channel_id=1, source_target_pairs={{0,2},{2,0},{4,6},{6,4},{8,10},{10,8},{12,14},{14,12},{16,18},{18,... | collective-permute-start | bytes 7077896 | tf_op jit(solution)/shard_map/ppermute | solution.py:293
  397.2 58.2 %collective-permute-start.55 = (bf16[2304,1024]{1,0:T(8,128)(2,1)}, bf16[2304,1024]{1,0:T(8,128)(2,1)}, u32[]{:S(2)}, u32[]{:S(2)}) collective-permute-start(bf16[2304,1024]{1,0:T(8,128)(2,1)} %pad_maximum_fusion), channel_id=1, source_target_pairs={{0,2},{2,0},{4,6},{6,4},{8,10},{10,8},{12,14},{14,12},{16,18},{18,... | collective-permute-start | bytes 14155784 | tf_op jit(solution)/shard_map/ppermute | solution.py:293
  422.7 1.2 collective-permute-start.28
  423.9 3.8 collective-permute-start.29
  427.7 3.9 collective-permute-start.30
  428.1 24.9 %collective-permute-start.46 = (bf16[3072,384]{1,0:T(8,128)(2,1)S(1)}, bf16[3072,384]{1,0:T(8,128)(2,1)S(1)}, u32[]{:S(2)}, u32[]{:S(2)}) collective-permute-start(bf16[3072,384]{1,0:T(8,128)(2,1)S(1)} %pad_maximum_fusion.5), channel_id=1, source_target_pairs={{0,2},{2,0},{4,6},{6,4},{8,10},{10,8},{12,14},{14,12},{16,18},{18,... | collective-permute-start | bytes 7077896 | tf_op jit(solution)/shard_map/ppermute | solution.py:293
  431.6 4.8 collective-permute-start.31
  433.6 4.2 collective-permute-start.32
  436.4 223.7 %collective-permute-start.26 = (bf16[1024,768]{1,0:T(8,128)(2,1)S(1)}, bf16[1024,768]{1,0:T(8,128)(2,1)S(1)}, u32[]{:S(2)}, u32[]{:S(2)}) collective-permute-start(bf16[1024,768]{1,0:T(8,128)(2,1)S(1)} %copy-done.95), channel_id=1, source_target_pairs={{0,1},{1,0},{2,3},{3,2},{4,5},{5,4},{6,7},{7,6},{8,9},{9,8},{10,11... | collective-permute-start | bytes 4718600 | tf_op jit(solution)/shard_map/ppermute | solution.py:290
  437.9 1.2 collective-permute-start.33
  439.1 3.9 collective-permute-start.34
  443.0 3.8 collective-permute-start.35
  446.8 15.1 %collective-permute-start.36 = (f32[8,768]{1,0:T(8,128)S(1)}, f32[8,768]{1,0:T(8,128)S(1)}, u32[]{:S(2)}, u32[]{:S(2)}) collective-permute-start(f32[8,768]{1,0:T(8,128)S(1)} %add.414), channel_id=1, source_target_pairs={{0,16},{2,18},{4,20},{6,22},{8,24},{10,26},{12,28},{14,30},{16,0},... | collective-permute-start | bytes 73736 | tf_op jit(solution)/shard_map/ppermute | solution.py:293
  452.9 46.1 %collective-permute-start.38 = (bf16[1536,384]{1,0:T(8,128)(2,1)S(1)}, bf16[1536,384]{1,0:T(8,128)(2,1)S(1)}, u32[]{:S(2)}, u32[]{:S(2)}) collective-permute-start(bf16[1536,384]{1,0:T(8,128)(2,1)S(1)} %add_convert_fusion.8), channel_id=1, source_target_pairs={{0,1},{1,0},{2,3},{3,2},{4,5},{5,4},{6,7},{7,6},{8,9},{9,8},{10,11... | collective-permute-start | bytes 3538952 | tf_op jit(solution)/shard_map/ppermute | solution.py:290
  453.4 70.9 %collective-permute-start.47 = (bf16[1536,384]{1,0:T(8,128)(2,1)S(1)}, bf16[1536,384]{1,0:T(8,128)(2,1)S(1)}, u32[]{:S(2)}, u32[]{:S(2)}) collective-permute-start(bf16[1536,384]{1,0:T(8,128)(2,1)S(1)} %add_convert_fusion.5), channel_id=1, source_target_pairs={{0,1},{1,0},{2,3},{3,2},{4,5},{5,4},{6,7},{7,6},{8,9},{9,8},{10,11... | collective-permute-start | bytes 3538952 | tf_op jit(solution)/shard_map/ppermute | solution.py:290
  460.2 110.9 %collective-permute-start.56 = (bf16[1152,1024]{1,0:T(8,128)(2,1)S(1)}, bf16[1152,1024]{1,0:T(8,128)(2,1)S(1)}, u32[]{:S(2)}, u32[]{:S(2)}) collective-permute-start(bf16[1152,1024]{1,0:T(8,128)(2,1)S(1)} %add_convert_fusion.1), channel_id=1, source_target_pairs={{0,1},{1,0},{2,3},{3,2},{4,5},{5,4},{6,7},{7,6},{8,9},{9,8},{10,11... | collective-permute-start | bytes 7077896 | tf_op jit(solution)/shard_map/ppermute | solution.py:290
  502.6 22.4 %collective-permute-start.39 = (bf16[768,384]{1,0:T(8,128)(2,1)S(1)}, bf16[768,384]{1,0:T(8,128)(2,1)S(1)}, u32[]{:S(2)}, u32[]{:S(2)}) collective-permute-start(bf16[768,384]{1,0:T(8,128)(2,1)S(1)} %constant_dynamic-slice_fusion.10), channel_id=1, source_target_pairs={{0,4},{2,6},{4,0},{6,2},{8,12},{10,14},{12,8},{14,10},{16,20},{18,... | collective-permute-start | bytes 1769480 | tf_op jit(solution)/shard_map/ppermute | solution.py:293
  524.9 51.7 %collective-permute-start.48 = (bf16[768,384]{1,0:T(8,128)(2,1)S(1)}, bf16[768,384]{1,0:T(8,128)(2,1)S(1)}, u32[]{:S(2)}, u32[]{:S(2)}) collective-permute-start(bf16[768,384]{1,0:T(8,128)(2,1)S(1)} %constant_dynamic-slice_fusion.5), channel_id=1, source_target_pairs={{0,4},{2,6},{4,0},{6,2},{8,12},{10,14},{12,8},{14,10},{16,20},{18,... | collective-permute-start | bytes 1769480 | tf_op jit(solution)/shard_map/ppermute | solution.py:293
  525.2 52.6 %collective-permute-start.40 = (bf16[384,384]{1,0:T(8,128)(2,1)S(1)}, bf16[384,384]{1,0:T(8,128)(2,1)S(1)}, u32[]{:S(2)}, u32[]{:S(2)}) collective-permute-start(bf16[384,384]{1,0:T(8,128)(2,1)S(1)} %constant_dynamic-slice_fusion.9), channel_id=1, source_target_pairs={{0,8},{2,10},{4,12},{6,14},{8,0},{10,2},{12,4},{14,6},{16,24},{18,... | collective-permute-start | bytes 884744 | tf_op jit(solution)/shard_map/ppermute | solution.py:293
  576.3 24.2 %collective-permute-start.57 = (bf16[576,1024]{1,0:T(8,128)(2,1)S(1)}, bf16[576,1024]{1,0:T(8,128)(2,1)S(1)}, u32[]{:S(2)}, u32[]{:S(2)}) collective-permute-start(bf16[576,1024]{1,0:T(8,128)(2,1)S(1)} %constant_dynamic-slice_fusion.2), channel_id=1, source_target_pairs={{0,4},{2,6},{4,0},{6,2},{8,12},{10,14},{12,8},{14,10},{16,20},{18,... | collective-permute-start | bytes 3538952 | tf_op jit(solution)/shard_map/ppermute | solution.py:293
  576.8 8.8 %collective-permute-start.49 = (bf16[384,384]{1,0:T(8,128)(2,1)S(1)}, bf16[384,384]{1,0:T(8,128)(2,1)S(1)}, u32[]{:S(2)}, u32[]{:S(2)}) collective-permute-start(bf16[384,384]{1,0:T(8,128)(2,1)S(1)} %constant_dynamic-slice_fusion.4), channel_id=1, source_target_pairs={{0,8},{2,10},{4,12},{6,14},{8,0},{10,2},{12,4},{14,6},{16,24},{18,... | collective-permute-start | bytes 884744 | tf_op jit(solution)/shard_map/ppermute | solution.py:293
  578.0 10.0 %collective-permute-start.41 = (bf16[192,384]{1,0:T(8,128)(2,1)S(1)}, bf16[192,384]{1,0:T(8,128)(2,1)S(1)}, u32[]{:S(2)}, u32[]{:S(2)}) collective-permute-start(bf16[192,384]{1,0:T(8,128)(2,1)S(1)} %constant_dynamic-slice_fusion.8), channel_id=1, source_target_pairs={{0,16},{2,18},{4,20},{6,22},{8,24},{10,26},{12,28},{14,30},{16,0},... | collective-permute-start | bytes 442376 | tf_op jit(solution)/shard_map/ppermute | solution.py:293
  585.8 17.7 %collective-permute-start.50 = (bf16[192,384]{1,0:T(8,128)(2,1)S(1)}, bf16[192,384]{1,0:T(8,128)(2,1)S(1)}, u32[]{:S(2)}, u32[]{:S(2)}) collective-permute-start(bf16[192,384]{1,0:T(8,128)(2,1)S(1)} %constant_dynamic-slice_fusion.3), channel_id=1, source_target_pairs={{0,16},{2,18},{4,20},{6,22},{8,24},{10,26},{12,28},{14,30},{16,0},... | collective-permute-start | bytes 442376 | tf_op jit(solution)/shard_map/ppermute | solution.py:293
  588.0 18.4 %collective-permute-start.42 = (bf16[192,384]{1,0:T(8,128)(2,1)S(1)}, bf16[192,384]{1,0:T(8,128)(2,1)S(1)}, u32[]{:S(2)}, u32[]{:S(2)}) collective-permute-start(bf16[192,384]{1,0:T(8,128)(2,1)S(1)} %add_convert_fusion.17), channel_id=1, source_target_pairs={{0,16},{2,18},{4,20},{6,22},{8,24},{10,26},{12,28},{14,30},{16,0},... | collective-permute-start | bytes 442376 | tf_op jit(solution)/shard_map/ppermute | solution.py:293
  601.0 21.9 %collective-permute-start.58 = (bf16[288,1024]{1,0:T(8,128)(2,1)S(1)}, bf16[288,1024]{1,0:T(8,128)(2,1)S(1)}, u32[]{:S(2)}, u32[]{:S(2)}) collective-permute-start(bf16[288,1024]{1,0:T(8,128)(2,1)S(1)} %constant_dynamic-slice_fusion.1), channel_id=1, source_target_pairs={{0,8},{2,10},{4,12},{6,14},{8,0},{10,2},{12,4},{14,6},{16,24},{18,... | collective-permute-start | bytes 1769480 | tf_op jit(solution)/shard_map/ppermute | solution.py:293
  603.5 19.8 %collective-permute-start.51 = (bf16[192,384]{1,0:T(8,128)(2,1)S(1)}, bf16[192,384]{1,0:T(8,128)(2,1)S(1)}, u32[]{:S(2)}, u32[]{:S(2)}) collective-permute-start(bf16[192,384]{1,0:T(8,128)(2,1)S(1)} %add_convert_fusion.16), channel_id=1, source_target_pairs={{0,16},{2,18},{4,20},{6,22},{8,24},{10,26},{12,28},{14,30},{16,0},... | collective-permute-start | bytes 442376 | tf_op jit(solution)/shard_map/ppermute | solution.py:293
  606.5 33.5 %collective-permute-start.43 = (bf16[384,384]{1,0:T(8,128)(2,1)S(1)}, bf16[384,384]{1,0:T(8,128)(2,1)S(1)}, u32[]{:S(2)}, u32[]{:S(2)}) collective-permute-start(bf16[384,384]{1,0:T(8,128)(2,1)S(1)} %pad_maximum_fusion.44), channel_id=1, source_target_pairs={{0,8},{2,10},{4,12},{6,14},{8,0},{10,2},{12,4},{14,6},{16,24},{18,... | collective-permute-start | bytes 884744 | tf_op jit(solution)/shard_map/ppermute | solution.py:293
  623.2 16.6 %collective-permute-start.59 = (bf16[144,1024]{1,0:T(8,128)(2,1)S(1)}, bf16[144,1024]{1,0:T(8,128)(2,1)S(1)}, u32[]{:S(2)}, u32[]{:S(2)}) collective-permute-start(bf16[144,1024]{1,0:T(8,128)(2,1)S(1)} %constant_dynamic-slice_fusion), channel_id=1, source_target_pairs={{0,16},{2,18},{4,20},{6,22},{8,24},{10,26},{12,28},{14,30},{16,0},... | collective-permute-start | bytes 884744 | tf_op jit(solution)/shard_map/ppermute | solution.py:293
  623.4 25.0 %collective-permute-start.52 = (bf16[384,384]{1,0:T(8,128)(2,1)S(1)}, bf16[384,384]{1,0:T(8,128)(2,1)S(1)}, u32[]{:S(2)}, u32[]{:S(2)}) collective-permute-start(bf16[384,384]{1,0:T(8,128)(2,1)S(1)} %pad_maximum_fusion.45), channel_id=1, source_target_pairs={{0,8},{2,10},{4,12},{6,14},{8,0},{10,2},{12,4},{14,6},{16,24},{18,... | collective-permute-start | bytes 884744 | tf_op jit(solution)/shard_map/ppermute | solution.py:293
  639.9 8.2 %collective-permute-start.60 = (bf16[144,1024]{1,0:T(8,128)(2,1)S(1)}, bf16[144,1024]{1,0:T(8,128)(2,1)S(1)}, u32[]{:S(2)}, u32[]{:S(2)}) collective-permute-start(bf16[144,1024]{1,0:T(8,128)(2,1)S(1)} %add_convert_fusion.13), channel_id=1, source_target_pairs={{0,16},{2,18},{4,20},{6,22},{8,24},{10,26},{12,28},{14,30},{16,0},... | collective-permute-start | bytes 884744 | tf_op jit(solution)/shard_map/ppermute | solution.py:293
  640.2 15.7 %collective-permute-start.44 = (bf16[768,384]{1,0:T(8,128)(2,1)S(1)}, bf16[768,384]{1,0:T(8,128)(2,1)S(1)}, u32[]{:S(2)}, u32[]{:S(2)}) collective-permute-start(bf16[768,384]{1,0:T(8,128)(2,1)S(1)} %pad_maximum_fusion.31), channel_id=1, source_target_pairs={{0,4},{2,6},{4,0},{6,2},{8,12},{10,14},{12,8},{14,10},{16,20},{18,... | collective-permute-start | bytes 1769480 | tf_op jit(solution)/shard_map/ppermute | solution.py:293
  648.3 10.5 %collective-permute-start.61 = (bf16[288,1024]{1,0:T(8,128)(2,1)S(1)}, bf16[288,1024]{1,0:T(8,128)(2,1)S(1)}, u32[]{:S(2)}, u32[]{:S(2)}) collective-permute-start(bf16[288,1024]{1,0:T(8,128)(2,1)S(1)} %pad_maximum_fusion.33), channel_id=1, source_target_pairs={{0,8},{2,10},{4,12},{6,14},{8,0},{10,2},{12,4},{14,6},{16,24},{18,... | collective-permute-start | bytes 1769480 | tf_op jit(solution)/shard_map/ppermute | solution.py:293
  648.6 19.9 %collective-permute-start.53 = (bf16[768,384]{1,0:T(8,128)(2,1)S(1)}, bf16[768,384]{1,0:T(8,128)(2,1)S(1)}, u32[]{:S(2)}, u32[]{:S(2)}) collective-permute-start(bf16[768,384]{1,0:T(8,128)(2,1)S(1)} %pad_maximum_fusion.32), channel_id=1, source_target_pairs={{0,4},{2,6},{4,0},{6,2},{8,12},{10,14},{12,8},{14,10},{16,20},{18,... | collective-permute-start | bytes 1769480 | tf_op jit(solution)/shard_map/ppermute | solution.py:293
  659.2 28.9 %collective-permute-start.62 = (bf16[576,1024]{1,0:T(8,128)(2,1)S(1)}, bf16[576,1024]{1,0:T(8,128)(2,1)S(1)}, u32[]{:S(2)}, u32[]{:S(2)}) collective-permute-start(bf16[576,1024]{1,0:T(8,128)(2,1)S(1)} %pad_maximum_fusion.21), channel_id=1, source_target_pairs={{0,4},{2,6},{4,0},{6,2},{8,12},{10,14},{12,8},{14,10},{16,20},{18,... | collective-permute-start | bytes 3538952 | tf_op jit(solution)/shard_map/ppermute | solution.py:293
  660.0 30.3 %collective-permute-start.45 = (bf16[1536,384]{1,0:T(8,128)(2,1)S(1)}, bf16[1536,384]{1,0:T(8,128)(2,1)S(1)}, u32[]{:S(2)}, u32[]{:S(2)}) collective-permute-start(bf16[1536,384]{1,0:T(8,128)(2,1)S(1)} %pad_maximum_fusion.19), channel_id=1, source_target_pairs={{0,2},{2,0},{4,6},{6,4},{8,10},{10,8},{12,14},{14,12},{16,18},{18,... | collective-permute-start | bytes 3538952 | tf_op jit(solution)/shard_map/ppermute | solution.py:293
  669.9 27.2 %collective-permute-start.54 = (bf16[1536,384]{1,0:T(8,128)(2,1)}, bf16[1536,384]{1,0:T(8,128)(2,1)}, u32[]{:S(2)}, u32[]{:S(2)}) collective-permute-start(bf16[1536,384]{1,0:T(8,128)(2,1)} %pad_maximum_fusion.20), channel_id=1, source_target_pairs={{0,2},{2,0},{4,6},{6,4},{8,10},{10,8},{12,14},{14,12},{16,18},{18,... | collective-permute-start | bytes 3538952 | tf_op jit(solution)/shard_map/ppermute | solution.py:293
  690.3 12.9 %collective-permute-start.63 = (bf16[1152,1024]{1,0:T(8,128)(2,1)}, bf16[1152,1024]{1,0:T(8,128)(2,1)}, u32[]{:S(2)}, u32[]{:S(2)}) collective-permute-start(bf16[1152,1024]{1,0:T(8,128)(2,1)} %pad_maximum_fusion.6), channel_id=1, source_target_pairs={{0,2},{2,0},{4,6},{6,4},{8,10},{10,8},{12,14},{14,12},{16,18},{18,... | collective-permute-start | bytes 7077896 | tf_op jit(solution)/shard_map/ppermute | solution.py:293
  (104 other events, 1621.6 us)

commit v2 on v0

v2 whole, which is shorter than its diff:
```python
import functools
import types

import jax
import jax.numpy as jnp
from jax import lax
from jax.experimental import pallas as pl
from jax.experimental.pallas import tpu as pltpu
from jax.sharding import PartitionSpec as P

HD = 64
EPSILON = 1e-06
NEGATIVE = -1e30
BQ = 128
BK = 256
F32 = jnp.float32
BF16 = jnp.bfloat16


def rows_of_two_heads(block):
    lane = lax.broadcasted_iota(jnp.int32, block.shape, 1)
    zero = jnp.zeros_like(block)
    return jnp.concatenate([jnp.where(lane < HD, block, zero), jnp.where(lane >= HD, block, zero)], axis=0)


def heads_side_by_side(wide):
    return jnp.concatenate([wide[:HD, :BQ], wide[HD:, BQ:]], axis=0).T


def columns_of_two_heads(block):
    turned = block.T
    row = lax.broadcasted_iota(jnp.int32, turned.shape, 0)
    zero = jnp.zeros_like(turned)
    return jnp.concatenate([jnp.where(row < HD, turned, zero), jnp.where(row >= HD, turned, zero)], axis=1)


def twice(row):
    return jnp.concatenate([row, row], axis=1)


def pair(g):
    return slice(2 * HD * g, 2 * HD * (g + 1))


def mask_of(interval_ref, part, b):
    first = interval_ref[2 * part, pl.ds(b, 1), :]
    last = interval_ref[2 * part + 1, pl.ds(b, 1), :]
    return twice(first), twice(last)


def blocks_of(first, last, n_keys):
    low = jnp.min(first.astype(F32)).astype(jnp.int32)
    high = jnp.max(last.astype(F32)).astype(jnp.int32)
    return jnp.clip(low, 0, n_keys) // BK, (jnp.clip(high, 0, n_keys) + BK - 1) // BK


def seen(first, last, j):
    key_iota = lax.broadcasted_iota(jnp.int32, (BK, 2 * BQ), 0)
    return (key_iota >= first - j * BK) & (key_iota < last - j * BK)


def plan_kernel(side_ref, tokens_ref, patches_ref, interval_ref, *, own_len, mem_len, halo):
    side = side_ref[0]
    first_own = side * own_len - halo
    n_blocks = own_len // BQ
    tokens, patches = tokens_ref[...], patches_ref[...]
    tokens_below, patches_below = [], []
    for segment in range(9):
        tokens_below.append(jnp.sum((tokens < segment).astype(F32), axis=1, keepdims=True))
        patches_below.append(jnp.sum((patches < segment).astype(F32), axis=1, keepdims=True))
    for b in range(n_blocks):
        own = tokens_ref[:, pl.ds(pl.multiple_of(side * own_len + b * BQ, BQ), BQ)]
        start_a, start_c, end_c = (jnp.zeros((1, BQ), F32) for _ in range(3))
        for segment in range(8):
            here = own == segment
            start_a = jnp.where(here, tokens_below[segment], start_a)
            start_c = jnp.where(here, patches_below[segment], start_c)
            end_c = jnp.where(here, patches_below[segment + 1], end_c)
        start_a, start_c, end_c = (x.astype(jnp.int32) for x in (start_a, start_c, end_c))
        place = lax.broadcasted_iota(jnp.int32, (1, BQ), 1) + (b * BQ + halo + 1)
        own_base, other_base = side * mem_len, (1 - side) * mem_len
        rows = (
            start_a - first_own,
            place,
            start_c - own_base,
            end_c - own_base,
            start_c - other_base,
            end_c - other_base,
        )
        for i, row in enumerate(rows):
            interval_ref[i, b : b + 1, :] = row


def make_plans(side, tokens, patches, own_len, mem_len, halo):
    intervals = pl.pallas_call(
        functools.partial(plan_kernel, own_len=own_len, mem_len=mem_len, halo=halo),
        grid_spec=pltpu.PrefetchScalarGridSpec(
            num_scalar_prefetch=1,
            grid=(1,),
            in_specs=[whole(tokens.shape), whole(patches.shape)],
            out_specs=whole((6, own_len // BQ, BQ)),
        ),
        out_shape=jax.ShapeDtypeStruct((6, own_len // BQ, BQ), jnp.int32),
        name="key_intervals",
    )(side.reshape(1).astype(jnp.int32), tokens, patches)
    return intervals


def forward_kernel(interval_ref, q_ref, *refs, first_part, n_parts, groups):
    key_refs, (out_ref, total_ref) = refs[: 2 * n_parts], refs[2 * n_parts :]
    b = pl.program_id(0)
    q_wide = []
    for g in range(groups):
        queries = q_ref[:, pair(g)].astype(F32) * (HD**-0.5)
        q_wide.append(columns_of_two_heads(queries).astype(BF16))
    carry = (
        (jnp.full((1, 2 * BQ), NEGATIVE, F32),) * groups,
        (jnp.zeros((1, 2 * BQ), F32),) * groups,
        (jnp.zeros((2 * HD, 2 * BQ), F32),) * groups,
    )
    for part in range(n_parts):
        k_ref, v_ref = key_refs[2 * part], key_refs[2 * part + 1]
        first, last = mask_of(interval_ref, first_part + part, b)
        low, high = blocks_of(first, last, k_ref.shape[0])

        def step(j, carry, k_ref=k_ref, v_ref=v_ref, first=first, last=last):
            rows = pl.ds(pl.multiple_of(j * BK, BK), BK)
            inside = seen(first, last, j)
            peaks, totals, accs = [], [], []
            scores = [
                jnp.where(inside, jnp.dot(k_ref[rows, pair(g)], q_wide[g], preferred_element_type=F32), NEGATIVE)
                for g in range(groups)
            ]
            for g in range(groups):
                peak, total, acc = (c[g] for c in carry)
                new_peak = jnp.maximum(peak, jnp.max(scores[g], axis=0, keepdims=True))
                shrink = jnp.exp(peak - new_peak)
                probs = jnp.exp(scores[g] - new_peak)
                peaks.append(new_peak)
                totals.append(total * shrink + jnp.sum(probs, axis=0, keepdims=True))
                accs.append(
                    acc * shrink
                    + lax.dot_general(
                        v_ref[rows, pair(g)],
                        probs.astype(BF16),
                        (((0,), (0,)), ((), ())),
                        preferred_element_type=F32,
                    )
                )
            return tuple(peaks), tuple(totals), tuple(accs)

        carry = lax.fori_loop(low, high, step, carry)
    for g in range(groups):
        peak, total, acc = (c[g] for c in carry)
        out_ref[:, pair(g)] = heads_side_by_side(acc / total).astype(BF16)
        total_ref[0, g : g + 1, :] = peak + jnp.log(total)


def backward_kernel(
    interval_ref, total_ref, q_ref, out_ref, grad_ref, *refs, first_part, n_parts, n_blocks, groups, q_offset, fused
):
    key_refs, refs = refs[: 2 * n_parts], refs[2 * n_parts :]
    if fused:
        (all_ref, dk_acc, dv_acc) = refs
        columns = all_ref.shape[1] // 3
    else:
        (dq_ref, dkv_ref, dk_acc, dv_acc) = refs
        columns = dq_ref.shape[1]
    b = pl.program_id(0)

    @pl.when(b == 0)
    def _():
        dk_acc[...] = jnp.zeros_like(dk_acc)
        dv_acc[...] = jnp.zeros_like(dv_acc)

    q_rows, q_wide, g_rows, g_wide, inner, log_total = [], [], [], [], [], []
    for g in range(groups):
        queries = q_ref[:, pair(g)].astype(F32) * (HD**-0.5)
        q_rows.append(rows_of_two_heads(queries).astype(BF16))
        q_wide.append(columns_of_two_heads(queries).astype(BF16))
        grad = grad_ref[:, pair(g)].astype(F32)
        g_rows.append(rows_of_two_heads(grad).astype(BF16))
        g_wide.append(columns_of_two_heads(grad).astype(BF16))
        product = (grad * out_ref[:, pair(g)].astype(F32)).T
        inner.append(
            jnp.concatenate(
                [jnp.sum(product[:HD], axis=0, keepdims=True), jnp.sum(product[HD:], axis=0, keepdims=True)], axis=1
            )
        )
        log_total.append(total_ref[0, g : g + 1, :])
    dq = (jnp.zeros((2 * HD, 2 * BQ), F32),) * groups
    base = 0
    for part in range(n_parts):
        k_ref, v_ref = key_refs[2 * part], key_refs[2 * part + 1]
        first, last = mask_of(interval_ref, first_part + part, b)
        low, high = blocks_of(first, last, k_ref.shape[0])

        def step(j, dq, k_ref=k_ref, v_ref=v_ref, first=first, last=last, base=base):
            rows = pl.ds(pl.multiple_of(j * BK, BK), BK)
            sums = pl.ds(pl.multiple_of(base + j * BK, BK), BK)
            inside = seen(first, last, j)
            new = []
            for g in range(groups):
                keys = k_ref[rows, pair(g)]
                scores = jnp.dot(keys, q_wide[g], preferred_element_type=F32)
                prob_grad = jnp.dot(v_ref[rows, pair(g)], g_wide[g], preferred_element_type=F32)
                probs = jnp.exp(jnp.where(inside, scores, NEGATIVE) - log_total[g])
                score_grad = (probs * (prob_grad - inner[g])).astype(BF16)
                dv_acc[sums, pair(g)] += jnp.dot(probs.astype(BF16), g_rows[g], preferred_element_type=F32)
                dk_acc[sums, pair(g)] += jnp.dot(score_grad, q_rows[g], preferred_element_type=F32)
                new.append(
                    dq[g]
                    + lax.dot_general(keys, score_grad, (((0,), (0,)), ((), ())), preferred_element_type=F32)
                )
            return tuple(new)

        dq = lax.fori_loop(low, high, step, dq)
        base += k_ref.shape[0]
    for g in range(groups):
        value = (heads_side_by_side(dq[g]) * (HD**-0.5)).astype(BF16)
        if fused:
            all_ref[pl.ds(pl.multiple_of(q_offset + b * BQ, BQ), BQ), pair(g)] = value
        else:
            dq_ref[:, pair(g)] = value

    @pl.when(b == n_blocks - 1)
    def _():
        if fused:
            if q_offset:
                all_ref[:q_offset, :columns] = jnp.zeros((q_offset, columns), BF16)
            all_ref[:, columns : 2 * columns] = dk_acc[...].astype(BF16)
            all_ref[:, 2 * columns :] = dv_acc[...].astype(BF16)
        else:
            dkv_ref[:, :columns] = dk_acc[...].astype(BF16)
            dkv_ref[:, columns:] = dv_acc[...].astype(BF16)


def row_block(columns, index=0, offset=0):
    return pl.BlockSpec((BQ, columns), lambda b, *_: (b + offset // BQ, index))


def whole(shape):
    return pl.BlockSpec(shape, lambda *_: (0,) * len(shape))


def params(mib):
    return pltpu.CompilerParams(dimension_semantics=("arbitrary",), vmem_limit_bytes=mib << 20)


def attend_forward(intervals, first_part, columns, q, parts, q_offset):
    q_array, q_index = q
    n_blocks = intervals.shape[1]
    length, groups = n_blocks * BQ, columns // (2 * HD)
    operands, specs = [intervals, q_array], [whole(intervals.shape), row_block(columns, q_index, q_offset)]
    for part in parts:
        operands += list(part)
        specs += [whole(x.shape) for x in part]
    return pl.pallas_call(
        functools.partial(forward_kernel, first_part=first_part, n_parts=len(parts), groups=groups),
        grid=(n_blocks,),
        in_specs=specs,
        out_specs=[row_block(columns), pl.BlockSpec((1, groups, 2 * BQ), lambda b: (b, 0, 0))],
        out_shape=[
            jax.ShapeDtypeStruct((length, columns), BF16),
            jax.ShapeDtypeStruct((n_blocks, groups, 2 * BQ), F32),
        ],
        compiler_params=params(14),
        cost_estimate=COST,
        name="attend_forward",
    )(*operands)


def attend_backward(intervals, first_part, columns, totals, q, out, out_grad, parts, q_offset, fused):
    q_array, q_index = q
    n_blocks = intervals.shape[1]
    length, groups = n_blocks * BQ, columns // (2 * HD)
    operands = [intervals, totals, q_array, out, out_grad]
    specs = [
        whole(intervals.shape),
        pl.BlockSpec((1, groups, 2 * BQ), lambda b: (b, 0, 0)),
        row_block(columns, q_index, q_offset),
        row_block(columns),
        row_block(columns),
    ]
    for part in parts:
        operands += list(part)
        specs += [whole(x.shape) for x in part]
    n_keys = sum(keys.shape[0] for keys, _ in parts)
    if fused:
        out_specs = [whole((n_keys, 3 * columns))]
        out_shape = [jax.ShapeDtypeStruct((n_keys, 3 * columns), BF16)]
    else:
        out_specs = [row_block(columns), whole((n_keys, 2 * columns))]
        out_shape = [
            jax.ShapeDtypeStruct((length, columns), BF16),
            jax.ShapeDtypeStruct((n_keys, 2 * columns), BF16),
        ]
    return pl.pallas_call(
        functools.partial(
            backward_kernel,
            first_part=first_part,
            n_parts=len(parts),
            n_blocks=n_blocks,
            groups=groups,
            q_offset=q_offset,
            fused=fused,
        ),
        grid=(n_blocks,),
        in_specs=specs,
        out_specs=out_specs,
        scratch_shapes=[pltpu.VMEM((n_keys, columns), F32), pltpu.VMEM((n_keys, columns), F32)],
        out_shape=out_shape,
        compiler_params=params(18 if fused else 26),
        cost_estimate=COST,
        name="attend_backward",
    )(*operands)


COST = pl.CostEstimate(flops=1 << 20, bytes_accessed=1 << 20, transcendentals=0)


def inverse_rms(rows):
    return lax.rsqrt(jnp.mean(rows * rows, axis=-1, keepdims=True) + EPSILON)


def normalize(rows, gain):
    return rows * inverse_rms(rows) * gain


def normalize_back(rows, gain, cotangent):
    inverse = inverse_rms(rows)
    unit = rows * inverse
    scaled = cotangent * gain
    grad = inverse * (scaled - unit * jnp.mean(scaled * unit, axis=-1, keepdims=True))
    return grad, jnp.sum(cotangent * unit, axis=0)


def gelu_parts(u):
    c = float((2.0 / jnp.pi) ** 0.5)
    t = jnp.tanh(c * (u + 0.044715 * u * u * u))
    half = 0.5 * (1.0 + t)
    slope = half + 0.5 * u * (1.0 - t * t) * (c * (1.0 + 3.0 * 0.044715 * u * u))
    return u * half, slope


def contract(a, b, i, j):
    return lax.dot_general(a, b, (((i,), (j,)), ((), ())), preferred_element_type=F32)


def nn(a, b):
    return contract(a, b, 1, 0)


def nt(a, b):
    return contract(a, b, 1, 1)


def tn(a, b):
    return contract(a, b, 0, 0)


def dot(a, b, i, j):
    return lax.dot_general(a, b, (((i,), (j,)), ((), ())), preferred_element_type=F32)


class Part:
    def __init__(self, array, columns=None, at=0, plane=None, row=0):
        self.array, self.at, self.plane, self.row = array, at, plane, row
        self.columns = array.shape[-1] if columns is None else columns

    def split(self, rows):
        at, row = self.at, self.row // rows
        return pl.BlockSpec((rows, self.columns), lambda i, *_: (row + i, at))

    def spec(self):
        if self.plane is None:
            at = self.at
            return pl.BlockSpec((self.array.shape[0], self.columns), lambda *_: (0, at))
        plane = self.plane
        return pl.BlockSpec((None,) + self.array.shape[1:], lambda *_: (plane, 0, 0))


def back_kernel(*refs, n, m, norm, stacked):
    grads, weights, refs = refs[:n], refs[n : 2 * n], refs[2 * n :]
    total = dot(grads[0][...], weights[0][...], 1, 1)
    for grad, weight in zip(grads[1:], weights[1:]):
        total = total + dot(grad[...], weight[...], 1, 1)
    if not norm:
        add, out_ref = refs[:-1], refs[-1]
        for ref in add:
            total = total + ref[...].astype(F32)
        out_ref[...] = total.astype(out_ref.dtype)
        return
    resid_ref, gain_ref, base_ref = refs[:3]
    out_weights, (grad_ref, full_ref, gain_out), outs = refs[3 : 3 + m], refs[3 + m : 6 + m], refs[6 + m :]
    rows = resid_ref[...]
    inverse = inverse_rms(rows)
    unit = rows * inverse
    scaled = total * gain_ref[...]
    grad = base_ref[...].astype(F32) + inverse * (scaled - unit * jnp.mean(scaled * unit, axis=-1, keepdims=True))
    grad_ref[...] = grad
    full = grad.astype(BF16)
    full_ref[...] = full

    @pl.when(pl.program_id(0) == 0)
    def _():
        gain_out[...] = jnp.zeros_like(gain_out)

    gain_out[...] += jnp.sum(total * unit, axis=0, keepdims=True)
    for weight, out in zip(out_weights, outs):
        out[...] = dot(full, weight[...], 1, 1).astype(BF16)


TILE = 256


def product_back(pairs, length, dtype, add=None):
    n, features = len(pairs), pairs[0][1].array.shape[-2]
    grads, weights = zip(*pairs)
    add = [] if add is None else [add]
    return pl.pallas_call(
        functools.partial(back_kernel, n=n, m=0, norm=False, stacked=0),
        grid=(length // TILE,),
        in_specs=[g.split(TILE) for g in grads] + [w.spec() for w in weights] + [Part(x).split(TILE) for x in add],
        out_specs=pl.BlockSpec((TILE, features), lambda i: (i, 0)),
        out_shape=jax.ShapeDtypeStruct((length, features), dtype),
        compiler_params=params(30),
        cost_estimate=COST,
        name="back",
    )(*[p.array for p in grads], *in_hbm([p.array for p in weights]), *add)


def norm_back(pairs, resid, gain, base, out_weights):
    n, m, (length, features) = len(pairs), len(out_weights), resid.shape
    grads, weights = zip(*pairs)
    tile = lambda x: Part(x).split(TILE)
    widths = [w.shape[0] for w in out_weights]
    return pl.pallas_call(
        functools.partial(back_kernel, n=n, m=m, norm=True, stacked=0),
        grid=(length // TILE,),
        in_specs=[g.split(TILE) for g in grads]
        + [w.spec() for w in weights]
        + [tile(resid), whole((1, features)), tile(base)]
        + [whole(w.shape) for w in out_weights],
        out_specs=[pl.BlockSpec((TILE, features), lambda i: (i, 0))] * 2
        + [whole((1, features))]
        + [pl.BlockSpec((TILE, w), lambda i: (i, 0)) for w in widths],
        out_shape=[
            jax.ShapeDtypeStruct((length, features), F32),
            jax.ShapeDtypeStruct((length, features), BF16),
            jax.ShapeDtypeStruct((1, features), F32),
        ]
        + [jax.ShapeDtypeStruct((length, w), BF16) for w in widths],
        compiler_params=params(34),
        cost_estimate=COST,
        name="norm_back",
    )(*[p.array for p in grads], *[p.array for p in weights], resid, gain.reshape(1, -1), base, *out_weights)


def weight_kernel(*refs, n, m):
    rows, grads, outs, turned = refs[:n], refs[n : n + m], refs[n + m : n + 2 * m], refs[-1]

    @pl.when(pl.program_id(0) == 0)
    def _():
        at = 0
        for ref in rows:
            for first in range(0, ref.shape[0], TILE):
                turned[:, at + first : at + first + TILE] = ref[first : first + TILE, :].astype(F32).T.astype(BF16)
            at += ref.shape[0]

    for grad, out in zip(grads, outs):
        out[...] = dot(turned[...], grad[...], 1, 0).astype(BF16)


def weight_grads(rows, grads, chunk):
    length, features = sum(x.shape[0] for x in rows), rows[0].shape[1]
    columns = grads[0].shape[1]
    return pl.pallas_call(
        functools.partial(weight_kernel, n=len(rows), m=len(grads)),
        grid=(columns // chunk,),
        in_specs=[whole(x.shape) for x in rows]
        + [pl.BlockSpec((length, chunk), lambda j: (0, j)) for _ in grads],
        out_specs=[pl.BlockSpec((features, chunk), lambda j: (0, j)) for _ in grads],
        out_shape=[jax.ShapeDtypeStruct((features, columns), BF16) for _ in grads],
        scratch_shapes=[pltpu.VMEM((features, length), BF16)],
        compiler_params=params(30),
        cost_estimate=COST,
        name="weight_grads",
    )(*rows, *grads)


def ffn_kernel(normed_ref, full_ref, gate_ref, up_ref, down_ref, hidden_ref, grads_ref, *, chunk, units):
    j = pl.program_id(0)
    gate = dot(normed_ref[...], gate_ref[...], 1, 0)
    up = dot(normed_ref[...], up_ref[...], 1, 0)
    hidden_grad = dot(full_ref[...], down_ref[...], 1, 1)
    act, slope = gelu_parts(gate)
    hidden_ref[...] = (act * up).astype(BF16)
    at = pl.multiple_of(j * chunk, chunk)
    grads_ref[:, pl.ds(at, chunk)] = (hidden_grad * up * slope).astype(BF16)
    grads_ref[:, pl.ds(pl.multiple_of(units + at, chunk), chunk)] = (hidden_grad * act).astype(BF16)


def feed_forward(normed, full, gate, up, down, chunk=256):
    (length, features), units = normed.shape, down.shape[0]

    def columns(part):
        if part.plane is None:
            first = part.at * part.columns // chunk
            return pl.BlockSpec((features, chunk), lambda j: (0, first + j))
        plane = part.plane
        return pl.BlockSpec((None, features, chunk), lambda j: (plane, 0, j))

    return pl.pallas_call(
        functools.partial(ffn_kernel, chunk=chunk, units=units),
        grid=(units // chunk,),
        in_specs=[
            whole(normed.shape),
            whole(full.shape),
            columns(gate),
            columns(up),
            pl.BlockSpec((chunk, features), lambda j: (j, 0)),
        ],
        out_specs=[pl.BlockSpec((length, chunk), lambda j: (0, j)), whole((length, 2 * units))],
        out_shape=[
            jax.ShapeDtypeStruct((length, units), BF16),
            jax.ShapeDtypeStruct((length, 2 * units), BF16),
        ],
        compiler_params=params(24),
        cost_estimate=COST,
        name="feed_forward",
    )(normed, full, *in_hbm([gate.array, up.array, down]))


def in_hbm(arrays):
    return [pltpu.with_memory_space_constraint(x, pltpu.HBM) for x in arrays]


def tie(x, *others):
    return lax.optimization_barrier((x, others))[0] if others else x


def arrange_kernel(scalars, mine_ref, theirs_ref, *out_refs, outputs):
    top = scalars[1]
    at = 0
    for out_ref, (width, planes) in zip(out_refs, outputs):
        for plane in range(max(planes, 1)):
            mine, theirs = (ref[0, :, at : at + width].astype(out_ref.dtype) for ref in (mine_ref, theirs_ref))
            at += width
            if planes:
                out_ref[plane, top, 0] = mine
                out_ref[plane, 1 - top, 0] = theirs
            else:
                out_ref[0, :, :width] = jnp.where(top == 0, mine, theirs)
                out_ref[0, :, width:] = jnp.where(top == 0, theirs, mine)


def arrange(mine, theirs, index, top, outputs, dtype):
    n, rows, columns = mine.shape
    scalars = jnp.stack([index, top]).astype(jnp.int32)
    specs, shapes = [], []
    for w, planes in outputs:
        if planes:
            specs.append(pl.BlockSpec((planes, 2, 1, rows, w), lambda i, sc: (0, 0, i, 0, 0)))
            shapes.append(jax.ShapeDtypeStruct((planes, 2, n, rows, w), dtype))
        else:
            specs.append(pl.BlockSpec((1, rows, 2 * w), lambda i, sc: (i, 0, 0)))
            shapes.append(jax.ShapeDtypeStruct((n, rows, 2 * w), dtype))
    outs = pl.pallas_call(
        functools.partial(arrange_kernel, outputs=outputs),
        grid_spec=pltpu.PrefetchScalarGridSpec(
            num_scalar_prefetch=1,
            grid=(n,),
            in_specs=[pl.BlockSpec((1, rows, columns), lambda i, sc: (i ^ sc[0], 0, 0))] * 2,
            out_specs=specs,
        ),
        out_shape=shapes,
        compiler_params=params(12),
        cost_estimate=COST,
        name="arrange",
    )(scalars, mine, theirs)
    return [
        x.reshape(x.shape[0], 2 * n * rows, w) if planes else x.reshape(n * rows, 2 * w)
        for x, (w, planes) in zip(outs, outputs)
    ]


class Links:
    def __init__(self, n_dp):
        self.n_dp = n_dp
        self.n_bits = n_dp.bit_length() - 1
        self.here = lax.axis_index("dp")

    def bit(self, k):
        return (self.here >> k) & 1

    def across_tp(self, x):
        return lax.ppermute(x, "tp", [(0, 1), (1, 0)])

    def across(self, x, mask):
        return lax.ppermute(x, "dp", [(i, i ^ mask) for i in range(self.n_dp)])


class Single:
    def __init__(self, move):
        self.move, self.started = move, False

    def send(self, x, *after):
        self.sent = tie(x, *after)
        self.got = [self.move(self.sent)]

    def take(self):
        return self.got[0]


class Fetch:
    def __init__(self, links, shards, bits, outputs):
        self.links, self.bits, self.outputs = links, list(bits), outputs
        self.n, self.index, self.got, self.held = 1 << len(bits), 0, None, None
        for place, k in enumerate(bits):
            self.index = self.index + (links.bit(k) << place)
        self.piece = jnp.concatenate([y for x in shards for y in self.pieces(x)], axis=2)

    def pieces(self, x):
        if isinstance(x, tuple):
            (x,) = x
            rows, columns, half = x.shape[0] * 2 // self.n, x.shape[1] // 2, self.n // 2
            at = (self.index % half * rows, self.index // half * columns)
            return [lax.dynamic_slice(x, at, (rows, columns))[None]]
        x = x.reshape(-1, self.n, x.shape[-2] // self.n, x.shape[-1])
        return list(lax.dynamic_slice_in_dim(x, self.index, 1, axis=1))

    def send(self, *after):
        if self.held is None:
            self.sent = tie(self.piece, *after)
            self.got = [self.links.across_tp(self.sent)]
        else:
            self.sent = tie(self.held, *after)
            self.got = [self.links.across(self.sent, 1 << self.bits[0])]

    def take(self):
        if self.held is None:
            self.held = self.got[0]
            return
        self.bits.pop(0)
        if self.bits:
            self.held = jnp.concatenate([self.held, self.got[0]], axis=0)
            if len(self.bits) == 1:
                self.last = self.bits[0]
        else:
            self.theirs = self.got[0]

    def ended(self):
        return not self.bits

    def finish(self):
        top, below = self.links.bit(self.last), self.index & (self.n // 2 - 1)
        whole_arrays = arrange(self.held, self.theirs, below, top, self.outputs, BF16)
        return [x[0] if x.ndim == 3 and x.shape[0] == 1 else x for x in whole_arrays]


TP = "tp"
HALO, PROJECT, MEMORY, GATE, DOWN, REST, CROSS, SELF = range(8)


class Reduction:
    def __init__(self, links, own, other, order, outputs):
        self.links, self.order, self.outputs = links, list(order), outputs
        self.back = [k for k in reversed(order) if k is not TP][:-1]
        self.n_blocks = links.n_dp
        view = lambda x: x.reshape(self.n_blocks, -1, x.shape[-1])
        self.own, self.other = [([view(x) for x in own], 0)], [([view(x) for x in other], 0)]
        self.at, self.size = 0, self.n_blocks
        self.index = 0
        self.result = self.theirs = None

    def piece(self, addends, at, size):
        total = 0.0
        for arrays, base in addends:
            parts = [lax.dynamic_slice_in_dim(x, at - base, size).astype(F32) for x in arrays]
            total = total + (jnp.concatenate(parts, axis=2) if len(parts) > 1 else parts[0])
        return total.astype(BF16)

    def send(self, *after):
        links = self.links
        if self.result is not None:
            bits = self.back[0] if self.back else (0,)
            masks = self.masks(bits)
            self.sent = tie(self.result, *after)
            self.got = [links.across(self.sent, mask) for mask in masks]
        elif self.order[0] is TP:
            self.sent = tie(self.piece(self.other, self.at, self.size), *after)
            self.got = [links.across_tp(self.sent)]
            self.other = None
        else:
            bits = self.order[0]
            masks = self.masks(bits)
            digit = 0
            for k in bits:
                digit = digit * 2 + links.bit(k)
            part = self.size // (len(masks) + 1)
            self.got, self.sent = [], []
            for i, mask in enumerate(masks):
                at = self.at + (digit ^ (i + 1)) * part
                sent = self.piece(self.own, at, part)
                if self.other is not None:
                    sent = jnp.concatenate([sent, self.piece(self.other, at, part)], axis=0)
                self.sent.append(tie(sent, *after))
                self.got.append(links.across(self.sent[-1], mask))
            self.at, self.size = self.at + digit * part, part
            if bits != (0,):
                self.index = self.index * (len(masks) + 1) + digit
        return self.got

    def masks(self, bits):
        out = []
        for i in range(1, 1 << len(bits)):
            out.append(sum(1 << k for place, k in enumerate(reversed(bits)) if (i >> place) & 1))
        return out

    def take(self):
        if self.result is not None:
            if self.back:
                self.back.pop(0)
                self.result = jnp.concatenate([self.result] + self.got, axis=0)
            else:
                self.theirs = self.got[0]
            return self.result
        self.order.pop(0)
        for got in self.got:
            self.own = self.own + [([got[: self.size]], self.at)]
            if self.other is not None:
                self.other = self.other + [([got[self.size :]], self.at)]
        if not self.order:
            self.result = self.piece(self.own, self.at, self.size)
        return self.got

    def ended(self):
        return self.theirs is not None

    def finish(self):
        return arrange(self.result, self.theirs, self.index, self.links.bit(0), self.outputs, F32)


class Agenda:
    def __init__(self, links):
        self.links, self.chains, self.now, self.strict = links, {}, (), True

    def at(self, x):
        return tie(x, *self.now)

    def after(self, *values):
        self.now = values

    def start(self, name, chain, *args):
        self.chains[name] = chain
        chain.send(*args, *self.now)
        self.now = (self.now, chain.sent)

    def go(self, name):
        chain = self.chains[name]
        if self.strict:
            chain.got = tie(chain.got, *self.now)
        came = chain.got
        chain.take()
        if chain.ended():
            self.now = (came,)
            return chain.finish()
        chain.send(came, *self.now)
        self.now = (came, chain.sent)

    def take(self, name):
        came = self.chains[name].take()
        if self.strict:
            came = tie(came, *self.now)
        self.now = (self.now, came)
        return came


def column_halves(x):
    half = x.shape[1] // 2
    return jnp.concatenate([x[:, :half], x[:, half:]], axis=0)


def beside(x):
    return jnp.concatenate(list(x), axis=1)


def shards(
    n_dp,
    decoder_rows,
    memory_rows,
    output_grad,
    token_segments,
    memory_segments,
    valid_mask,
    norm_gains,
    self_project,
    self_output,
    cross_query,
    cross_memory,
    cross_output,
    gate_up,
    down_weight,
):
    links = Links(n_dp)
    side = lax.axis_index("tp")
    decoder, memory, out_grad = decoder_rows[0], memory_rows[0], output_grad[0]
    valid = valid_mask[0]
    own_len, features = decoder.shape
    mem_len, columns = memory.shape[0], cross_query.shape[1]
    halo = token_segments.shape[1] // 4
    both = (0, 1)

    d, units = features, down_weight.shape[0]
    half_len = mem_len // 2
    agenda = Agenda(links)
    at, after, start, go, take = agenda.at, agenda.after, agenda.start, agenda.go, agenda.take
    v = types.SimpleNamespace()
    v.kv_own_of = [None, None]
    v.self_of = [None, None]
    v.cross_of = [None, None]
    v.query_grad_of = [None, None]
    v.kv_grad_of = [None, None]
    v.memory_dw_of = [None, None]
    v.proj_grad_of = [None, None]
    v.memory_came, v.memory_got = [], []
    bit0, bit1, rest = (0,), (1,), [(k,) for k in range(2, links.n_bits)]
    tp_first, tp_second, tp_third = (
        [bit0, TP, bit1] + rest,
        [bit0, bit1, TP] + rest,
        [bit0, bit1] + rest[:1] + [TP] + rest[1:],
    )
    resid0 = decoder.astype(F32)
    valid_rows = valid.astype(F32)[:, None]
    grad_m = out_grad.astype(F32) * valid_rows
    full_m = grad_m.astype(BF16)

    def sums(name, order, outputs, parts):
        after(parts)
        start(name, Reduction(links, *parts, order, outputs))

    def send_halo():
        start(HALO, Single(lambda x: lax.ppermute(x, "tp", [(0, 1)])), decoder[-halo:])

    def send_project():
        start(PROJECT, Fetch(links, [self_project], BITS, ((columns, 3),)))

    def send_memory(i):
        start(MEMORY, Single(links.across_tp), memory)

    def send_ffn():
        def mine(x):
            blocks = x.reshape(-1, links.n_dp, x.shape[-2] // links.n_dp, x.shape[-1])
            return jnp.concatenate(list(lax.dynamic_index_in_dim(blocks, links.here, 1, False)), axis=1)

        start(GATE, Single(links.across_tp), mine(gate_up))
        start(DOWN, Single(links.across_tp), mine(down_weight))

    def gather_ffn():
        gate_other = lax.all_gather(take(GATE), "dp", axis=0, tiled=True)
        v.gate_w = [Part(gate_up, plane=c) for c in both], [Part(gate_other, units, c) for c in both]
        v.down_w = (down_weight, lax.all_gather(take(DOWN), "dp", axis=0, tiled=True))

    def send_rest():
        start(
            REST,
            Fetch(
                links,
                [cross_memory, cross_query, (self_output,), (cross_output,)],
                BITS,
                ((columns, 2), (columns, 1), (columns, 0), (columns, 0)),
            ),
        )

    def plan():
        v.intervals = make_plans(side, token_segments, memory_segments, own_len, mem_len, halo)
        after(v.intervals)

    def norm_a():
        v.rows_a = jnp.concatenate([take(HALO), decoder], axis=0).astype(F32)
        v.normed_a = normalize(v.rows_a, norm_gains[0]).astype(BF16)

    def self_forward(h):
        if h:
            v.project = (self_project, out[PROJECT][0])
        weights = v.project[1] if h else self_project
        rows = at(v.normed_a)
        proj = [nn(rows, weights[c]).astype(BF16) for c in range(3)]
        att, totals = attend_forward(v.intervals, 0, columns, (proj[0], 0), ((proj[1], proj[2]),), halo)
        v.self_of[h] = proj, att, totals
        after(att)

    def keys_of(rows, h):
        return tuple(nn(rows, v.memory_w[h][c]).astype(BF16) for c in both)

    def keys_own(h):
        v.kv_own_of[h] = keys_of(at(memory), h)
        after(v.kv_own_of[h])

    def weights_rest():
        other_memory, other_query, other_out_a, other_out_c = out[REST]
        v.memory_w = (cross_memory, other_memory)
        v.out_a, v.out_c, v.query_w = (
            (self_output, other_out_a),
            (cross_output, other_out_c),
            (cross_query, other_query),
        )

    def queries():
        weights_rest()
        v.proj_a, v.att_a, v.totals_a = zip(*v.self_of)
        att = at(v.att_a)
        v.branch_a = nn(att[0], v.out_a[0]) + nn(att[1], v.out_a[1])
        v.resid1 = resid0 + v.branch_a
        v.normed_c = normalize(v.resid1, norm_gains[1]).astype(BF16)
        v.query_c = [nn(v.normed_c, v.query_w[h]).astype(BF16) for h in both]
        after(v.query_c)

    def take_memory():
        v.memory_came.append(take(MEMORY))

    def cross_forward(h):
        if not h:
            (v.memory_other,) = v.memory_came
        keys = (v.kv_own_of[h], keys_of(at(v.memory_other), h))
        att, totals = attend_forward(v.intervals, 1, columns, (v.query_c[h], 0), keys, 0)
        v.cross_of[h] = keys, att, totals
        after(att)

    def ffn():
        v.keys_c, v.att_c, v.totals_c = zip(*v.cross_of)
        att = at(v.att_c)
        v.branch_c = nn(att[0], v.out_c[0]) + nn(att[1], v.out_c[1])
        v.resid2 = v.resid1 + v.branch_c
        v.normed_m = normalize(v.resid2, norm_gains[2]).astype(BF16)
        v.hidden, v.gate_grads = zip(
            *[feed_forward(v.normed_m, full_m, *v.gate_w[h], v.down_w[h]) for h in both]
        )
        after(v.gate_grads)

    def gate_dw():
        agenda.strict = False
        parts = weight_grads([v.normed_m], at(list(v.gate_grads)), 512)
        sums(GATE, ORDERS[GATE], ((units, 2),), [[x] for x in parts])

    def down_dw():
        v.down_dw = weight_grads([at(full_m)], list(v.hidden), 512)
        after(v.down_dw)

    def norm_m_grad():
        v.gate_late = at(v.gate_grads)

    def norm_m_back():
        pairs = [(Part(v.gate_late[h], units, c), v.gate_w[h][c]) for h in both for c in both]
        v.grad_c, v.full_c, gain, *v.att_c_grad = norm_back(pairs, v.resid2, norm_gains[2], full_m, v.out_c)
        v.gain_m = gain[0]
        after(v.att_c_grad)

    def outs_dw():
        grad = at(v.full_c)
        out_dw = [weight_grads([v.att_c[h]], [grad], grad.shape[1])[0] for h in both]
        parts = [[v.down_dw[h], column_halves(out_dw[h])] for h in both]
        sums(DOWN, ORDERS[DOWN], ((units, 1), (columns, 0)), parts)

    def cross_backward(h):
        grad = at(v.att_c_grad[h])
        query = (v.query_c[h], 0)
        v.query_grad_of[h], v.kv_grad_of[h] = attend_backward(
            v.intervals, 1, columns, v.totals_c[h], query, v.att_c[h], grad, v.keys_c[h], 0, False
        )
        after(v.query_grad_of[h])

    def norm_c_back():
        grads = at(v.query_grad_of)
        pairs = [(Part(grads[h]), Part(v.query_w[h])) for h in both]
        v.grad_a, v.full_a, gain, *v.att_a_grad = norm_back(pairs, v.resid1, norm_gains[1], v.grad_c, v.out_a)
        v.gain_c = gain[0]
        after(v.att_a_grad)

    def memory_back(own):
        kv = at(v.kv_grad_of)
        row = 0 if own else mem_len
        pairs = [(Part(kv[h], columns, c, row=row), Part(v.memory_w[h], plane=c)) for h in both for c in both]
        if own:
            v.memory_grad = product_back(pairs, mem_len, F32, v.memory_got[0])
            after(v.memory_grad)
        else:
            v.memory_partial = product_back(pairs, mem_len, BF16)
            after(v.memory_partial)

    def send_partial(i):
        start(MEMORY, Single(links.across_tp), v.memory_partial)

    def take_partial():
        v.memory_got.append(take(MEMORY))

    def memory_dw(h):
        if h:
            v.memory_dw_of = weight_grads([memory, v.memory_other], at(v.kv_grad_of), 384)
            after(v.memory_dw_of)

    def cross_dw():
        query_dw = weight_grads([at(v.normed_c)], v.query_grad_of, columns)
        out_dw = [weight_grads([v.att_a[h]], [at(v.full_a)], v.full_a.shape[1])[0] for h in both]
        parts = [[v.memory_dw_of[h], query_dw[h], column_halves(out_dw[h])] for h in both]
        sums(CROSS, ORDERS[CROSS], ((columns, 2), (columns, 1), (columns, 0)), parts)

    def self_backward(h):
        grad = at(v.att_a_grad[h])
        proj, *keys = v.proj_a[h]
        v.proj_grad_of[h] = attend_backward(
            v.intervals, 0, columns, v.totals_a[h], (proj, 0), v.att_a[h], grad, (keys,), halo, True
        )[0]
        after(v.proj_grad_of[h])

    def norm_a_grad():
        grads = at(v.proj_grad_of)
        pairs = [(Part(grads[h], columns, c), Part(v.project[h], plane=c)) for h in both for c in range(3)]
        v.normed_a_grad = total = product_back(pairs, own_len + halo, F32)
        after(total)
        start(HALO, Single(lambda x: lax.ppermute(x, "tp", [(1, 0)])), total[:halo].astype(BF16))
        v.branch_m = nn(v.hidden[0], v.down_w[0]) + nn(v.hidden[1], v.down_w[1])
        v.result = v.resid2 + v.branch_m
        gain_a = jnp.sum(total * v.rows_a * inverse_rms(v.rows_a), axis=0)
        rows = [jnp.sum(x * x * valid_rows, axis=0) for x in (v.result, v.branch_a, v.branch_c, v.branch_m)]
        rows += [jnp.sum(jnp.broadcast_to(valid_rows, resid0.shape), axis=0), v.gain_m, v.gain_c, gain_a]
        v.stats = jnp.pad(jnp.stack(rows), ((0, 2 * HD - len(rows)), (0, 0))).T.astype(BF16)

    def self_dw():
        parts = [[x, v.stats] for x in weight_grads([v.normed_a], at(v.proj_grad_of), 384)]
        sums(SELF, ORDERS[SELF], ((columns, 3), (2 * HD, 1)), parts)

    def norm_a_back():
        came = take(HALO).astype(F32)
        own = at(v.normed_a_grad[halo:])
        own = jnp.concatenate([own[:-halo], own[-halo:] + came], axis=0)
        resid0_grad, _ = normalize_back(resid0, norm_gains[0], own)
        v.decoder_grad = v.grad_a + resid0_grad
        after(v.decoder_grad)

    BITS = (2, 1, 0)
    ORDERS = {GATE: tp_first, DOWN: tp_second, CROSS: tp_second, SELF: tp_first}
    v.memory_w = (None, None)
    out = {}

    def keys_first():
        v.memory_w = (cross_memory, None)
        keys_own(0)

    def advance(name):
        came = go(name)
        if came is not None:
            out[name] = came
            after(came)

    def for_each(block):
        return [functools.partial(block, h) for h in both]

    mem0, mem1 = for_each(send_memory)
    self0, self1 = for_each(self_forward)
    keys0, keys1 = keys_first, functools.partial(keys_own, 1)
    cross0, cross1 = for_each(cross_forward)
    cross_b0, cross_b1 = for_each(cross_backward)
    part0, part1 = for_each(send_partial)
    mem_dw0, mem_dw1 = for_each(memory_dw)
    self_b0, self_b1 = for_each(self_backward)
    mem_b0, mem_b1 = for_each(memory_back)
    P_, R, A, B, E, D = [functools.partial(advance, name) for name in (PROJECT, REST, GATE, DOWN, CROSS, SELF)]
    agenda_steps = (
        send_halo, send_project, send_ffn, plan, norm_a, P_, gather_ffn, send_rest, self0, P_, mem0, R, keys0, P_, R,
        P_, self1, take_memory, R, R, queries, keys1, cross0, cross1, ffn, gate_dw, down_dw, norm_m_grad, A,
        norm_m_back, outs_dw, cross_b0, B, cross_b1, A, norm_c_back, mem_b0, part0, B, mem_dw0, mem_dw1, cross_dw, A,
        B, self_b1, E, A, B, self_b0, A, B, norm_a_grad, self_dw, E, A, B, take_partial, D, mem_b1, A, B, norm_a_back,
        E, D, A, B, E, D, A, E, D, B, E, D, E, D, E, D, E, D, D,
    )
    for step in agenda_steps:
        step()
    for name in (GATE, DOWN, CROSS, SELF):
        while name not in out:
            advance(name)

    stats = out[SELF][1][0, :, :8].T
    gains_grad = jnp.stack([stats[7], stats[6], stats[5]])
    root_squares = jnp.sqrt(jnp.sum(stats[:4], axis=1) / jnp.sum(stats[4]))
    return (
        v.result.astype(BF16)[None],
        v.decoder_grad[None],
        v.memory_grad[None],
        root_squares,
        gains_grad,
        out[SELF][0],
        out[CROSS][2],
        out[CROSS][1][0],
        out[CROSS][0],
        out[DOWN][1],
        out[GATE][0],
        out[DOWN][0][0].T,
    )


def solution(mesh):
    assert mesh.shape["tp"] == 2
    return jax.shard_map(
        functools.partial(shards, mesh.shape["dp"]),
        mesh=mesh,
        in_specs=(
            P("dp", "tp", None),
            P("dp", "tp", None),
            P("dp", "tp", None),
            P("dp", None),
            P("dp", None),
            P("dp", "tp"),
            P(),
            P(None, None, "tp"),
            P("tp", None),
            P(None, "tp"),
            P(None, None, "tp"),
            P("tp", None),
            P(None, None, "tp"),
            P("tp", None),
        ),
        out_specs=(
            P("dp", "tp", None),
            P("dp", "tp", None),
            P("dp", "tp", None),
            P(),
            P(),
            P(None, None, "tp"),
            P("tp", None),
            P(None, "tp"),
            P(None, None, "tp"),
            P("tp", None),
            P(None, None, "tp"),
            P("tp", None),
        ),
        check_vma=False,
    )
```

time: 1110 us -> 517 us (0.47)
  matrix products: 275 us -> 23.7 us
  waiting for transfers between devices: 372 us -> 152 us
  other arithmetic: 210 us -> 32.2 us
  Pallas kernels: 0 us -> 149 us
  blocking collectives: 95.7 us -> 0 us
  starting transfers between devices: 10.9 us -> 58.4 us
  local copies, waits for them, and re-layouts: 118 us -> 80.3 us
    dot_general x46 -> x22, matrix products: 275 us -> 23.7 us  [contract(): lax.dot_general(a, b, (((i,), (j,)), ((), ())), preferred_element_type=F32)]
    ppermute x0 -> x50, waiting for transfers between devices: none -> 152 us  [the longest x38 119 us: across(): return lax.ppermute(x, 'dp', [(i, i ^ mask) for i in range(self.n_dp)])]
    psum x1 -> x0, waiting for transfers between devices: 151 us -> none  [shards(): lax.psum((self_project_grad, self_output_grad, cross_query_grad, cross_me...]
    pallas_call x0 -> x31, Pallas kernels: none -> 149 us  [the longest x4 35 us: attend_backward(): pl.pallas_call(functools.partial(backward_kernel, first_part=first_part,...]
    all_gather x11 -> x2, waiting for transfers between devices: 132 us -> 0.01 us  [the longest x1 0.01 us: gather_ffn(): lax.all_gather(take(DOWN), 'dp', axis=0, tiled=True)]
    unnamed x8 -> x0, other arithmetic: 89.1 us -> none
    reduce_scatter x3 -> x0, waiting for transfers between devices: 76.9 us -> none  [the longest x2 46.3 us: collect_grad(): lax.psum_scatter(partial_value, 'tp', scatter_dimension=1, tiled=True)]
    convert_element_type x11 -> x26, other arithmetic: 71.1 us -> 8.11 us  [the longest x22 6.67 us: piece(): return total.astype(BF16)]
  transfers between devices with their start and end apart: 17 -> 52, of which waited for: 11 -> 24; matrix products, arithmetic and copies ran while one was open for 49% -> 17% of each run, Pallas kernels for 0% -> 19%
where the time goes in v2:
time: 517 us; the launch traced here: 513 us
  waiting for transfers between devices  152 us (29%)
  Pallas kernels  149 us (29%)
  local copies, waits for them, and re-layouts  80.3 us (16%)
  starting transfers between devices  58.4 us (11%)
  other arithmetic  32.2 us (6%)
  matrix products  23.7 us (5%)
  between operations  17.4 us (3%)
    ppermute x38, waiting for transfers between devices, across(): return lax.ppermute(x, 'dp', [(i, i ^ mask) for i in range(self.n_dp)])  119 us
    unnamed x345, local copies, waits for them, and re-layouts  45.7 us
    pallas_call x4, Pallas kernels, attend_backward(): pl.pallas_call(functools.partial(backward_kernel, first_part=first_part,...  35 us
    ppermute x38, starting transfers between devices, across(): return lax.ppermute(x, 'dp', [(i, i ^ mask) for i in range(self.n_dp)])  32.7 us
    ppermute x10, waiting for transfers between devices, across_tp(): return lax.ppermute(x, 'tp', [(0, 1), (1, 0)])  32.3 us
    pallas_call x9, Pallas kernels, weight_grads(): pl.pallas_call(functools.partial(weight_kernel, n=len(rows), m=len(grads)...  24.7 us
    dot_general x22, matrix products, contract(): lax.dot_general(a, b, (((i,), (j,)), ((), ())), preferred_element_type=F32)  23.7 us
    pallas_call x6, Pallas kernels, arrange(): pl.pallas_call(functools.partial(arrange_kernel, outputs=outputs), grid_s...  22.6 us
  transfers between devices with their start and end apart: 52, of which 24 were waited for; matrix products, arithmetic and copies ran while one was open for 17% of the time, Pallas kernels for 19%

profile of v2, /device:TPU:0, one launch (start us, length us, event | category | flops | bytes accessed | tf_op | source)
XLA Modules:
  0.0 512.9 jit_solution(15298645381131761806)
XLA Ops:
  8.3 5.0 collective-permute-start
  15.4 2.1 collective-permute-start.2
  29.0 2.6 collective-permute-done.2
  33.1 2.3 convolution_convert_fusion.13.q_ref
  38.6 2.5 collective-permute-start.6
  41.5 3.8 attend_forward.4
  48.1 2.1 collective-permute-start.5
  53.8 6.4 %collective-permute-done.5 = bf16[2,96,1152]{2,1,0:T(8,128)(2,1)S(1)} collective-permute-done((bf16[2,96,1152]{2,1,0:T(8,128)(2,1)S(1)}, bf16[2,96,1152]{2,1,0:T(8,128)(2,1)S(1)}, u32[]{:S(2)}, u32[]{:S(2)}) %collective-permute-start.5) | collective-permute-done | bytes 442400 | tf_op jit(solution)/shard_map/ppermute | solution.py:601
  64.1 12.1 %collective-permute-done.8 = bf16[1,96,1920]{2,1,0:T(8,128)(2,1)S(1)} collective-permute-done((bf16[1,96,1920]{2,1,0:T(8,128)(2,1)}, bf16[1,96,1920]{2,1,0:T(8,128)(2,1)S(1)}, u32[]{:S(2)}, u32[]{:S(2)}) %collective-permute-start.8) | collective-permute-done | bytes 368672 | tf_op jit(solution)/shard_map/ppermute | solution.py:601
  79.6 3.1 arrange.6
  86.4 3.8 attend_forward.5
  90.9 7.2 %collective-permute-done.10.refs_1_ = bf16[1024,768]{1,0:T(8,128)(2,1)S(1)} collective-permute-done((bf16[1024,768]{1,0:T(8,128)(2,1)}, bf16[1024,768]{1,0:T(8,128)(2,1)S(1)}, u32[]{:S(2)}, u32[]{:S(2)}) %collective-permute-start.10) | collective-permute-done | bytes 1572896 | tf_op jit(solution)/shard_map/ppermute | solution.py:598
  100.8 3.0 collective-permute-done.11.theirs_ref
  103.8 3.3 arrange.7
  108.9 2.4 multiply_reduce_fusion.5
  120.6 7.6 %attend_forward.6 = (bf16[512,384]{1,0:T(8,128)(2,1)S(1)}, f32[4,3,256]{2,1,0:T(4,128)S(1)}) custom-call(s32[6,4,128]{2,1,0:T(4,128)S(1)} %copy-done.91, bf16[512,384]{1,0:T(8,128)(2,1)S(1)} %convolution_convert_fusion.15.q_ref, bf16[1024,384]{1,0:T(8,128)(2,1)S(1)} %convolution_convert_fusion.7.refs_0_, ...), custom_call_target="tpu_custom_call" | custom-call | flops 1048576 | bytes 1048576 | tf_op jit(solution)/shard_map/attend_forward/pallas_call | solution.py:258
  130.2 7.2 %attend_forward.7 = (bf16[512,384]{1,0:T(8,128)(2,1)S(1)}, f32[4,3,256]{2,1,0:T(4,128)S(1)}) custom-call(s32[6,4,128]{2,1,0:T(4,128)S(1)} %copy-done.91, bf16[512,384]{1,0:T(8,128)(2,1)S(1)} %convolution_convert_fusion.14.q_ref, bf16[1024,384]{1,0:T(8,128)(2,1)S(1)} %convolution_convert_fusion.5.refs_0_, ...), custom_call_target="tpu_custom_call" | custom-call | flops 1048576 | bytes 1048576 | tf_op jit(solution)/shard_map/attend_forward/pallas_call | solution.py:258
  140.8 5.4 %feed_forward.2 = (bf16[512,1024]{1,0:T(8,128)(2,1)S(1)}, bf16[512,2048]{1,0:T(8,128)(2,1)S(1)}) custom-call(bf16[512,768]{1,0:T(8,128)(2,1)S(1)} %get-tuple-element.372.normed_ref.refs_0_, bf16[512,768]{1,0:T(8,128)(2,1)S(1)} %get-tuple-element.206.full_ref.refs_0_.refs_10_, bf16[2,768,1024]{2,1,0:T(8,128)(2,1)} %refs_5_.3, bf16[2,768,1024]{2,1,0:T(8,128)(2,1)} %refs_5_.3, ...), custom_call_target="tpu_custom_call" | custom-call | flops 1048576 | bytes 1048576 | tf_op jit(solution)/shard_map/feed_forward/pallas_call | solution.py:514
  148.5 5.3 %feed_forward.3 = (bf16[512,1024]{1,0:T(8,128)(2,1)S(1)}, bf16[512,2048]{1,0:T(8,128)(2,1)S(1)}) custom-call(bf16[512,768]{1,0:T(8,128)(2,1)S(1)} %get-tuple-element.372.normed_ref.refs_0_, bf16[512,768]{1,0:T(8,128)(2,1)S(1)} %get-tuple-element.206.full_ref.refs_0_.refs_10_, bf16[768,2048]{1,0:T(8,128)(2,1)} %all-gather.3.cloned.1.call-done.gate_ref.up_ref.refs_6_.refs_7_, ...), custom_call_target="tpu_custom_call" | custom-call | flops 1048576 | bytes 1048576 | tf_op jit(solution)/shard_map/feed_forward/pallas_call | solution.py:514
  153.8 5.0 weight_grads.9
  161.8 1.9 pad_maximum_fusion
  163.7 2.6 weight_grads.10
  166.4 7.7 %norm_back.2 = (f32[512,768]{1,0:T(8,128)S(1)}, bf16[512,768]{1,0:T(8,128)(2,1)S(1)}, f32[1,768]{1,0:T(1,128)S(1)}, bf16[512,384]{1,0:T(8,128)(2,1)S(1)}, bf16[512,384]{1,0:T(8,128)(2,1)S(1)}) custom-call(bf16[512,2048]{1,0:T(8,128)(2,1)S(1)} %copy-done.12, bf16[512,2048]{1,0:T(8,128)(2,1)S(1)} %copy-done.12, ...), custom_call_target="tpu_custom_call" | custom-call | flops 1048576 | bytes 1048576 | tf_op jit(solution)/shard_map/norm_back/pallas_call | solution.py:438
  188.7 11.3 %attend_backward.4 = (bf16[512,384]{1,0:T(8,128)(2,1)S(1)}, bf16[2048,768]{1,0:T(8,128)(2,1)S(1)}) custom-call(s32[6,4,128]{2,1,0:T(4,128)S(1)} %copy-done.91, f32[4,3,256]{2,1,0:T(4,128)S(1)} %copy-done.107, bf16[512,384]{1,0:T(8,128)(2,1)S(1)} %copy-done.87, bf16[512,384]{1,0:T(8,128)(2,1)S(1)} %copy-done.21, bf16[512,384]{1,0:T(8,128)(2,1)S(1)} %copy-done.99, ...), custom_call_target="tpu_custom_call" | custom-call | flops 1048576 | bytes 1048576 | tf_op jit(solution)/shard_map/attend_backward/pallas_call | solution.py:298
  205.4 2.0 add_convert_fusion
  207.4 8.2 %collective-permute-start.14 = (bf16[8,48,2048]{2,1,0:T(8,128)(2,1)S(1)}, bf16[8,48,2048]{2,1,0:T(8,128)(2,1)S(1)}, u32[]{:S(2)}, u32[]{:S(2)}) collective-permute-start(bf16[8,48,2048]{2,1,0:T(8,128)(2,1)S(1)} %add_convert_fusion), channel_id=1, source_target_pairs={{0,1},{1,0},{2,3},{3,2},{4,5},{5,4},{6,7},{7,6},{8,9},{9,8},{10,11... | collective-permute-start | bytes 4718600 | tf_op jit(solution)/shard_map/ppermute | solution.py:598
  219.4 2.4 multiply_reduce_fusion
  221.9 11.3 %attend_backward.5 = (bf16[512,384]{1,0:T(8,128)(2,1)S(1)}, bf16[2048,768]{1,0:T(8,128)(2,1)S(1)}) custom-call(s32[6,4,128]{2,1,0:T(4,128)S(1)} %copy-done.91, f32[4,3,256]{2,1,0:T(4,128)S(1)} %copy-done.105, bf16[512,384]{1,0:T(8,128)(2,1)S(1)} %copy-done.85, bf16[512,384]{1,0:T(8,128)(2,1)S(1)} %copy-done.24, bf16[512,384]{1,0:T(8,128)(2,1)S(1)} %copy-done.97, ...), custom_call_target="tpu_custom_call" | custom-call | flops 1048576 | bytes 1048576 | tf_op jit(solution)/shard_map/attend_backward/pallas_call | solution.py:298
  233.2 2.7 slice.205
  236.2 12.9 %collective-permute-done.14 = bf16[8,48,2048]{2,1,0:T(8,128)(2,1)S(1)} collective-permute-done((bf16[8,48,2048]{2,1,0:T(8,128)(2,1)S(1)}, bf16[8,48,2048]{2,1,0:T(8,128)(2,1)S(1)}, u32[]{:S(2)}, u32[]{:S(2)}) %collective-permute-start.14) | collective-permute-done | bytes 1572896 | tf_op jit(solution)/shard_map/ppermute | solution.py:598
  249.5 3.9 norm_back.3
  254.5 6.8 %back.3 = bf16[1024,768]{1,0:T(8,128)(2,1)} custom-call(bf16[2048,768]{1,0:T(8,128)(2,1)S(1)} %get-tuple-element.271.refs_0_.refs_1_.refs_2_, bf16[2048,768]{1,0:T(8,128)(2,1)S(1)} %get-tuple-element.271.refs_0_.refs_1_.refs_2_, bf16[2048,768]{1,0:T(8,128)(2,1)S(1)} %get-tuple-element.272.refs_2_.refs_3_, ...), custom_call_target="tpu_custom_call" | custom-call | flops 1048576 | bytes 1048576 | tf_op jit(solution)/shard_map/back/pallas_call | solution.py:421
  261.4 8.6 %weight_grads.13 = (bf16[768,768]{1,0:T(8,128)(2,1)S(1)}, bf16[768,768]{1,0:T(8,128)(2,1)S(1)}) custom-call(bf16[1024,768]{1,0:T(8,128)(2,1)S(1)} %bitcast.178, bf16[1024,768]{1,0:T(8,128)(2,1)S(1)} %copy-done.75, bf16[2048,768]{1,0:T(8,128)(2,1)S(1)} %get-tuple-element.271.refs_0_.refs_1_.refs_2_, bf16[2048,768]{1,0:T(8,128)(2,1)S(1)} %get-tuple-element.272.refs_2_.refs_3_), custom_call_target="tpu_custom_call" | custom-call | flops 1048576 | bytes 1048576 | tf_op jit(solution)/shard_map/weight_grads/pallas_call | solution.py:478
  276.1 1.8 collective-permute-start.16
  282.7 8.5 %collective-permute-done.16 = bf16[4,48,1408]{2,1,0:T(8,128)(2,1)S(1)} collective-permute-done((bf16[4,48,1408]{2,1,0:T(8,128)(2,1)S(1)}, bf16[4,48,1408]{2,1,0:T(8,128)(2,1)S(1)}, u32[]{:S(2)}, u32[]{:S(2)}) %collective-permute-start.16) | collective-permute-done | bytes 540704 | tf_op jit(solution)/shard_map/ppermute | solution.py:598
  291.4 6.2 %collective-permute-done.17 = bf16[4,48,2048]{2,1,0:T(8,128)(2,1)S(1)} collective-permute-done((bf16[4,48,2048]{2,1,0:T(8,128)(2,1)S(1)}, bf16[4,48,2048]{2,1,0:T(8,128)(2,1)S(1)}, u32[]{:S(2)}, u32[]{:S(2)}) %collective-permute-start.17) | collective-permute-done | bytes 786464 | tf_op jit(solution)/shard_map/ppermute | solution.py:601
  298.5 2.0 collective-permute-start.19
  301.9 6.1 %attend_backward.6.refs_3_.refs_4_.refs_5_.refs_2_ = bf16[768,1152]{1,0:T(8,128)(2,1)S(1)} custom-call(s32[6,4,128]{2,1,0:T(4,128)S(1)} %copy-done.91, f32[4,3,256]{2,1,0:T(4,128)S(1)} %copy-done.103, bf16[768,384]{1,0:T(8,128)(2,1)S(1)} %copy-done.59, bf16[512,384]{1,0:T(8,128)(2,1)S(1)} %copy-done.18, bf16[512,384]{1,0:T(8,128)(2,1)S(1)} %get-tuple-element.250.grad_ref, ...), custom_call_target="tpu_custom_call" | custom-call | flops 1048576 | bytes 1048576 | tf_op jit(solution)/shard_map/attend_backward/pallas_call | solution.py:298
  308.1 6.1 %collective-permute-done.19 = bf16[2,48,2048]{2,1,0:T(8,128)(2,1)S(1)} collective-permute-done((bf16[2,48,2048]{2,1,0:T(8,128)(2,1)S(1)}, bf16[2,48,2048]{2,1,0:T(8,128)(2,1)S(1)}, u32[]{:S(2)}, u32[]{:S(2)}) %collective-permute-start.19) | collective-permute-done | bytes 393248 | tf_op jit(solution)/shard_map/ppermute | solution.py:601
  317.1 2.4 collective-permute-start.21
  323.7 6.4 %attend_backward.7.refs_0_.refs_1_.refs_2_ = bf16[768,1152]{1,0:T(8,128)(2,1)S(1)} custom-call(s32[6,4,128]{2,1,0:T(4,128)S(1)} %copy-done.91, f32[4,3,256]{2,1,0:T(4,128)S(1)} %copy-done.101, bf16[768,384]{1,0:T(8,128)(2,1)S(1)} %copy-done.53, bf16[512,384]{1,0:T(8,128)(2,1)S(1)} %get-tuple-element.187.refs_0_.out_ref, ...), custom_call_target="tpu_custom_call" | custom-call | flops 1048576 | bytes 1048576 | tf_op jit(solution)/shard_map/attend_backward/pallas_call | solution.py:298
  330.2 3.4 collective-permute-done.22
  333.8 2.9 collective-permute-start.23
  336.7 6.5 %back.4 = f32[768,768]{1,0:T(8,128)S(1)} custom-call(bf16[768,1152]{1,0:T(8,128)(2,1)S(1)} %attend_backward.7.refs_0_.refs_1_.refs_2_, bf16[768,1152]{1,0:T(8,128)(2,1)S(1)} %attend_backward.7.refs_0_.refs_1_.refs_2_, bf16[768,1152]{1,0:T(8,128)(2,1)S(1)} %attend_backward.7.refs_0_.refs_1_.refs_2_, ...), custom_call_target="tpu_custom_call" | custom-call | flops 1048576 | bytes 1048576 | tf_op jit(solution)/shard_map/back/pallas_call | solution.py:421
  345.4 5.3 %weight_grads.17 = (bf16[768,1152]{1,0:T(8,128)(2,1)S(1)}, bf16[768,1152]{1,0:T(8,128)(2,1)S(1)}) custom-call(bf16[768,768]{1,0:T(8,128)(2,1)S(1)} %copy-done.14, bf16[768,1152]{1,0:T(8,128)(2,1)S(1)} %attend_backward.7.refs_0_.refs_1_.refs_2_, bf16[768,1152]{1,0:T(8,128)(2,1)S(1)} %attend_backward.6.refs_3_.refs_4_.refs_5_.refs_2_), custom_call_target="tpu_custom_call" | custom-call | flops 1048576 | bytes 1048576 | tf_op jit(solution)/shard_map/weight_grads/pallas_call | solution.py:478
  363.4 1.9 collective-permute-start.26
  367.4 12.8 %collective-permute-done.26 = bf16[2,48,1408]{2,1,0:T(8,128)(2,1)S(1)} collective-permute-done((bf16[2,48,1408]{2,1,0:T(8,128)(2,1)S(1)}, bf16[2,48,1408]{2,1,0:T(8,128)(2,1)S(1)}, u32[]{:S(2)}, u32[]{:S(2)}) %collective-permute-start.26) | collective-permute-done | bytes 270368 | tf_op jit(solution)/shard_map/ppermute | solution.py:601
  384.1 2.7 collective-permute-start.31
  386.9 7.4 %back.5 = f32[1024,768]{1,0:T(8,128)} custom-call(bf16[2048,768]{1,0:T(8,128)(2,1)S(1)} %get-tuple-element.271.refs_0_.refs_1_.refs_2_, bf16[2048,768]{1,0:T(8,128)(2,1)S(1)} %get-tuple-element.271.refs_0_.refs_1_.refs_2_, bf16[2048,768]{1,0:T(8,128)(2,1)S(1)} %copy-done.1, bf16[2048,768]{1,0:T(8,128)(2,1)S(1)} %copy-done.1, bf16[2,768,384]{2,1,0:T(8,128)(2,1)} %refs_5_.5, ...), custom_call_target="tpu_custom_call" | custom-call | flops 1048576 | bytes 1048576 | tf_op jit(solution)/shard_map/back/pallas_call | solution.py:421
  399.5 15.3 %collective-permute-done.36 = bf16[4,48,2048]{2,1,0:T(8,128)(2,1)S(1)} collective-permute-done((bf16[4,48,2048]{2,1,0:T(8,128)(2,1)S(1)}, bf16[4,48,2048]{2,1,0:T(8,128)(2,1)S(1)}, u32[]{:S(2)}, u32[]{:S(2)}) %collective-permute-start.36) | collective-permute-done | bytes 786464 | tf_op jit(solution)/shard_map/ppermute | solution.py:601
  418.3 8.1 %collective-permute-done.35 = bf16[4,48,1408]{2,1,0:T(8,128)(2,1)S(1)} collective-permute-done((bf16[4,48,1408]{2,1,0:T(8,128)(2,1)S(1)}, bf16[4,48,1408]{2,1,0:T(8,128)(2,1)S(1)}, u32[]{:S(2)}, u32[]{:S(2)}) %collective-permute-start.35) | collective-permute-done | bytes 540704 | tf_op jit(solution)/shard_map/ppermute | solution.py:601
  429.0 5.6 %collective-permute-done.33 = bf16[4,48,1280]{2,1,0:T(8,128)(2,1)S(1)} collective-permute-done((bf16[4,48,1280]{2,1,0:T(8,128)(2,1)S(1)}, bf16[4,48,1280]{2,1,0:T(8,128)(2,1)S(1)}, u32[]{:S(2)}, u32[]{:S(2)}) %collective-permute-start.33) | collective-permute-done | bytes 491552 | tf_op jit(solution)/shard_map/ppermute | solution.py:601
  435.4 2.6 collective-permute-done.38
  438.1 4.6 arrange.8
  443.2 3.5 arrange.9
  448.4 2.5 collective-permute-start.40
  452.4 5.1 collective-permute-done.40
  457.6 4.8 collective-permute-done.44
  463.4 7.3 %collective-permute-done.43 = bf16[1,48,1280]{2,1,0:T(8,128)(2,1)S(1)} collective-permute-done((bf16[1,48,1280]{2,1,0:T(8,128)(2,1)S(1)}, bf16[1,48,1280]{2,1,0:T(8,128)(2,1)S(1)}, u32[]{:S(2)}, u32[]{:S(2)}) %collective-permute-start.43) | collective-permute-done | bytes 122912 | tf_op jit(solution)/shard_map/ppermute | solution.py:601
  470.8 6.4 %collective-permute-done.46 = bf16[4,48,1536]{2,1,0:T(8,128)(2,1)S(1)} collective-permute-done((bf16[4,48,1536]{2,1,0:T(8,128)(2,1)S(1)}, bf16[4,48,1536]{2,1,0:T(8,128)(2,1)S(1)}, u32[]{:S(2)}, u32[]{:S(2)}) %collective-permute-start.46) | collective-permute-done | bytes 589856 | tf_op jit(solution)/shard_map/ppermute | solution.py:601
  479.1 12.1 %collective-permute-done.47 = bf16[4,48,1280]{2,1,0:T(8,128)(2,1)S(1)} collective-permute-done((bf16[4,48,1280]{2,1,0:T(8,128)(2,1)S(1)}, bf16[4,48,1280]{2,1,0:T(8,128)(2,1)S(1)}, u32[]{:S(2)}, u32[]{:S(2)}) %collective-permute-start.47) | collective-permute-done | bytes 491552 | tf_op jit(solution)/shard_map/ppermute | solution.py:601
  491.3 4.1 arrange.10
  495.5 3.5 copy.28
  499.0 3.9 arrange.11
  (585 shorter events, 149.2 us)
Async XLA Ops:
  7.2 141.3 %all-gather.5.cloned.1.call-start = ((), (), s32[]{:S(2)}) async-start(), calls=%async_computation.1 | async-start | bytes 1671168 | tf_op jit(solution)/shard_map/all_gather | solution.py:863
  8.3 19.2 %copy-start.167 = (f32[3,768]{1,0:T(4,128)S(1)}, f32[3,768]{1,0:T(4,128)}, u32[]{:S(2)}) copy-start(f32[3,768]{1,0:T(4,128)} %param.20) | copy-start | bytes 27652
  8.3 20.4 %copy-start.112 = (bf16[1,512,768]{2,1,0:T(8,128)(2,1)S(1)}, bf16[1,512,768]{2,1,0:T(8,128)(2,1)}, u32[]{:S(2)}) copy-start(bf16[1,512,768]{2,1,0:T(8,128)(2,1)} %param.14) | copy-start | bytes 2359300
  8.3 20.4 %collective-permute-start = (bf16[256,768]{1,0:T(8,128)(2,1)S(1)}, bf16[256,768]{1,0:T(8,128)(2,1)S(1)}, u32[]{:S(2)}, u32[]{:S(2)}) collective-permute-start(bf16[256,768]{1,0:T(8,128)(2,1)S(1)} %slice_bitcast_fusion), channel_id=1, source_target_pairs={{0,1},{2,3},{4,5},{6,7},{8,9},{10,11},{12,13},{14,15},{16,17},{18,... | collective-permute-start | bytes 1179656 | tf_op jit(solution)/shard_map/ppermute | solution.py:844
  14.3 14.7 %collective-permute-start.1 = (bf16[1,96,1152]{2,1,0:T(8,128)(2,1)S(1)}, bf16[1,96,1152]{2,1,0:T(8,128)(2,1)}, u32[]{:S(2)}, u32[]{:S(2)}) collective-permute-start(bf16[1,96,1152]{2,1,0:T(8,128)(2,1)S(1)} %pad_maximum_fusion.22), channel_id=1, source_target_pairs={{0,1},{1,0},{2,3},{3,2},{4,5},{5,4},{6,7},{7,6},{8,9},{9,8},{10,11... | collective-permute-start | bytes 663560 | tf_op jit(solution)/shard_map/ppermute | solution.py:598
  15.4 16.2 %collective-permute-start.2 = (bf16[48,2048]{1,0:T(8,128)(2,1)S(1)}, bf16[48,2048]{1,0:T(8,128)(2,1)S(1)}, u32[]{:S(2)}, u32[]{:S(2)}) collective-permute-start(bf16[48,2048]{1,0:T(8,128)(2,1)S(1)} %pad_maximum_fusion.23), channel_id=1, source_target_pairs={{0,1},{1,0},{2,3},{3,2},{4,5},{5,4},{6,7},{7,6},{8,9},{9,8},{10,11... | collective-permute-start | bytes 589832 | tf_op jit(solution)/shard_map/ppermute | solution.py:598
  18.4 14.3 %collective-permute-start.3 = (bf16[64,768]{1,0:T(8,128)(2,1)S(1)}, bf16[64,768]{1,0:T(8,128)(2,1)S(1)}, u32[]{:S(2)}, u32[]{:S(2)}) collective-permute-start(bf16[64,768]{1,0:T(8,128)(2,1)S(1)} %dynamic-slice_bitcast_fusion.2), channel_id=1, source_target_pairs={{0,1},{1,0},{2,3},{3,2},{4,5},{5,4},{6,7},{7,6},{8,9},{9,8},{10,11... | collective-permute-start | bytes 294920 | tf_op jit(solution)/shard_map/ppermute | solution.py:598
  33.0 52.5 %copy-start.13 = (bf16[768,768]{1,0:T(8,128)(2,1)}, bf16[768,768]{1,0:T(8,128)(2,1)S(1)}, u32[]{:S(2)}) copy-start(bf16[768,768]{1,0:T(8,128)(2,1)S(1)} %fusion.2.refs_0_) | copy-start | bytes 3538948
  37.0 10.0 %collective-permute-start.4 = (bf16[1,96,1152]{2,1,0:T(8,128)(2,1)}, bf16[1,96,1152]{2,1,0:T(8,128)(2,1)}, u32[]{:S(2)}, u32[]{:S(2)}) collective-permute-start(bf16[1,96,1152]{2,1,0:T(8,128)(2,1)} %collective-permute-done.1), channel_id=1, source_target_pairs={{0,8},{2,10},{4,12},{6,14},{8,0},{10,2},{12,4},{14,6},{16,24},{18,... | collective-permute-start | bytes 663560 | tf_op jit(solution)/shard_map/ppermute | solution.py:601
  38.6 13.2 %collective-permute-start.6 = (bf16[1,96,1920]{2,1,0:T(8,128)(2,1)}, bf16[1,96,1920]{2,1,0:T(8,128)(2,1)}, u32[]{:S(2)}, u32[]{:S(2)}) collective-permute-start(bf16[1,96,1920]{2,1,0:T(8,128)(2,1)} %bitcast_dynamic-update-slice_fusion), channel_id=1, source_target_pairs={{0,1},{1,0},{2,3},{3,2},{4,5},{5,4},{6,7},{7,6},{8,9},{9,8},{10,11... | collective-permute-start | bytes 1105928 | tf_op jit(solution)/shard_map/ppermute | solution.py:598
  41.1 107.3 %all-gather.3.cloned.1.call-start = ((), (), s32[]{:S(2)}) async-start(), calls=%async_computation | async-start | bytes 3342336 | tf_op jit(solution)/shard_map/all_gather | solution.py:861
  48.1 12.1 %collective-permute-start.5 = (bf16[2,96,1152]{2,1,0:T(8,128)(2,1)S(1)}, bf16[2,96,1152]{2,1,0:T(8,128)(2,1)S(1)}, u32[]{:S(2)}, u32[]{:S(2)}) collective-permute-start(bf16[2,96,1152]{2,1,0:T(8,128)(2,1)S(1)} %pad_maximum_fusion.17), channel_id=1, source_target_pairs={{0,4},{2,6},{4,0},{6,2},{8,12},{10,14},{12,8},{14,10},{16,20},{18,... | collective-permute-start | bytes 1327112 | tf_op jit(solution)/shard_map/ppermute | solution.py:601
  52.8 67.7 %copy-start.28 = (bf16[1024,384]{1,0:T(8,128)(2,1)}, bf16[1024,384]{1,0:T(8,128)(2,1)S(1)}, u32[]{:S(2)}) copy-start(bf16[1024,384]{1,0:T(8,128)(2,1)S(1)} %convolution_convert_fusion.7.refs_0_) | copy-start | bytes 2359300
  53.8 66.7 %copy-start.30 = (bf16[1024,384]{1,0:T(8,128)(2,1)}, bf16[1024,384]{1,0:T(8,128)(2,1)S(1)}, u32[]{:S(2)}) copy-start(bf16[1024,384]{1,0:T(8,128)(2,1)S(1)} %convolution_convert_fusion.6.refs_1_) | copy-start | bytes 2359300
  61.0 18.6 %collective-permute-start.7 = (bf16[4,96,1152]{2,1,0:T(8,128)(2,1)}, bf16[4,96,1152]{2,1,0:T(8,128)(2,1)}, u32[]{:S(2)}, u32[]{:S(2)}) collective-permute-start(bf16[4,96,1152]{2,1,0:T(8,128)(2,1)} %constant_dynamic-update-slice_fusion.mine_ref), channel_id=1, source_target_pairs={{0,2},{2,0},{4,6},{6,4},{8,10},{10,8},{12,14},{14,12},{16,18},{18,... | collective-permute-start | bytes 2654216 | tf_op jit(solution)/shard_map/ppermute | solution.py:601
  61.0 15.2 %collective-permute-start.8 = (bf16[1,96,1920]{2,1,0:T(8,128)(2,1)}, bf16[1,96,1920]{2,1,0:T(8,128)(2,1)S(1)}, u32[]{:S(2)}, u32[]{:S(2)}) collective-permute-start(bf16[1,96,1920]{2,1,0:T(8,128)(2,1)} %collective-permute-done.6), channel_id=1, source_target_pairs={{0,8},{2,10},{4,12},{6,14},{8,0},{10,2},{12,4},{14,6},{16,24},{18,... | collective-permute-start | bytes 1105928 | tf_op jit(solution)/shard_map/ppermute | solution.py:601
  61.3 36.8 %collective-permute-start.10 = (bf16[1024,768]{1,0:T(8,128)(2,1)}, bf16[1024,768]{1,0:T(8,128)(2,1)S(1)}, u32[]{:S(2)}, u32[]{:S(2)}) collective-permute-start(bf16[1024,768]{1,0:T(8,128)(2,1)} %bitcast.173), channel_id=1, source_target_pairs={{0,1},{1,0},{2,3},{3,2},{4,5},{5,4},{6,7},{7,6},{8,9},{9,8},{10,11... | collective-permute-start | bytes 4718600 | tf_op jit(solution)/shard_map/ppermute | solution.py:598
  77.2 20.9 %collective-permute-start.9 = (bf16[2,96,1920]{2,1,0:T(8,128)(2,1)S(1)}, bf16[2,96,1920]{2,1,0:T(8,128)(2,1)S(1)}, u32[]{:S(2)}, u32[]{:S(2)}) collective-permute-start(bf16[2,96,1920]{2,1,0:T(8,128)(2,1)S(1)} %pad_maximum_fusion.9), channel_id=1, source_target_pairs={{0,4},{2,6},{4,0},{6,2},{8,12},{10,14},{12,8},{14,10},{16,20},{18,... | collective-permute-start | bytes 2211848 | tf_op jit(solution)/shard_map/ppermute | solution.py:601
  90.9 16.9 %copy-start.17 = (bf16[512,384]{1,0:T(8,128)(2,1)}, bf16[512,384]{1,0:T(8,128)(2,1)S(1)}, u32[]{:S(2)}) copy-start(bf16[512,384]{1,0:T(8,128)(2,1)S(1)} %get-tuple-element.188.refs_0_.out_ref) | copy-start | bytes 1179652
  100.2 3.6 collective-permute-start.11
  107.1 31.5 %copy-start.66 = (bf16[4,96,768]{2,1,0:T(8,128)(2,1)}, bf16[4,96,768]{2,1,0:T(8,128)(2,1)S(1)}, u32[]{:S(2)}) copy-start(bf16[4,96,768]{2,1,0:T(8,128)(2,1)S(1)} %get-tuple-element.186) | copy-start | bytes 1769476
  111.3 27.4 %copy-start.8 = (f32[512,768]{1,0:T(8,128)}, f32[512,768]{1,0:T(8,128)S(1)}, u32[]{:S(2)}) copy-start(f32[512,768]{1,0:T(8,128)S(1)} %get-tuple-element.308.refs_4_) | copy-start | bytes 4718596
  140.4 25.9 %copy-start.6 = (f32[512,768]{1,0:T(8,128)}, f32[512,768]{1,0:T(8,128)S(1)}, u32[]{:S(2)}) copy-start(f32[512,768]{1,0:T(8,128)S(1)} %get-tuple-element.306.refs_8_) | copy-start | bytes 4718596
  178.8 22.7 %collective-permute-start.12 = (bf16[16,48,1408]{2,1,0:T(8,128)(2,1)}, bf16[16,48,1408]{2,1,0:T(8,128)(2,1)}, u32[]{:S(2)}, u32[]{:S(2)}) collective-permute-start(bf16[16,48,1408]{2,1,0:T(8,128)(2,1)} %maximum_maximum_fusion.1), channel_id=1, source_target_pairs={{0,2},{2,0},{4,6},{6,4},{8,10},{10,8},{12,14},{14,12},{16,18},{18,... | collective-permute-start | bytes 6488072 | tf_op jit(solution)/shard_map/ppermute | solution.py:601
  178.9 26.5 %collective-permute-start.13 = (bf16[16,48,2048]{2,1,0:T(8,128)(2,1)}, bf16[16,48,2048]{2,1,0:T(8,128)(2,1)}, u32[]{:S(2)}, u32[]{:S(2)}) collective-permute-start(bf16[16,48,2048]{2,1,0:T(8,128)(2,1)} %pad_maximum_fusion), channel_id=1, source_target_pairs={{0,2},{2,0},{4,6},{6,4},{8,10},{10,8},{12,14},{14,12},{16,18},{18,... | collective-permute-start | bytes 9437192 | tf_op jit(solution)/shard_map/ppermute | solution.py:601
  203.7 32.2 %collective-permute-start.15 = (bf16[8,48,1408]{2,1,0:T(8,128)(2,1)S(1)}, bf16[8,48,1408]{2,1,0:T(8,128)(2,1)S(1)}, u32[]{:S(2)}, u32[]{:S(2)}) collective-permute-start(bf16[8,48,1408]{2,1,0:T(8,128)(2,1)S(1)} %pad_maximum_fusion.5), channel_id=1, source_target_pairs={{0,4},{2,6},{4,0},{6,2},{8,12},{10,14},{12,8},{14,10},{16,20},{18,... | collective-permute-start | bytes 3244040 | tf_op jit(solution)/shard_map/ppermute | solution.py:601
  207.4 41.6 %collective-permute-start.14 = (bf16[8,48,2048]{2,1,0:T(8,128)(2,1)S(1)}, bf16[8,48,2048]{2,1,0:T(8,128)(2,1)S(1)}, u32[]{:S(2)}, u32[]{:S(2)}) collective-permute-start(bf16[8,48,2048]{2,1,0:T(8,128)(2,1)S(1)} %add_convert_fusion), channel_id=1, source_target_pairs={{0,1},{1,0},{2,3},{3,2},{4,5},{5,4},{6,7},{7,6},{8,9},{9,8},{10,11... | collective-permute-start | bytes 4718600 | tf_op jit(solution)/shard_map/ppermute | solution.py:598
  221.8 27.6 %copy-start.95 = (bf16[1,2,4,96,384]{4,3,2,1,0:T(8,128)(2,1)S(1)}, bf16[1,2,4,96,384]{4,3,2,1,0:T(8,128)(2,1)}, u32[]{:S(2)}) copy-start(bf16[1,2,4,96,384]{4,3,2,1,0:T(8,128)(2,1)} %copy-done.94) | copy-start | bytes 1769476
  233.2 28.2 %copy-start = (bf16[2048,768]{1,0:T(8,128)(2,1)}, bf16[2048,768]{1,0:T(8,128)(2,1)S(1)}, u32[]{:S(2)}) copy-start(bf16[2048,768]{1,0:T(8,128)(2,1)S(1)} %get-tuple-element.272.refs_2_.refs_3_) | copy-start | bytes 9437188
  273.5 40.9 %collective-permute-start.20 = (bf16[16,48,1536]{2,1,0:T(8,128)(2,1)S(1)}, bf16[16,48,1536]{2,1,0:T(8,128)(2,1)S(1)}, u32[]{:S(2)}, u32[]{:S(2)}) collective-permute-start(bf16[16,48,1536]{2,1,0:T(8,128)(2,1)S(1)} %maximum_maximum_fusion), channel_id=1, source_target_pairs={{0,2},{2,0},{4,6},{6,4},{8,10},{10,8},{12,14},{14,12},{16,18},{18,... | collective-permute-start | bytes 7077896 | tf_op jit(solution)/shard_map/ppermute | solution.py:601
  276.1 15.1 %collective-permute-start.16 = (bf16[4,48,1408]{2,1,0:T(8,128)(2,1)S(1)}, bf16[4,48,1408]{2,1,0:T(8,128)(2,1)S(1)}, u32[]{:S(2)}, u32[]{:S(2)}) collective-permute-start(bf16[4,48,1408]{2,1,0:T(8,128)(2,1)S(1)} %add_convert_fusion.6), channel_id=1, source_target_pairs={{0,1},{1,0},{2,3},{3,2},{4,5},{5,4},{6,7},{7,6},{8,9},{9,8},{10,11... | collective-permute-start | bytes 1622024 | tf_op jit(solution)/shard_map/ppermute | solution.py:598
  277.9 19.7 %collective-permute-start.17 = (bf16[4,48,2048]{2,1,0:T(8,128)(2,1)S(1)}, bf16[4,48,2048]{2,1,0:T(8,128)(2,1)S(1)}, u32[]{:S(2)}, u32[]{:S(2)}) collective-permute-start(bf16[4,48,2048]{2,1,0:T(8,128)(2,1)S(1)} %add_convert_fusion.2), channel_id=1, source_target_pairs={{0,4},{2,6},{4,0},{6,2},{8,12},{10,14},{12,8},{14,10},{16,20},{18,... | collective-permute-start | bytes 2359304 | tf_op jit(solution)/shard_map/ppermute | solution.py:601
  279.7 104.4 %collective-permute-start.29 = (bf16[1024,768]{1,0:T(8,128)(2,1)}, bf16[1024,768]{1,0:T(8,128)(2,1)}, u32[]{:S(2)}, u32[]{:S(2)}) collective-permute-start(bf16[1024,768]{1,0:T(8,128)(2,1)} %back.3), channel_id=1, source_target_pairs={{0,1},{1,0},{2,3},{3,2},{4,5},{5,4},{6,7},{7,6},{8,9},{9,8},{10,11... | collective-permute-start | bytes 4718600 | tf_op jit(solution)/shard_map/ppermute | solution.py:598
  297.8 10.2 %collective-permute-start.18 = (bf16[2,48,1408]{2,1,0:T(8,128)(2,1)S(1)}, bf16[2,48,1408]{2,1,0:T(8,128)(2,1)S(1)}, u32[]{:S(2)}, u32[]{:S(2)}) collective-permute-start(bf16[2,48,1408]{2,1,0:T(8,128)(2,1)S(1)} %add_convert_fusion.12), channel_id=1, source_target_pairs={{0,8},{2,10},{4,12},{6,14},{8,0},{10,2},{12,4},{14,6},{16,24},{18,... | collective-permute-start | bytes 811016 | tf_op jit(solution)/shard_map/ppermute | solution.py:601
  298.5 15.7 %collective-permute-start.19 = (bf16[2,48,2048]{2,1,0:T(8,128)(2,1)S(1)}, bf16[2,48,2048]{2,1,0:T(8,128)(2,1)S(1)}, u32[]{:S(2)}, u32[]{:S(2)}) collective-permute-start(bf16[2,48,2048]{2,1,0:T(8,128)(2,1)S(1)} %add_convert_fusion.10), channel_id=1, source_target_pairs={{0,8},{2,10},{4,12},{6,14},{8,0},{10,2},{12,4},{14,6},{16,24},{18,... | collective-permute-start | bytes 1179656 | tf_op jit(solution)/shard_map/ppermute | solution.py:601
  317.1 12.9 %collective-permute-start.21 = (bf16[1,48,1408]{2,1,0:T(8,128)(2,1)S(1)}, bf16[1,48,1408]{2,1,0:T(8,128)(2,1)S(1)}, u32[]{:S(2)}, u32[]{:S(2)}) collective-permute-start(bf16[1,48,1408]{2,1,0:T(8,128)(2,1)S(1)} %add_convert_fusion.19), channel_id=1, source_target_pairs={{0,16},{2,18},{4,20},{6,22},{8,24},{10,26},{12,28},{14,30},{16,0},... | collective-permute-start | bytes 405512 | tf_op jit(solution)/shard_map/ppermute | solution.py:601
  321.4 12.1 %collective-permute-start.22 = (bf16[1,48,2048]{2,1,0:T(8,128)(2,1)S(1)}, bf16[1,48,2048]{2,1,0:T(8,128)(2,1)S(1)}, u32[]{:S(2)}, u32[]{:S(2)}) collective-permute-start(bf16[1,48,2048]{2,1,0:T(8,128)(2,1)S(1)} %add_convert_fusion.15), channel_id=1, source_target_pairs={{0,16},{2,18},{4,20},{6,22},{8,24},{10,26},{12,28},{14,30},{16,0},... | collective-permute-start | bytes 589832 | tf_op jit(solution)/shard_map/ppermute | solution.py:601
  321.9 39.9 %collective-permute-start.25 = (bf16[8,48,1536]{2,1,0:T(8,128)(2,1)}, bf16[8,48,1536]{2,1,0:T(8,128)(2,1)}, u32[]{:S(2)}, u32[]{:S(2)}) collective-permute-start(bf16[8,48,1536]{2,1,0:T(8,128)(2,1)} %pad_maximum_fusion.3), channel_id=1, source_target_pairs={{0,4},{2,6},{4,0},{6,2},{8,12},{10,14},{12,8},{14,10},{16,20},{18,... | collective-permute-start | bytes 3538952 | tf_op jit(solution)/shard_map/ppermute | solution.py:601
  333.7 27.1 %collective-permute-start.24 = (bf16[1,48,2048]{2,1,0:T(8,128)(2,1)S(1)}, bf16[1,48,2048]{2,1,0:T(8,128)(2,1)}, u32[]{:S(2)}, u32[]{:S(2)}) collective-permute-start(bf16[1,48,2048]{2,1,0:T(8,128)(2,1)S(1)} %add_convert_fusion.14), channel_id=1, source_target_pairs={{0,16},{2,18},{4,20},{6,22},{8,24},{10,26},{12,28},{14,30},{16,0},... | collective-permute-start | bytes 589832 | tf_op jit(solution)/shard_map/ppermute | solution.py:601
  333.8 25.9 %collective-permute-start.23 = (bf16[1,48,1408]{2,1,0:T(8,128)(2,1)S(1)}, bf16[1,48,1408]{2,1,0:T(8,128)(2,1)}, u32[]{:S(2)}, u32[]{:S(2)}) collective-permute-start(bf16[1,48,1408]{2,1,0:T(8,128)(2,1)S(1)} %add_convert_fusion.18), channel_id=1, source_target_pairs={{0,16},{2,18},{4,20},{6,22},{8,24},{10,26},{12,28},{14,30},{16,0},... | collective-permute-start | bytes 405512 | tf_op jit(solution)/shard_map/ppermute | solution.py:601
  359.4 24.4 %collective-permute-start.28 = (bf16[16,48,1280]{2,1,0:T(8,128)(2,1)S(1)}, bf16[16,48,1280]{2,1,0:T(8,128)(2,1)S(1)}, u32[]{:S(2)}, u32[]{:S(2)}) collective-permute-start(bf16[16,48,1280]{2,1,0:T(8,128)(2,1)S(1)} %maximum_maximum_fusion.2), channel_id=1, source_target_pairs={{0,2},{2,0},{4,6},{6,4},{8,10},{10,8},{12,14},{14,12},{16,18},{18,... | collective-permute-start | bytes 5898248 | tf_op jit(solution)/shard_map/ppermute | solution.py:601
  363.2 19.3 %collective-permute-start.27 = (bf16[2,48,2048]{2,1,0:T(8,128)(2,1)S(1)}, bf16[2,48,2048]{2,1,0:T(8,128)(2,1)S(1)}, u32[]{:S(2)}, u32[]{:S(2)}) collective-permute-start(bf16[2,48,2048]{2,1,0:T(8,128)(2,1)S(1)} %pad_maximum_fusion.18), channel_id=1, source_target_pairs={{0,8},{2,10},{4,12},{6,14},{8,0},{10,2},{12,4},{14,6},{16,24},{18,... | collective-permute-start | bytes 1179656 | tf_op jit(solution)/shard_map/ppermute | solution.py:601
  363.4 16.8 %collective-permute-start.26 = (bf16[2,48,1408]{2,1,0:T(8,128)(2,1)S(1)}, bf16[2,48,1408]{2,1,0:T(8,128)(2,1)S(1)}, u32[]{:S(2)}, u32[]{:S(2)}) collective-permute-start(bf16[2,48,1408]{2,1,0:T(8,128)(2,1)S(1)} %pad_maximum_fusion.20), channel_id=1, source_target_pairs={{0,8},{2,10},{4,12},{6,14},{8,0},{10,2},{12,4},{14,6},{16,24},{18,... | collective-permute-start | bytes 811016 | tf_op jit(solution)/shard_map/ppermute | solution.py:601
  365.3 18.3 %collective-permute-start.32 = (bf16[4,48,1536]{2,1,0:T(8,128)(2,1)S(1)}, bf16[4,48,1536]{2,1,0:T(8,128)(2,1)S(1)}, u32[]{:S(2)}, u32[]{:S(2)}) collective-permute-start(bf16[4,48,1536]{2,1,0:T(8,128)(2,1)S(1)} %add_convert_fusion.3), channel_id=1, source_target_pairs={{0,1},{1,0},{2,3},{3,2},{4,5},{5,4},{6,7},{7,6},{8,9},{9,8},{10,11... | collective-permute-start | bytes 1769480 | tf_op jit(solution)/shard_map/ppermute | solution.py:598
  367.3 16.3 %copy-start.123 = (bf16[8,48,1536]{2,1,0:T(8,128)(2,1)S(1)}, bf16[8,48,1536]{2,1,0:T(8,128)(2,1)}, u32[]{:S(2)}) copy-start(bf16[8,48,1536]{2,1,0:T(8,128)(2,1)} %copy-done.122) | copy-start | bytes 3538948
  380.2 16.1 %collective-permute-start.30 = (bf16[256,768]{1,0:T(8,128)(2,1)S(1)}, bf16[256,768]{1,0:T(8,128)(2,1)S(1)}, u32[]{:S(2)}, u32[]{:S(2)}) collective-permute-start(bf16[256,768]{1,0:T(8,128)(2,1)S(1)} %copy-done.140), channel_id=1, source_target_pairs={{1,0},{3,2},{5,4},{7,6},{9,8},{11,10},{13,12},{15,14},{17,16},{19,... | collective-permute-start | bytes 1179656 | tf_op jit(solution)/shard_map/ppermute | solution.py:1022
  384.1 31.7 %collective-permute-start.31 = (bf16[8,48,1280]{2,1,0:T(8,128)(2,1)S(1)}, bf16[8,48,1280]{2,1,0:T(8,128)(2,1)S(1)}, u32[]{:S(2)}, u32[]{:S(2)}) collective-permute-start(bf16[8,48,1280]{2,1,0:T(8,128)(2,1)S(1)} %add_convert_fusion.1), channel_id=1, source_target_pairs={{0,1},{1,0},{2,3},{3,2},{4,5},{5,4},{6,7},{7,6},{8,9},{9,8},{10,11... | collective-permute-start | bytes 2949128 | tf_op jit(solution)/shard_map/ppermute | solution.py:598
  394.2 20.5 %collective-permute-start.36 = (bf16[4,48,2048]{2,1,0:T(8,128)(2,1)S(1)}, bf16[4,48,2048]{2,1,0:T(8,128)(2,1)S(1)}, u32[]{:S(2)}, u32[]{:S(2)}) collective-permute-start(bf16[4,48,2048]{2,1,0:T(8,128)(2,1)S(1)} %pad_maximum_fusion.8), channel_id=1, source_target_pairs={{0,4},{2,6},{4,0},{6,2},{8,12},{10,14},{12,8},{14,10},{16,20},{18,... | collective-permute-start | bytes 2359304 | tf_op jit(solution)/shard_map/ppermute | solution.py:601
  396.0 30.4 %collective-permute-start.35 = (bf16[4,48,1408]{2,1,0:T(8,128)(2,1)S(1)}, bf16[4,48,1408]{2,1,0:T(8,128)(2,1)S(1)}, u32[]{:S(2)}, u32[]{:S(2)}) collective-permute-start(bf16[4,48,1408]{2,1,0:T(8,128)(2,1)S(1)} %pad_maximum_fusion.15), channel_id=1, source_target_pairs={{0,4},{2,6},{4,0},{6,2},{8,12},{10,14},{12,8},{14,10},{16,20},{18,... | collective-permute-start | bytes 1622024 | tf_op jit(solution)/shard_map/ppermute | solution.py:601
  416.1 22.0 %collective-permute-start.39 = (bf16[8,48,2048]{2,1,0:T(8,128)(2,1)S(1)}, bf16[8,48,2048]{2,1,0:T(8,128)(2,1)S(1)}, u32[]{:S(2)}, u32[]{:S(2)}) collective-permute-start(bf16[8,48,2048]{2,1,0:T(8,128)(2,1)S(1)} %pad_maximum_fusion.1.mine_ref), channel_id=1, source_target_pairs={{0,2},{2,0},{4,6},{6,4},{8,10},{10,8},{12,14},{14,12},{16,18},{18,... | collective-permute-start | bytes 4718600 | tf_op jit(solution)/shard_map/ppermute | solution.py:601
  416.3 11.3 %collective-permute-start.34 = (bf16[2,48,1536]{2,1,0:T(8,128)(2,1)S(1)}, bf16[2,48,1536]{2,1,0:T(8,128)(2,1)S(1)}, u32[]{:S(2)}, u32[]{:S(2)}) collective-permute-start(bf16[2,48,1536]{2,1,0:T(8,128)(2,1)S(1)} %add_convert_fusion.11), channel_id=1, source_target_pairs={{0,8},{2,10},{4,12},{6,14},{8,0},{10,2},{12,4},{14,6},{16,24},{18,... | collective-permute-start | bytes 884744 | tf_op jit(solution)/shard_map/ppermute | solution.py:601
  416.6 18.0 %collective-permute-start.33 = (bf16[4,48,1280]{2,1,0:T(8,128)(2,1)S(1)}, bf16[4,48,1280]{2,1,0:T(8,128)(2,1)S(1)}, u32[]{:S(2)}, u32[]{:S(2)}) collective-permute-start(bf16[4,48,1280]{2,1,0:T(8,128)(2,1)S(1)} %add_convert_fusion.9), channel_id=1, source_target_pairs={{0,4},{2,6},{4,0},{6,2},{8,12},{10,14},{12,8},{14,10},{16,20},{18,... | collective-permute-start | bytes 1474568 | tf_op jit(solution)/shard_map/ppermute | solution.py:601
  427.4 15.7 %collective-permute-start.42 = (bf16[8,48,1408]{2,1,0:T(8,128)(2,1)S(1)}, bf16[8,48,1408]{2,1,0:T(8,128)(2,1)S(1)}, u32[]{:S(2)}, u32[]{:S(2)}) collective-permute-start(bf16[8,48,1408]{2,1,0:T(8,128)(2,1)S(1)} %pad_maximum_fusion.6.mine_ref), channel_id=1, source_target_pairs={{0,2},{2,0},{4,6},{6,4},{8,10},{10,8},{12,14},{14,12},{16,18},{18,... | collective-permute-start | bytes 3244040 | tf_op jit(solution)/shard_map/ppermute | solution.py:601
  427.7 10.2 %collective-permute-start.38 = (bf16[1,48,1536]{2,1,0:T(8,128)(2,1)S(1)}, bf16[1,48,1536]{2,1,0:T(8,128)(2,1)S(1)}, u32[]{:S(2)}, u32[]{:S(2)}) collective-permute-start(bf16[1,48,1536]{2,1,0:T(8,128)(2,1)S(1)} %add_convert_fusion.17), channel_id=1, source_target_pairs={{0,16},{2,18},{4,20},{6,22},{8,24},{10,26},{12,28},{14,30},{16,0},... | collective-permute-start | bytes 442376 | tf_op jit(solution)/shard_map/ppermute | solution.py:601
  434.8 8.3 %collective-permute-start.37 = (bf16[2,48,1280]{2,1,0:T(8,128)(2,1)S(1)}, bf16[2,48,1280]{2,1,0:T(8,128)(2,1)S(1)}, u32[]{:S(2)}, u32[]{:S(2)}) collective-permute-start(bf16[2,48,1280]{2,1,0:T(8,128)(2,1)S(1)} %add_convert_fusion.13), channel_id=1, source_target_pairs={{0,8},{2,10},{4,12},{6,14},{8,0},{10,2},{12,4},{14,6},{16,24},{18,... | collective-permute-start | bytes 737288 | tf_op jit(solution)/shard_map/ppermute | solution.py:601
  442.6 9.6 %collective-permute-start.41 = (bf16[1,48,1536]{2,1,0:T(8,128)(2,1)S(1)}, bf16[1,48,1536]{2,1,0:T(8,128)(2,1)S(1)}, u32[]{:S(2)}, u32[]{:S(2)}) collective-permute-start(bf16[1,48,1536]{2,1,0:T(8,128)(2,1)S(1)} %add_convert_fusion.16), channel_id=1, source_target_pairs={{0,16},{2,18},{4,20},{6,22},{8,24},{10,26},{12,28},{14,30},{16,0},... | collective-permute-start | bytes 442376 | tf_op jit(solution)/shard_map/ppermute | solution.py:601
  448.4 9.1 %collective-permute-start.40 = (bf16[1,48,1280]{2,1,0:T(8,128)(2,1)S(1)}, bf16[1,48,1280]{2,1,0:T(8,128)(2,1)S(1)}, u32[]{:S(2)}, u32[]{:S(2)}) collective-permute-start(bf16[1,48,1280]{2,1,0:T(8,128)(2,1)S(1)} %add_convert_fusion.21), channel_id=1, source_target_pairs={{0,16},{2,18},{4,20},{6,22},{8,24},{10,26},{12,28},{14,30},{16,0},... | collective-permute-start | bytes 368648 | tf_op jit(solution)/shard_map/ppermute | solution.py:601
  452.3 10.1 %collective-permute-start.44 = (bf16[2,48,1536]{2,1,0:T(8,128)(2,1)S(1)}, bf16[2,48,1536]{2,1,0:T(8,128)(2,1)S(1)}, u32[]{:S(2)}, u32[]{:S(2)}) collective-permute-start(bf16[2,48,1536]{2,1,0:T(8,128)(2,1)S(1)} %pad_maximum_fusion.19), channel_id=1, source_target_pairs={{0,8},{2,10},{4,12},{6,14},{8,0},{10,2},{12,4},{14,6},{16,24},{18,... | collective-permute-start | bytes 884744 | tf_op jit(solution)/shard_map/ppermute | solution.py:601
  462.5 14.8 %collective-permute-start.46 = (bf16[4,48,1536]{2,1,0:T(8,128)(2,1)S(1)}, bf16[4,48,1536]{2,1,0:T(8,128)(2,1)S(1)}, u32[]{:S(2)}, u32[]{:S(2)}) collective-permute-start(bf16[4,48,1536]{2,1,0:T(8,128)(2,1)S(1)} %pad_maximum_fusion.14), channel_id=1, source_target_pairs={{0,4},{2,6},{4,0},{6,2},{8,12},{10,14},{12,8},{14,10},{16,20},{18,... | collective-permute-start | bytes 1769480 | tf_op jit(solution)/shard_map/ppermute | solution.py:601
  463.4 7.3 %collective-permute-start.43 = (bf16[1,48,1280]{2,1,0:T(8,128)(2,1)S(1)}, bf16[1,48,1280]{2,1,0:T(8,128)(2,1)S(1)}, u32[]{:S(2)}, u32[]{:S(2)}) collective-permute-start(bf16[1,48,1280]{2,1,0:T(8,128)(2,1)S(1)} %add_convert_fusion.20), channel_id=1, source_target_pairs={{0,16},{2,18},{4,20},{6,22},{8,24},{10,26},{12,28},{14,30},{16,0},... | collective-permute-start | bytes 368648 | tf_op jit(solution)/shard_map/ppermute | solution.py:601
  470.8 6.9 %collective-permute-start.45 = (bf16[2,48,1280]{2,1,0:T(8,128)(2,1)S(1)}, bf16[2,48,1280]{2,1,0:T(8,128)(2,1)S(1)}, u32[]{:S(2)}, u32[]{:S(2)}) collective-permute-start(bf16[2,48,1280]{2,1,0:T(8,128)(2,1)S(1)} %pad_maximum_fusion.21), channel_id=1, source_target_pairs={{0,8},{2,10},{4,12},{6,14},{8,0},{10,2},{12,4},{14,6},{16,24},{18,... | collective-permute-start | bytes 737288 | tf_op jit(solution)/shard_map/ppermute | solution.py:601
  477.4 13.9 %collective-permute-start.48 = (bf16[8,48,1536]{2,1,0:T(8,128)(2,1)S(1)}, bf16[8,48,1536]{2,1,0:T(8,128)(2,1)S(1)}, u32[]{:S(2)}, u32[]{:S(2)}) collective-permute-start(bf16[8,48,1536]{2,1,0:T(8,128)(2,1)S(1)} %pad_maximum_fusion.4.mine_ref), channel_id=1, source_target_pairs={{0,2},{2,0},{4,6},{6,4},{8,10},{10,8},{12,14},{14,12},{16,18},{18,... | collective-permute-start | bytes 3538952 | tf_op jit(solution)/shard_map/ppermute | solution.py:601
  477.7 13.5 %collective-permute-start.47 = (bf16[4,48,1280]{2,1,0:T(8,128)(2,1)S(1)}, bf16[4,48,1280]{2,1,0:T(8,128)(2,1)S(1)}, u32[]{:S(2)}, u32[]{:S(2)}) collective-permute-start(bf16[4,48,1280]{2,1,0:T(8,128)(2,1)S(1)} %pad_maximum_fusion.16), channel_id=1, source_target_pairs={{0,4},{2,6},{4,0},{6,2},{8,12},{10,14},{12,8},{14,10},{16,20},{18,... | collective-permute-start | bytes 1474568 | tf_op jit(solution)/shard_map/ppermute | solution.py:601
  495.5 3.5 collective-permute-start.49
  (157 other events, 848.1 us)
Sparse Core Ops, SparseCore 0:
  41.3 40.7 all-gather.4
  100.3 45.5 all-gather.2

commit v3 on v2

--- a/solution.py
+++ b/solution.py
@@ -1039,7 +1039,7 @@
         v.decoder_grad = v.grad_a + resid0_grad
         after(v.decoder_grad)
 
-    BITS = (2, 1, 0)
+    BITS = (1, 0)
     ORDERS = {GATE: tp_first, DOWN: tp_second, CROSS: tp_second, SELF: tp_first}
     v.memory_w = (None, None)
     out = {}
@@ -1051,6 +1051,8 @@
     def advance(name):
         came = go(name)
         if came is not None:
+            if name == DOWN:
+                came[0] = came[0][0].T
             out[name] = came
             after(came)
 
@@ -1068,11 +1070,11 @@
     mem_b0, mem_b1 = for_each(memory_back)
     P_, R, A, B, E, D = [functools.partial(advance, name) for name in (PROJECT, REST, GATE, DOWN, CROSS, SELF)]
     agenda_steps = (
-        send_halo, send_project, send_ffn, plan, norm_a, P_, gather_ffn, send_rest, self0, P_, mem0, R, keys0, P_, R,
-        P_, self1, take_memory, R, R, queries, keys1, cross0, cross1, ffn, gate_dw, down_dw, norm_m_grad, A,
-        norm_m_back, outs_dw, cross_b0, B, cross_b1, A, norm_c_back, mem_b0, part0, B, mem_dw0, mem_dw1, cross_dw, A,
-        B, self_b1, E, A, B, self_b0, A, B, norm_a_grad, self_dw, E, A, B, take_partial, D, mem_b1, A, B, norm_a_back,
-        E, D, A, B, E, D, A, E, D, B, E, D, E, D, E, D, E, D, D,
+        send_halo, send_project, send_ffn, plan, norm_a, P_, gather_ffn, send_rest, self0, P_, mem0, R, keys0, P_,
+        self1, R, R, take_memory, queries, keys1, cross0, cross1, ffn, gate_dw, down_dw, norm_m_grad, A, norm_m_back,
+        outs_dw, cross_b0, B, cross_b1, A, norm_c_back, mem_b0, part0, B, mem_dw0, mem_dw1, cross_dw, A, B, self_b1,
+        E, A, B, self_b0, A, B, norm_a_grad, self_dw, E, A, B, take_partial, D, mem_b1, A, B, norm_a_back, E, D, A, B,
+        E, D, A, E, D, B, E, D, E, D, E, D, E, D, D,
     )
     for step in agenda_steps:
         step()
@@ -1095,7 +1097,7 @@
         out[CROSS][0],
         out[DOWN][1],
         out[GATE][0],
-        out[DOWN][0][0].T,
+        out[DOWN][0],
     )
 
 

time: 517 us -> 511 us (0.988)
  matrix products: 23.7 us -> 40.2 us
  starting transfers between devices: 58.4 us -> 43.4 us
  local copies, waits for them, and re-layouts: 80.3 us -> 70.7 us
  waiting for transfers between devices: 152 us -> 144 us
  Pallas kernels: 149 us -> 156 us
    ppermute x38 -> x36, waiting for transfers between devices: 119 us -> 102 us  [across(): return lax.ppermute(x, 'dp', [(i, i ^ mask) for i in range(self.n_dp)])]
    dot_general x22, matrix products: 23.7 us -> 40.2 us  [contract(): lax.dot_general(a, b, (((i,), (j,)), ((), ())), preferred_element_type=F32)]
    unnamed x345 -> x339, local copies, waits for them, and re-layouts: 45.7 us -> 35.6 us
    ppermute x10, waiting for transfers between devices: 32.3 us -> 42.2 us  [across_tp(): return lax.ppermute(x, 'tp', [(0, 1), (1, 0)])]
    ppermute x38 -> x36, starting transfers between devices: 32.7 us -> 24.4 us  [across(): return lax.ppermute(x, 'dp', [(i, i ^ mask) for i in range(self.n_dp)])]
    ppermute x10, starting transfers between devices: 19.2 us -> 12.6 us  [across_tp(): return lax.ppermute(x, 'tp', [(0, 1), (1, 0)])]
  transfers between devices with their start and end apart: 52 -> 50, of which waited for: 24 -> 26; matrix products, arithmetic and copies ran while one was open for 17% -> 21% of each run, Pallas kernels for 19% -> 20%
where the time goes in v3:
time: 511 us; the launch traced here: 504 us
  Pallas kernels  156 us (31%)
  waiting for transfers between devices  144 us (28%)
  local copies, waits for them, and re-layouts  70.7 us (14%)
  starting transfers between devices  43.4 us (8%)
  matrix products  40.2 us (8%)
  other arithmetic  32.6 us (6%)
  between operations  17.4 us (3%)
    ppermute x36, waiting for transfers between devices, across(): return lax.ppermute(x, 'dp', [(i, i ^ mask) for i in range(self.n_dp)])  102 us
    ppermute x10, waiting for transfers between devices, across_tp(): return lax.ppermute(x, 'tp', [(0, 1), (1, 0)])  42.2 us
    dot_general x22, matrix products, contract(): lax.dot_general(a, b, (((i,), (j,)), ((), ())), preferred_element_type=F32)  40.2 us
    pallas_call x4, Pallas kernels, attend_backward(): pl.pallas_call(functools.partial(backward_kernel, first_part=first_part,...  40.1 us
    unnamed x339, local copies, waits for them, and re-layouts  35.6 us
    pallas_call x9, Pallas kernels, weight_grads(): pl.pallas_call(functools.partial(weight_kernel, n=len(rows), m=len(grads)...  26.4 us
    pallas_call x4, Pallas kernels, attend_forward(): pl.pallas_call(functools.partial(forward_kernel, first_part=first_part, n...  25.7 us
    ppermute x36, starting transfers between devices, across(): return lax.ppermute(x, 'dp', [(i, i ^ mask) for i in range(self.n_dp)])  24.4 us
  transfers between devices with their start and end apart: 50, of which 26 were waited for; matrix products, arithmetic and copies ran while one was open for 21% of the time, Pallas kernels for 20%

profile of v3, /device:TPU:0, one launch (start us, length us, event | category | flops | bytes accessed | tf_op | source)
XLA Modules:
  0.0 504.2 jit_solution(16110024865592689908)
XLA Ops:
  8.3 4.9 collective-permute-start
  32.1 4.2 collective-permute-done.2
  42.9 2.4 collective-permute-start.6
  47.5 3.8 attend_forward.4
  54.0 2.4 collective-permute-start.9
  56.4 6.6 %collective-permute-done.6 = bf16[1,192,1920]{2,1,0:T(8,128)(2,1)} collective-permute-done((bf16[1,192,1920]{2,1,0:T(8,128)(2,1)}, bf16[1,192,1920]{2,1,0:T(8,128)(2,1)}, u32[]{:S(2)}, u32[]{:S(2)}) %collective-permute-start.6) | collective-permute-done | bytes 737312 | tf_op jit(solution)/shard_map/ppermute | solution.py:598
  64.5 3.3 convolution_convert_fusion.7.refs_0_
  67.8 3.3 convolution_convert_fusion.6.refs_1_
  75.7 3.8 attend_forward.5
  79.5 2.3 collective-permute-done.7
  82.6 2.8 collective-permute-done.8.theirs_ref
  87.6 7.0 %collective-permute-done.9.refs_1_ = bf16[1024,768]{1,0:T(8,128)(2,1)} collective-permute-done((bf16[1024,768]{1,0:T(8,128)(2,1)}, bf16[1024,768]{1,0:T(8,128)(2,1)}, u32[]{:S(2)}, u32[]{:S(2)}) %collective-permute-start.9) | collective-permute-done | bytes 1572896 | tf_op jit(solution)/shard_map/ppermute | solution.py:598
  95.3 2.4 multiply_reduce_fusion.5
  100.5 2.4 convolution_convert_fusion.5.refs_0_
  103.0 2.7 convolution_convert_fusion.4.refs_1_
  105.7 2.7 convolution_convert_fusion.3.refs_2_
  108.4 2.7 convolution_convert_fusion.2.refs_3_
  111.1 8.8 %attend_forward.6 = (bf16[512,384]{1,0:T(8,128)(2,1)S(1)}, f32[4,3,256]{2,1,0:T(4,128)S(1)}) custom-call(s32[6,4,128]{2,1,0:T(4,128)S(1)} %copy-done.84, bf16[512,384]{1,0:T(8,128)(2,1)S(1)} %convolution_convert_fusion.15.q_ref, bf16[1024,384]{1,0:T(8,128)(2,1)S(1)} %copy-done.27, bf16[1024,384]{1,0:T(8,128)(2,1)S(1)} %copy-done.29, ...), custom_call_target="tpu_custom_call" | custom-call | flops 1048576 | bytes 1048576 | tf_op jit(solution)/shard_map/attend_forward/pallas_call | solution.py:258
  120.0 2.5 convolution_convert_fusion.1.refs_2_
  122.6 2.7 convolution_convert_fusion.refs_3_
  125.3 9.2 %attend_forward.7 = (bf16[512,384]{1,0:T(8,128)(2,1)S(1)}, f32[4,3,256]{2,1,0:T(4,128)S(1)}) custom-call(s32[6,4,128]{2,1,0:T(4,128)S(1)} %copy-done.84, bf16[512,384]{1,0:T(8,128)(2,1)S(1)} %convolution_convert_fusion.14.q_ref, bf16[1024,384]{1,0:T(8,128)(2,1)S(1)} %convolution_convert_fusion.5.refs_0_, ...), custom_call_target="tpu_custom_call" | custom-call | flops 1048576 | bytes 1048576 | tf_op jit(solution)/shard_map/attend_forward/pallas_call | solution.py:258
  138.0 5.3 %feed_forward.2 = (bf16[512,1024]{1,0:T(8,128)(2,1)S(1)}, bf16[512,2048]{1,0:T(8,128)(2,1)S(1)}) custom-call(bf16[512,768]{1,0:T(8,128)(2,1)S(1)} %get-tuple-element.364.normed_ref.refs_0_, bf16[512,768]{1,0:T(8,128)(2,1)S(1)} %get-tuple-element.198.full_ref.refs_0_.refs_10_, bf16[2,768,1024]{2,1,0:T(8,128)(2,1)} %refs_5_.3, bf16[2,768,1024]{2,1,0:T(8,128)(2,1)} %refs_5_.3, ...), custom_call_target="tpu_custom_call" | custom-call | flops 1048576 | bytes 1048576 | tf_op jit(solution)/shard_map/feed_forward/pallas_call | solution.py:514
  145.6 5.3 %feed_forward.3 = (bf16[512,1024]{1,0:T(8,128)(2,1)S(1)}, bf16[512,2048]{1,0:T(8,128)(2,1)S(1)}) custom-call(bf16[512,768]{1,0:T(8,128)(2,1)S(1)} %get-tuple-element.364.normed_ref.refs_0_, bf16[512,768]{1,0:T(8,128)(2,1)S(1)} %get-tuple-element.198.full_ref.refs_0_.refs_10_, bf16[768,2048]{1,0:T(8,128)(2,1)} %all-gather.3.cloned.1.call-done.gate_ref.up_ref.refs_6_.refs_7_, ...), custom_call_target="tpu_custom_call" | custom-call | flops 1048576 | bytes 1048576 | tf_op jit(solution)/shard_map/feed_forward/pallas_call | solution.py:514
  151.0 5.0 weight_grads.9
  160.9 2.6 weight_grads.10
  163.6 7.5 %norm_back.2 = (f32[512,768]{1,0:T(8,128)S(1)}, bf16[512,768]{1,0:T(8,128)(2,1)S(1)}, f32[1,768]{1,0:T(1,128)S(1)}, bf16[512,384]{1,0:T(8,128)(2,1)S(1)}, bf16[512,384]{1,0:T(8,128)(2,1)S(1)}) custom-call(bf16[512,2048]{1,0:T(8,128)(2,1)S(1)} %copy-done.12, bf16[512,2048]{1,0:T(8,128)(2,1)S(1)} %copy-done.12, ...), custom_call_target="tpu_custom_call" | custom-call | flops 1048576 | bytes 1048576 | tf_op jit(solution)/shard_map/norm_back/pallas_call | solution.py:438
  185.7 14.0 %attend_backward.4 = (bf16[512,384]{1,0:T(8,128)(2,1)S(1)}, bf16[2048,768]{1,0:T(8,128)(2,1)S(1)}) custom-call(s32[6,4,128]{2,1,0:T(4,128)S(1)} %copy-done.84, f32[4,3,256]{2,1,0:T(4,128)S(1)} %copy-done.100, bf16[512,384]{1,0:T(8,128)(2,1)S(1)} %copy-done.80, bf16[512,384]{1,0:T(8,128)(2,1)S(1)} %copy-done.21, bf16[512,384]{1,0:T(8,128)(2,1)S(1)} %copy-done.92, ...), custom_call_target="tpu_custom_call" | custom-call | flops 1048576 | bytes 1048576 | tf_op jit(solution)/shard_map/attend_backward/pallas_call | solution.py:298
  211.0 2.4 multiply_reduce_fusion
  213.4 13.9 %attend_backward.5 = (bf16[512,384]{1,0:T(8,128)(2,1)S(1)}, bf16[2048,768]{1,0:T(8,128)(2,1)S(1)}) custom-call(s32[6,4,128]{2,1,0:T(4,128)S(1)} %copy-done.84, f32[4,3,256]{2,1,0:T(4,128)S(1)} %copy-done.98, bf16[512,384]{1,0:T(8,128)(2,1)S(1)} %copy-done.78, bf16[512,384]{1,0:T(8,128)(2,1)S(1)} %copy-done.24, bf16[512,384]{1,0:T(8,128)(2,1)S(1)} %copy-done.90, ...), custom_call_target="tpu_custom_call" | custom-call | flops 1048576 | bytes 1048576 | tf_op jit(solution)/shard_map/attend_backward/pallas_call | solution.py:298
  227.3 2.7 slice.205
  230.3 12.3 %collective-permute-done.12 = bf16[8,48,2048]{2,1,0:T(8,128)(2,1)S(1)} collective-permute-done((bf16[8,48,2048]{2,1,0:T(8,128)(2,1)S(1)}, bf16[8,48,2048]{2,1,0:T(8,128)(2,1)S(1)}, u32[]{:S(2)}, u32[]{:S(2)}) %collective-permute-start.12) | collective-permute-done | bytes 1572896 | tf_op jit(solution)/shard_map/ppermute | solution.py:598
  243.1 3.7 norm_back.3
  246.7 7.1 %back.3 = bf16[1024,768]{1,0:T(8,128)(2,1)} custom-call(bf16[2048,768]{1,0:T(8,128)(2,1)S(1)} %get-tuple-element.263.refs_0_.refs_1_.refs_2_, bf16[2048,768]{1,0:T(8,128)(2,1)S(1)} %get-tuple-element.263.refs_0_.refs_1_.refs_2_, bf16[2048,768]{1,0:T(8,128)(2,1)S(1)} %get-tuple-element.264.refs_2_.refs_3_, ...), custom_call_target="tpu_custom_call" | custom-call | flops 1048576 | bytes 1048576 | tf_op jit(solution)/shard_map/back/pallas_call | solution.py:421
  253.9 10.4 %weight_grads.13 = (bf16[768,768]{1,0:T(8,128)(2,1)S(1)}, bf16[768,768]{1,0:T(8,128)(2,1)S(1)}) custom-call(bf16[1024,768]{1,0:T(8,128)(2,1)} %bitcast.24.refs_0_, bf16[1024,768]{1,0:T(8,128)(2,1)} %collective-permute-done.9.refs_1_, bf16[2048,768]{1,0:T(8,128)(2,1)S(1)} %get-tuple-element.263.refs_0_.refs_1_.refs_2_, ...), custom_call_target="tpu_custom_call" | custom-call | flops 1048576 | bytes 1048576 | tf_op jit(solution)/shard_map/weight_grads/pallas_call | solution.py:478
  275.4 10.0 %collective-permute-done.14 = bf16[4,48,1408]{2,1,0:T(8,128)(2,1)S(1)} collective-permute-done((bf16[4,48,1408]{2,1,0:T(8,128)(2,1)S(1)}, bf16[4,48,1408]{2,1,0:T(8,128)(2,1)S(1)}, u32[]{:S(2)}, u32[]{:S(2)}) %collective-permute-start.14) | collective-permute-done | bytes 540704 | tf_op jit(solution)/shard_map/ppermute | solution.py:598
  285.6 4.7 collective-permute-done.15
  290.6 2.4 collective-permute-start.16
  295.1 6.1 %attend_backward.6.refs_3_.refs_4_.refs_5_.refs_2_ = bf16[768,1152]{1,0:T(8,128)(2,1)S(1)} custom-call(s32[6,4,128]{2,1,0:T(4,128)S(1)} %copy-done.84, f32[4,3,256]{2,1,0:T(4,128)S(1)} %copy-done.96, bf16[768,384]{1,0:T(8,128)(2,1)S(1)} %copy-done.58, bf16[512,384]{1,0:T(8,128)(2,1)S(1)} %copy-done.18, bf16[512,384]{1,0:T(8,128)(2,1)S(1)} %get-tuple-element.242.grad_ref, ...), custom_call_target="tpu_custom_call" | custom-call | flops 1048576 | bytes 1048576 | tf_op jit(solution)/shard_map/attend_backward/pallas_call | solution.py:298
  301.2 6.3 %collective-permute-done.17 = bf16[2,48,2048]{2,1,0:T(8,128)(2,1)S(1)} collective-permute-done((bf16[2,48,2048]{2,1,0:T(8,128)(2,1)S(1)}, bf16[2,48,2048]{2,1,0:T(8,128)(2,1)S(1)}, u32[]{:S(2)}, u32[]{:S(2)}) %collective-permute-start.17) | collective-permute-done | bytes 393248 | tf_op jit(solution)/shard_map/ppermute | solution.py:601
  315.7 6.1 %attend_backward.7.refs_0_.refs_1_.refs_2_ = bf16[768,1152]{1,0:T(8,128)(2,1)S(1)} custom-call(s32[6,4,128]{2,1,0:T(4,128)S(1)} %copy-done.84, f32[4,3,256]{2,1,0:T(4,128)S(1)} %copy-done.94, bf16[768,384]{1,0:T(8,128)(2,1)S(1)} %copy-done.52, bf16[512,384]{1,0:T(8,128)(2,1)S(1)} %get-tuple-element.179.refs_0_.out_ref, ...), custom_call_target="tpu_custom_call" | custom-call | flops 1048576 | bytes 1048576 | tf_op jit(solution)/shard_map/attend_backward/pallas_call | solution.py:298
  321.8 2.2 collective-permute-done.19
  324.1 3.1 collective-permute-done.20
  327.5 2.9 collective-permute-start.21
  330.4 6.7 %back.4 = f32[768,768]{1,0:T(8,128)S(1)} custom-call(bf16[768,1152]{1,0:T(8,128)(2,1)S(1)} %attend_backward.7.refs_0_.refs_1_.refs_2_, bf16[768,1152]{1,0:T(8,128)(2,1)S(1)} %attend_backward.7.refs_0_.refs_1_.refs_2_, bf16[768,1152]{1,0:T(8,128)(2,1)S(1)} %attend_backward.7.refs_0_.refs_1_.refs_2_, ...), custom_call_target="tpu_custom_call" | custom-call | flops 1048576 | bytes 1048576 | tf_op jit(solution)/shard_map/back/pallas_call | solution.py:421
  339.3 5.3 %weight_grads.17 = (bf16[768,1152]{1,0:T(8,128)(2,1)S(1)}, bf16[768,1152]{1,0:T(8,128)(2,1)S(1)}) custom-call(bf16[768,768]{1,0:T(8,128)(2,1)S(1)} %copy-done.14, bf16[768,1152]{1,0:T(8,128)(2,1)S(1)} %attend_backward.7.refs_0_.refs_1_.refs_2_, bf16[768,1152]{1,0:T(8,128)(2,1)S(1)} %attend_backward.6.refs_3_.refs_4_.refs_5_.refs_2_), custom_call_target="tpu_custom_call" | custom-call | flops 1048576 | bytes 1048576 | tf_op jit(solution)/shard_map/weight_grads/pallas_call | solution.py:478
  362.0 12.2 %collective-permute-done.24 = bf16[2,48,1408]{2,1,0:T(8,128)(2,1)S(1)} collective-permute-done((bf16[2,48,1408]{2,1,0:T(8,128)(2,1)S(1)}, bf16[2,48,1408]{2,1,0:T(8,128)(2,1)S(1)}, u32[]{:S(2)}, u32[]{:S(2)}) %collective-permute-start.24) | collective-permute-done | bytes 270368 | tf_op jit(solution)/shard_map/ppermute | solution.py:601
  378.1 2.7 collective-permute-start.29
  380.8 7.1 %back.5 = f32[1024,768]{1,0:T(8,128)} custom-call(bf16[2048,768]{1,0:T(8,128)(2,1)S(1)} %get-tuple-element.263.refs_0_.refs_1_.refs_2_, bf16[2048,768]{1,0:T(8,128)(2,1)S(1)} %get-tuple-element.263.refs_0_.refs_1_.refs_2_, bf16[2048,768]{1,0:T(8,128)(2,1)S(1)} %copy-done.1, bf16[2048,768]{1,0:T(8,128)(2,1)S(1)} %copy-done.1, bf16[2,768,384]{2,1,0:T(8,128)(2,1)} %refs_5_.5, ...), custom_call_target="tpu_custom_call" | custom-call | flops 1048576 | bytes 1048576 | tf_op jit(solution)/shard_map/back/pallas_call | solution.py:421
  393.2 15.3 %collective-permute-done.34 = bf16[4,48,2048]{2,1,0:T(8,128)(2,1)S(1)} collective-permute-done((bf16[4,48,2048]{2,1,0:T(8,128)(2,1)S(1)}, bf16[4,48,2048]{2,1,0:T(8,128)(2,1)S(1)}, u32[]{:S(2)}, u32[]{:S(2)}) %collective-permute-start.34) | collective-permute-done | bytes 786464 | tf_op jit(solution)/shard_map/ppermute | solution.py:601
  411.2 8.8 %collective-permute-done.33 = bf16[4,48,1408]{2,1,0:T(8,128)(2,1)S(1)} collective-permute-done((bf16[4,48,1408]{2,1,0:T(8,128)(2,1)S(1)}, bf16[4,48,1408]{2,1,0:T(8,128)(2,1)S(1)}, u32[]{:S(2)}, u32[]{:S(2)}) %collective-permute-start.33) | collective-permute-done | bytes 540704 | tf_op jit(solution)/shard_map/ppermute | solution.py:601
  421.6 6.7 %collective-permute-done.31 = bf16[4,48,1280]{2,1,0:T(8,128)(2,1)S(1)} collective-permute-done((bf16[4,48,1280]{2,1,0:T(8,128)(2,1)S(1)}, bf16[4,48,1280]{2,1,0:T(8,128)(2,1)S(1)}, u32[]{:S(2)}, u32[]{:S(2)}) %collective-permute-start.31) | collective-permute-done | bytes 491552 | tf_op jit(solution)/shard_map/ppermute | solution.py:601
  429.1 2.4 collective-permute-done.36
  431.7 4.6 arrange.8
  437.5 3.5 arrange.9
  441.0 2.4 copy.27
  443.3 2.5 collective-permute-start.38
  446.0 6.1 %collective-permute-done.38 = bf16[1,48,1280]{2,1,0:T(8,128)(2,1)S(1)} collective-permute-done((bf16[1,48,1280]{2,1,0:T(8,128)(2,1)}, bf16[1,48,1280]{2,1,0:T(8,128)(2,1)S(1)}, u32[]{:S(2)}, u32[]{:S(2)}) %collective-permute-start.38) | collective-permute-done | bytes 122912 | tf_op jit(solution)/shard_map/ppermute | solution.py:601
  453.2 2.4 collective-permute-done.42
  457.9 5.6 %collective-permute-done.41 = bf16[1,48,1280]{2,1,0:T(8,128)(2,1)S(1)} collective-permute-done((bf16[1,48,1280]{2,1,0:T(8,128)(2,1)S(1)}, bf16[1,48,1280]{2,1,0:T(8,128)(2,1)S(1)}, u32[]{:S(2)}, u32[]{:S(2)}) %collective-permute-start.41) | collective-permute-done | bytes 122912 | tf_op jit(solution)/shard_map/ppermute | solution.py:601
  463.9 5.8 %collective-permute-done.44 = bf16[4,48,1536]{2,1,0:T(8,128)(2,1)S(1)} collective-permute-done((bf16[4,48,1536]{2,1,0:T(8,128)(2,1)S(1)}, bf16[4,48,1536]{2,1,0:T(8,128)(2,1)S(1)}, u32[]{:S(2)}, u32[]{:S(2)}) %collective-permute-start.44) | collective-permute-done | bytes 589856 | tf_op jit(solution)/shard_map/ppermute | solution.py:601
  471.5 12.0 %collective-permute-done.45 = bf16[4,48,1280]{2,1,0:T(8,128)(2,1)S(1)} collective-permute-done((bf16[4,48,1280]{2,1,0:T(8,128)(2,1)S(1)}, bf16[4,48,1280]{2,1,0:T(8,128)(2,1)S(1)}, u32[]{:S(2)}, u32[]{:S(2)}) %collective-permute-start.45) | collective-permute-done | bytes 491552 | tf_op jit(solution)/shard_map/ppermute | solution.py:601
  483.7 4.1 arrange.10
  487.8 2.6 collective-permute-done.47.theirs_ref
  490.4 3.9 arrange.11
  (573 shorter events, 145.3 us)
Async XLA Ops:
  7.2 138.5 %all-gather.5.cloned.1.call-start = ((), (), s32[]{:S(2)}) async-start(), calls=%async_computation.1 | async-start | bytes 1671168 | tf_op jit(solution)/shard_map/all_gather | solution.py:863
  8.3 22.1 %collective-permute-start = (bf16[256,768]{1,0:T(8,128)(2,1)S(1)}, bf16[256,768]{1,0:T(8,128)(2,1)S(1)}, u32[]{:S(2)}, u32[]{:S(2)}) collective-permute-start(bf16[256,768]{1,0:T(8,128)(2,1)S(1)} %slice_bitcast_fusion), channel_id=1, source_target_pairs={{0,1},{2,3},{4,5},{6,7},{8,9},{10,11},{12,13},{14,15},{16,17},{18,... | collective-permute-start | bytes 1179656 | tf_op jit(solution)/shard_map/ppermute | solution.py:844
  14.3 16.1 %copy-start.105 = (bf16[1,512,768]{2,1,0:T(8,128)(2,1)S(1)}, bf16[1,512,768]{2,1,0:T(8,128)(2,1)}, u32[]{:S(2)}) copy-start(bf16[1,512,768]{2,1,0:T(8,128)(2,1)} %param.14) | copy-start | bytes 2359300
  14.3 17.8 %collective-permute-start.1 = (bf16[1,192,1152]{2,1,0:T(8,128)(2,1)S(1)}, bf16[1,192,1152]{2,1,0:T(8,128)(2,1)}, u32[]{:S(2)}, u32[]{:S(2)}) collective-permute-start(bf16[1,192,1152]{2,1,0:T(8,128)(2,1)S(1)} %pad_maximum_fusion.16), channel_id=1, source_target_pairs={{0,1},{1,0},{2,3},{3,2},{4,5},{5,4},{6,7},{7,6},{8,9},{9,8},{10,11... | collective-permute-start | bytes 1327112 | tf_op jit(solution)/shard_map/ppermute | solution.py:598
  16.1 20.2 %collective-permute-start.2 = (bf16[48,2048]{1,0:T(8,128)(2,1)}, bf16[48,2048]{1,0:T(8,128)(2,1)S(1)}, u32[]{:S(2)}, u32[]{:S(2)}) collective-permute-start(bf16[48,2048]{1,0:T(8,128)(2,1)} %pad_maximum_fusion.21), channel_id=1, source_target_pairs={{0,1},{1,0},{2,3},{3,2},{4,5},{5,4},{6,7},{7,6},{8,9},{9,8},{10,11... | collective-permute-start | bytes 589832 | tf_op jit(solution)/shard_map/ppermute | solution.py:598
  19.6 17.8 %collective-permute-start.3 = (bf16[64,768]{1,0:T(8,128)(2,1)}, bf16[64,768]{1,0:T(8,128)(2,1)S(1)}, u32[]{:S(2)}, u32[]{:S(2)}) collective-permute-start(bf16[64,768]{1,0:T(8,128)(2,1)} %dynamic-slice_bitcast_fusion.7), channel_id=1, source_target_pairs={{0,1},{1,0},{2,3},{3,2},{4,5},{5,4},{6,7},{7,6},{8,9},{9,8},{10,11... | collective-permute-start | bytes 294920 | tf_op jit(solution)/shard_map/ppermute | solution.py:598
  31.1 43.8 %copy-start.13 = (bf16[768,768]{1,0:T(8,128)(2,1)}, bf16[768,768]{1,0:T(8,128)(2,1)S(1)}, u32[]{:S(2)}) copy-start(bf16[768,768]{1,0:T(8,128)(2,1)S(1)} %fusion.2.refs_0_) | copy-start | bytes 3538948
  41.4 11.4 %collective-permute-start.4 = (bf16[1,192,1152]{2,1,0:T(8,128)(2,1)}, bf16[1,192,1152]{2,1,0:T(8,128)(2,1)}, u32[]{:S(2)}, u32[]{:S(2)}) collective-permute-start(bf16[1,192,1152]{2,1,0:T(8,128)(2,1)} %collective-permute-done.1), channel_id=1, source_target_pairs={{0,4},{2,6},{4,0},{6,2},{8,12},{10,14},{12,8},{14,10},{16,20},{18,... | collective-permute-start | bytes 1327112 | tf_op jit(solution)/shard_map/ppermute | solution.py:601
  42.9 20.1 %collective-permute-start.6 = (bf16[1,192,1920]{2,1,0:T(8,128)(2,1)}, bf16[1,192,1920]{2,1,0:T(8,128)(2,1)}, u32[]{:S(2)}, u32[]{:S(2)}) collective-permute-start(bf16[1,192,1920]{2,1,0:T(8,128)(2,1)} %bitcast_dynamic-update-slice_fusion), channel_id=1, source_target_pairs={{0,1},{1,0},{2,3},{3,2},{4,5},{5,4},{6,7},{7,6},{8,9},{9,8},{10,11... | collective-permute-start | bytes 2211848 | tf_op jit(solution)/shard_map/ppermute | solution.py:598
  47.2 98.4 %all-gather.3.cloned.1.call-start = ((), (), s32[]{:S(2)}) async-start(), calls=%async_computation | async-start | bytes 3342336 | tf_op jit(solution)/shard_map/all_gather | solution.py:861
  53.9 17.2 %collective-permute-start.5 = (bf16[2,192,1152]{2,1,0:T(8,128)(2,1)S(1)}, bf16[2,192,1152]{2,1,0:T(8,128)(2,1)S(1)}, u32[]{:S(2)}, u32[]{:S(2)}) collective-permute-start(bf16[2,192,1152]{2,1,0:T(8,128)(2,1)S(1)} %constant_dynamic-update-slice_fusion.mine_ref), channel_id=1, source_target_pairs={{0,2},{2,0},{4,6},{6,4},{8,10},{10,8},{12,14},{14,12},{16,18},{18,... | collective-permute-start | bytes 2654216 | tf_op jit(solution)/shard_map/ppermute | solution.py:601
  54.0 40.7 %collective-permute-start.9 = (bf16[1024,768]{1,0:T(8,128)(2,1)}, bf16[1024,768]{1,0:T(8,128)(2,1)}, u32[]{:S(2)}, u32[]{:S(2)}) collective-permute-start(bf16[1024,768]{1,0:T(8,128)(2,1)} %bitcast.24.refs_0_), channel_id=1, source_target_pairs={{0,1},{1,0},{2,3},{3,2},{4,5},{5,4},{6,7},{7,6},{8,9},{9,8},{10,11... | collective-permute-start | bytes 4718600 | tf_op jit(solution)/shard_map/ppermute | solution.py:598
  63.0 18.8 %collective-permute-start.7 = (bf16[1,192,1920]{2,1,0:T(8,128)(2,1)}, bf16[1,192,1920]{2,1,0:T(8,128)(2,1)S(1)}, u32[]{:S(2)}, u32[]{:S(2)}) collective-permute-start(bf16[1,192,1920]{2,1,0:T(8,128)(2,1)} %collective-permute-done.6), channel_id=1, source_target_pairs={{0,4},{2,6},{4,0},{6,2},{8,12},{10,14},{12,8},{14,10},{16,20},{18,... | collective-permute-start | bytes 2211848 | tf_op jit(solution)/shard_map/ppermute | solution.py:601
  79.5 15.7 %copy-start.17 = (bf16[512,384]{1,0:T(8,128)(2,1)}, bf16[512,384]{1,0:T(8,128)(2,1)S(1)}, u32[]{:S(2)}) copy-start(bf16[512,384]{1,0:T(8,128)(2,1)S(1)} %get-tuple-element.180.refs_0_.out_ref) | copy-start | bytes 1179652
  81.9 3.5 collective-permute-start.8
  87.6 48.2 %copy-start.65 = (bf16[2,192,768]{2,1,0:T(8,128)(2,1)}, bf16[2,192,768]{2,1,0:T(8,128)(2,1)S(1)}, u32[]{:S(2)}) copy-start(bf16[2,192,768]{2,1,0:T(8,128)(2,1)S(1)} %get-tuple-element.177) | copy-start | bytes 1769476
  97.7 38.1 %copy-start.8 = (f32[512,768]{1,0:T(8,128)}, f32[512,768]{1,0:T(8,128)S(1)}, u32[]{:S(2)}) copy-start(f32[512,768]{1,0:T(8,128)S(1)} %get-tuple-element.300.refs_4_) | copy-start | bytes 4718596
  100.4 24.9 %copy-start.77 = (bf16[512,384]{1,0:T(8,128)(2,1)}, bf16[512,384]{1,0:T(8,128)(2,1)S(1)}, u32[]{:S(2)}) copy-start(bf16[512,384]{1,0:T(8,128)(2,1)S(1)} %convolution_convert_fusion.14.q_ref) | copy-start | bytes 1179652
  102.9 22.3 %copy-start.31 = (bf16[1024,384]{1,0:T(8,128)(2,1)}, bf16[1024,384]{1,0:T(8,128)(2,1)S(1)}, u32[]{:S(2)}) copy-start(bf16[1024,384]{1,0:T(8,128)(2,1)S(1)} %convolution_convert_fusion.5.refs_0_) | copy-start | bytes 2359300
  105.7 19.6 %copy-start.33 = (bf16[1024,384]{1,0:T(8,128)(2,1)}, bf16[1024,384]{1,0:T(8,128)(2,1)S(1)}, u32[]{:S(2)}) copy-start(bf16[1024,384]{1,0:T(8,128)(2,1)S(1)} %convolution_convert_fusion.4.refs_1_) | copy-start | bytes 2359300
  137.6 25.9 %copy-start.6 = (f32[512,768]{1,0:T(8,128)}, f32[512,768]{1,0:T(8,128)S(1)}, u32[]{:S(2)}) copy-start(f32[512,768]{1,0:T(8,128)S(1)} %get-tuple-element.298.refs_8_) | copy-start | bytes 4718596
  175.7 25.5 %collective-permute-start.10 = (bf16[16,48,1408]{2,1,0:T(8,128)(2,1)}, bf16[16,48,1408]{2,1,0:T(8,128)(2,1)}, u32[]{:S(2)}, u32[]{:S(2)}) collective-permute-start(bf16[16,48,1408]{2,1,0:T(8,128)(2,1)} %maximum_maximum_fusion.1), channel_id=1, source_target_pairs={{0,2},{2,0},{4,6},{6,4},{8,10},{10,8},{12,14},{14,12},{16,18},{18,... | collective-permute-start | bytes 6488072 | tf_op jit(solution)/shard_map/ppermute | solution.py:601
  175.7 27.8 %collective-permute-start.11 = (bf16[16,48,2048]{2,1,0:T(8,128)(2,1)}, bf16[16,48,2048]{2,1,0:T(8,128)(2,1)}, u32[]{:S(2)}, u32[]{:S(2)}) collective-permute-start(bf16[16,48,2048]{2,1,0:T(8,128)(2,1)} %pad_maximum_fusion), channel_id=1, source_target_pairs={{0,2},{2,0},{4,6},{6,4},{8,10},{10,8},{12,14},{14,12},{16,18},{18,... | collective-permute-start | bytes 9437192 | tf_op jit(solution)/shard_map/ppermute | solution.py:601
  203.5 26.6 %collective-permute-start.13 = (bf16[8,48,1408]{2,1,0:T(8,128)(2,1)S(1)}, bf16[8,48,1408]{2,1,0:T(8,128)(2,1)S(1)}, u32[]{:S(2)}, u32[]{:S(2)}) collective-permute-start(bf16[8,48,1408]{2,1,0:T(8,128)(2,1)S(1)} %pad_maximum_fusion.5), channel_id=1, source_target_pairs={{0,4},{2,6},{4,0},{6,2},{8,12},{10,14},{12,8},{14,10},{16,20},{18,... | collective-permute-start | bytes 3244040 | tf_op jit(solution)/shard_map/ppermute | solution.py:601
  207.1 35.5 %collective-permute-start.12 = (bf16[8,48,2048]{2,1,0:T(8,128)(2,1)S(1)}, bf16[8,48,2048]{2,1,0:T(8,128)(2,1)S(1)}, u32[]{:S(2)}, u32[]{:S(2)}) collective-permute-start(bf16[8,48,2048]{2,1,0:T(8,128)(2,1)S(1)} %add_convert_fusion), channel_id=1, source_target_pairs={{0,1},{1,0},{2,3},{3,2},{4,5},{5,4},{6,7},{7,6},{8,9},{9,8},{10,11... | collective-permute-start | bytes 4718600 | tf_op jit(solution)/shard_map/ppermute | solution.py:598
  213.4 29.6 %copy-start.88 = (bf16[1,2,2,192,384]{4,3,2,1,0:T(8,128)(2,1)S(1)}, bf16[1,2,2,192,384]{4,3,2,1,0:T(8,128)(2,1)}, u32[]{:S(2)}) copy-start(bf16[1,2,2,192,384]{4,3,2,1,0:T(8,128)(2,1)} %copy-done.87) | copy-start | bytes 1769476
  227.3 26.5 %copy-start = (bf16[2048,768]{1,0:T(8,128)(2,1)}, bf16[2048,768]{1,0:T(8,128)(2,1)S(1)}, u32[]{:S(2)}) copy-start(bf16[2048,768]{1,0:T(8,128)(2,1)S(1)} %get-tuple-element.264.refs_2_.refs_3_) | copy-start | bytes 9437188
  267.7 39.9 %collective-permute-start.18 = (bf16[16,48,1536]{2,1,0:T(8,128)(2,1)S(1)}, bf16[16,48,1536]{2,1,0:T(8,128)(2,1)S(1)}, u32[]{:S(2)}, u32[]{:S(2)}) collective-permute-start(bf16[16,48,1536]{2,1,0:T(8,128)(2,1)S(1)} %maximum_maximum_fusion), channel_id=1, source_target_pairs={{0,2},{2,0},{4,6},{6,4},{8,10},{10,8},{12,14},{14,12},{16,18},{18,... | collective-permute-start | bytes 7077896 | tf_op jit(solution)/shard_map/ppermute | solution.py:601
  270.3 15.1 %collective-permute-start.14 = (bf16[4,48,1408]{2,1,0:T(8,128)(2,1)S(1)}, bf16[4,48,1408]{2,1,0:T(8,128)(2,1)S(1)}, u32[]{:S(2)}, u32[]{:S(2)}) collective-permute-start(bf16[4,48,1408]{2,1,0:T(8,128)(2,1)S(1)} %add_convert_fusion.6), channel_id=1, source_target_pairs={{0,1},{1,0},{2,3},{3,2},{4,5},{5,4},{6,7},{7,6},{8,9},{9,8},{10,11... | collective-permute-start | bytes 1622024 | tf_op jit(solution)/shard_map/ppermute | solution.py:598
  270.7 19.7 %collective-permute-start.15 = (bf16[4,48,2048]{2,1,0:T(8,128)(2,1)S(1)}, bf16[4,48,2048]{2,1,0:T(8,128)(2,1)S(1)}, u32[]{:S(2)}, u32[]{:S(2)}) collective-permute-start(bf16[4,48,2048]{2,1,0:T(8,128)(2,1)S(1)} %add_convert_fusion.2), channel_id=1, source_target_pairs={{0,4},{2,6},{4,0},{6,2},{8,12},{10,14},{12,8},{14,10},{16,20},{18,... | collective-permute-start | bytes 2359304 | tf_op jit(solution)/shard_map/ppermute | solution.py:601
  270.9 107.1 %collective-permute-start.27 = (bf16[1024,768]{1,0:T(8,128)(2,1)}, bf16[1024,768]{1,0:T(8,128)(2,1)}, u32[]{:S(2)}, u32[]{:S(2)}) collective-permute-start(bf16[1024,768]{1,0:T(8,128)(2,1)} %back.3), channel_id=1, source_target_pairs={{0,1},{1,0},{2,3},{3,2},{4,5},{5,4},{6,7},{7,6},{8,9},{9,8},{10,11... | collective-permute-start | bytes 4718600 | tf_op jit(solution)/shard_map/ppermute | solution.py:598
  290.6 10.5 %collective-permute-start.16 = (bf16[2,48,1408]{2,1,0:T(8,128)(2,1)S(1)}, bf16[2,48,1408]{2,1,0:T(8,128)(2,1)S(1)}, u32[]{:S(2)}, u32[]{:S(2)}) collective-permute-start(bf16[2,48,1408]{2,1,0:T(8,128)(2,1)S(1)} %add_convert_fusion.12), channel_id=1, source_target_pairs={{0,8},{2,10},{4,12},{6,14},{8,0},{10,2},{12,4},{14,6},{16,24},{18,... | collective-permute-start | bytes 811016 | tf_op jit(solution)/shard_map/ppermute | solution.py:601
  293.6 13.9 %collective-permute-start.17 = (bf16[2,48,2048]{2,1,0:T(8,128)(2,1)S(1)}, bf16[2,48,2048]{2,1,0:T(8,128)(2,1)S(1)}, u32[]{:S(2)}, u32[]{:S(2)}) collective-permute-start(bf16[2,48,2048]{2,1,0:T(8,128)(2,1)S(1)} %add_convert_fusion.10), channel_id=1, source_target_pairs={{0,8},{2,10},{4,12},{6,14},{8,0},{10,2},{12,4},{14,6},{16,24},{18,... | collective-permute-start | bytes 1179656 | tf_op jit(solution)/shard_map/ppermute | solution.py:601
  310.5 13.5 %collective-permute-start.19 = (bf16[1,48,1408]{2,1,0:T(8,128)(2,1)S(1)}, bf16[1,48,1408]{2,1,0:T(8,128)(2,1)S(1)}, u32[]{:S(2)}, u32[]{:S(2)}) collective-permute-start(bf16[1,48,1408]{2,1,0:T(8,128)(2,1)S(1)} %add_convert_fusion.19), channel_id=1, source_target_pairs={{0,16},{2,18},{4,20},{6,22},{8,24},{10,26},{12,28},{14,30},{16,0},... | collective-permute-start | bytes 405512 | tf_op jit(solution)/shard_map/ppermute | solution.py:601
  314.1 13.1 %collective-permute-start.20 = (bf16[1,48,2048]{2,1,0:T(8,128)(2,1)S(1)}, bf16[1,48,2048]{2,1,0:T(8,128)(2,1)S(1)}, u32[]{:S(2)}, u32[]{:S(2)}) collective-permute-start(bf16[1,48,2048]{2,1,0:T(8,128)(2,1)S(1)} %add_convert_fusion.15), channel_id=1, source_target_pairs={{0,16},{2,18},{4,20},{6,22},{8,24},{10,26},{12,28},{14,30},{16,0},... | collective-permute-start | bytes 589832 | tf_op jit(solution)/shard_map/ppermute | solution.py:601
  315.3 40.5 %collective-permute-start.23 = (bf16[8,48,1536]{2,1,0:T(8,128)(2,1)}, bf16[8,48,1536]{2,1,0:T(8,128)(2,1)}, u32[]{:S(2)}, u32[]{:S(2)}) collective-permute-start(bf16[8,48,1536]{2,1,0:T(8,128)(2,1)} %pad_maximum_fusion.3), channel_id=1, source_target_pairs={{0,4},{2,6},{4,0},{6,2},{8,12},{10,14},{12,8},{14,10},{16,20},{18,... | collective-permute-start | bytes 3538952 | tf_op jit(solution)/shard_map/ppermute | solution.py:601
  327.4 27.4 %collective-permute-start.22 = (bf16[1,48,2048]{2,1,0:T(8,128)(2,1)S(1)}, bf16[1,48,2048]{2,1,0:T(8,128)(2,1)}, u32[]{:S(2)}, u32[]{:S(2)}) collective-permute-start(bf16[1,48,2048]{2,1,0:T(8,128)(2,1)S(1)} %add_convert_fusion.14), channel_id=1, source_target_pairs={{0,16},{2,18},{4,20},{6,22},{8,24},{10,26},{12,28},{14,30},{16,0},... | collective-permute-start | bytes 589832 | tf_op jit(solution)/shard_map/ppermute | solution.py:601
  327.5 26.2 %collective-permute-start.21 = (bf16[1,48,1408]{2,1,0:T(8,128)(2,1)S(1)}, bf16[1,48,1408]{2,1,0:T(8,128)(2,1)}, u32[]{:S(2)}, u32[]{:S(2)}) collective-permute-start(bf16[1,48,1408]{2,1,0:T(8,128)(2,1)S(1)} %add_convert_fusion.18), channel_id=1, source_target_pairs={{0,16},{2,18},{4,20},{6,22},{8,24},{10,26},{12,28},{14,30},{16,0},... | collective-permute-start | bytes 405512 | tf_op jit(solution)/shard_map/ppermute | solution.py:601
  353.4 24.4 %collective-permute-start.26 = (bf16[16,48,1280]{2,1,0:T(8,128)(2,1)S(1)}, bf16[16,48,1280]{2,1,0:T(8,128)(2,1)S(1)}, u32[]{:S(2)}, u32[]{:S(2)}) collective-permute-start(bf16[16,48,1280]{2,1,0:T(8,128)(2,1)S(1)} %maximum_maximum_fusion.2), channel_id=1, source_target_pairs={{0,2},{2,0},{4,6},{6,4},{8,10},{10,8},{12,14},{14,12},{16,18},{18,... | collective-permute-start | bytes 5898248 | tf_op jit(solution)/shard_map/ppermute | solution.py:601
  357.1 19.3 %collective-permute-start.25 = (bf16[2,48,2048]{2,1,0:T(8,128)(2,1)S(1)}, bf16[2,48,2048]{2,1,0:T(8,128)(2,1)S(1)}, u32[]{:S(2)}, u32[]{:S(2)}) collective-permute-start(bf16[2,48,2048]{2,1,0:T(8,128)(2,1)S(1)} %pad_maximum_fusion.17), channel_id=1, source_target_pairs={{0,8},{2,10},{4,12},{6,14},{8,0},{10,2},{12,4},{14,6},{16,24},{18,... | collective-permute-start | bytes 1179656 | tf_op jit(solution)/shard_map/ppermute | solution.py:601
  357.2 17.0 %collective-permute-start.24 = (bf16[2,48,1408]{2,1,0:T(8,128)(2,1)S(1)}, bf16[2,48,1408]{2,1,0:T(8,128)(2,1)S(1)}, u32[]{:S(2)}, u32[]{:S(2)}) collective-permute-start(bf16[2,48,1408]{2,1,0:T(8,128)(2,1)S(1)} %pad_maximum_fusion.19), channel_id=1, source_target_pairs={{0,8},{2,10},{4,12},{6,14},{8,0},{10,2},{12,4},{14,6},{16,24},{18,... | collective-permute-start | bytes 811016 | tf_op jit(solution)/shard_map/ppermute | solution.py:601
  359.9 17.7 %collective-permute-start.30 = (bf16[4,48,1536]{2,1,0:T(8,128)(2,1)S(1)}, bf16[4,48,1536]{2,1,0:T(8,128)(2,1)S(1)}, u32[]{:S(2)}, u32[]{:S(2)}) collective-permute-start(bf16[4,48,1536]{2,1,0:T(8,128)(2,1)S(1)} %add_convert_fusion.3), channel_id=1, source_target_pairs={{0,1},{1,0},{2,3},{3,2},{4,5},{5,4},{6,7},{7,6},{8,9},{9,8},{10,11... | collective-permute-start | bytes 1769480 | tf_op jit(solution)/shard_map/ppermute | solution.py:598
  361.9 15.6 %copy-start.115 = (bf16[8,48,1536]{2,1,0:T(8,128)(2,1)S(1)}, bf16[8,48,1536]{2,1,0:T(8,128)(2,1)}, u32[]{:S(2)}) copy-start(bf16[8,48,1536]{2,1,0:T(8,128)(2,1)} %copy-done.114) | copy-start | bytes 3538948
  374.2 15.8 %collective-permute-start.28 = (bf16[256,768]{1,0:T(8,128)(2,1)S(1)}, bf16[256,768]{1,0:T(8,128)(2,1)S(1)}, u32[]{:S(2)}, u32[]{:S(2)}) collective-permute-start(bf16[256,768]{1,0:T(8,128)(2,1)S(1)} %copy-done.136), channel_id=1, source_target_pairs={{1,0},{3,2},{5,4},{7,6},{9,8},{11,10},{13,12},{15,14},{17,16},{19,... | collective-permute-start | bytes 1179656 | tf_op jit(solution)/shard_map/ppermute | solution.py:1022
  378.1 31.5 %collective-permute-start.29 = (bf16[8,48,1280]{2,1,0:T(8,128)(2,1)S(1)}, bf16[8,48,1280]{2,1,0:T(8,128)(2,1)S(1)}, u32[]{:S(2)}, u32[]{:S(2)}) collective-permute-start(bf16[8,48,1280]{2,1,0:T(8,128)(2,1)S(1)} %add_convert_fusion.1), channel_id=1, source_target_pairs={{0,1},{1,0},{2,3},{3,2},{4,5},{5,4},{6,7},{7,6},{8,9},{9,8},{10,11... | collective-permute-start | bytes 2949128 | tf_op jit(solution)/shard_map/ppermute | solution.py:598
  387.9 20.5 %collective-permute-start.34 = (bf16[4,48,2048]{2,1,0:T(8,128)(2,1)S(1)}, bf16[4,48,2048]{2,1,0:T(8,128)(2,1)S(1)}, u32[]{:S(2)}, u32[]{:S(2)}) collective-permute-start(bf16[4,48,2048]{2,1,0:T(8,128)(2,1)S(1)} %pad_maximum_fusion.8), channel_id=1, source_target_pairs={{0,4},{2,6},{4,0},{6,2},{8,12},{10,14},{12,8},{14,10},{16,20},{18,... | collective-permute-start | bytes 2359304 | tf_op jit(solution)/shard_map/ppermute | solution.py:601
  388.3 31.7 %collective-permute-start.33 = (bf16[4,48,1408]{2,1,0:T(8,128)(2,1)S(1)}, bf16[4,48,1408]{2,1,0:T(8,128)(2,1)S(1)}, u32[]{:S(2)}, u32[]{:S(2)}) collective-permute-start(bf16[4,48,1408]{2,1,0:T(8,128)(2,1)S(1)} %pad_maximum_fusion.14), channel_id=1, source_target_pairs={{0,4},{2,6},{4,0},{6,2},{8,12},{10,14},{12,8},{14,10},{16,20},{18,... | collective-permute-start | bytes 1622024 | tf_op jit(solution)/shard_map/ppermute | solution.py:601
  393.2 43.5 %copy-start.118 = (bf16[8,48,1280]{2,1,0:T(8,128)(2,1)}, bf16[8,48,1280]{2,1,0:T(8,128)(2,1)S(1)}, u32[]{:S(2)}) copy-start(bf16[8,48,1280]{2,1,0:T(8,128)(2,1)S(1)} %slice.218) | copy-start | bytes 2949124
  409.5 27.2 %copy-start.129 = (bf16[8,48,1280]{2,1,0:T(8,128)(2,1)}, bf16[8,48,1280]{2,1,0:T(8,128)(2,1)S(1)}, u32[]{:S(2)}) copy-start(bf16[8,48,1280]{2,1,0:T(8,128)(2,1)S(1)} %collective-permute-done.29) | copy-start | bytes 2949124
  409.8 21.9 %collective-permute-start.37 = (bf16[8,48,2048]{2,1,0:T(8,128)(2,1)S(1)}, bf16[8,48,2048]{2,1,0:T(8,128)(2,1)S(1)}, u32[]{:S(2)}, u32[]{:S(2)}) collective-permute-start(bf16[8,48,2048]{2,1,0:T(8,128)(2,1)S(1)} %pad_maximum_fusion.1.mine_ref), channel_id=1, source_target_pairs={{0,2},{2,0},{4,6},{6,4},{8,10},{10,8},{12,14},{14,12},{16,18},{18,... | collective-permute-start | bytes 4718600 | tf_op jit(solution)/shard_map/ppermute | solution.py:601
  410.5 10.7 %collective-permute-start.32 = (bf16[2,48,1536]{2,1,0:T(8,128)(2,1)S(1)}, bf16[2,48,1536]{2,1,0:T(8,128)(2,1)S(1)}, u32[]{:S(2)}, u32[]{:S(2)}) collective-permute-start(bf16[2,48,1536]{2,1,0:T(8,128)(2,1)S(1)} %add_convert_fusion.11), channel_id=1, source_target_pairs={{0,8},{2,10},{4,12},{6,14},{8,0},{10,2},{12,4},{14,6},{16,24},{18,... | collective-permute-start | bytes 884744 | tf_op jit(solution)/shard_map/ppermute | solution.py:601
  410.9 17.4 %collective-permute-start.31 = (bf16[4,48,1280]{2,1,0:T(8,128)(2,1)S(1)}, bf16[4,48,1280]{2,1,0:T(8,128)(2,1)S(1)}, u32[]{:S(2)}, u32[]{:S(2)}) collective-permute-start(bf16[4,48,1280]{2,1,0:T(8,128)(2,1)S(1)} %add_convert_fusion.9), channel_id=1, source_target_pairs={{0,4},{2,6},{4,0},{6,2},{8,12},{10,14},{12,8},{14,10},{16,20},{18,... | collective-permute-start | bytes 1474568 | tf_op jit(solution)/shard_map/ppermute | solution.py:601
  421.1 16.4 %collective-permute-start.40 = (bf16[8,48,1408]{2,1,0:T(8,128)(2,1)S(1)}, bf16[8,48,1408]{2,1,0:T(8,128)(2,1)S(1)}, u32[]{:S(2)}, u32[]{:S(2)}) collective-permute-start(bf16[8,48,1408]{2,1,0:T(8,128)(2,1)S(1)} %pad_maximum_fusion.6.mine_ref), channel_id=1, source_target_pairs={{0,2},{2,0},{4,6},{6,4},{8,10},{10,8},{12,14},{14,12},{16,18},{18,... | collective-permute-start | bytes 3244040 | tf_op jit(solution)/shard_map/ppermute | solution.py:601
  421.3 10.2 %collective-permute-start.36 = (bf16[1,48,1536]{2,1,0:T(8,128)(2,1)S(1)}, bf16[1,48,1536]{2,1,0:T(8,128)(2,1)S(1)}, u32[]{:S(2)}, u32[]{:S(2)}) collective-permute-start(bf16[1,48,1536]{2,1,0:T(8,128)(2,1)S(1)} %add_convert_fusion.17), channel_id=1, source_target_pairs={{0,16},{2,18},{4,20},{6,22},{8,24},{10,26},{12,28},{14,30},{16,0},... | collective-permute-start | bytes 442376 | tf_op jit(solution)/shard_map/ppermute | solution.py:601
  428.4 8.3 %collective-permute-start.35 = (bf16[2,48,1280]{2,1,0:T(8,128)(2,1)S(1)}, bf16[2,48,1280]{2,1,0:T(8,128)(2,1)S(1)}, u32[]{:S(2)}, u32[]{:S(2)}) collective-permute-start(bf16[2,48,1280]{2,1,0:T(8,128)(2,1)S(1)} %add_convert_fusion.13), channel_id=1, source_target_pairs={{0,8},{2,10},{4,12},{6,14},{8,0},{10,2},{12,4},{14,6},{16,24},{18,... | collective-permute-start | bytes 737288 | tf_op jit(solution)/shard_map/ppermute | solution.py:601
  436.2 9.6 %collective-permute-start.39 = (bf16[1,48,1536]{2,1,0:T(8,128)(2,1)S(1)}, bf16[1,48,1536]{2,1,0:T(8,128)(2,1)S(1)}, u32[]{:S(2)}, u32[]{:S(2)}) collective-permute-start(bf16[1,48,1536]{2,1,0:T(8,128)(2,1)S(1)} %add_convert_fusion.16), channel_id=1, source_target_pairs={{0,16},{2,18},{4,20},{6,22},{8,24},{10,26},{12,28},{14,30},{16,0},... | collective-permute-start | bytes 442376 | tf_op jit(solution)/shard_map/ppermute | solution.py:601
  443.3 8.7 %collective-permute-start.38 = (bf16[1,48,1280]{2,1,0:T(8,128)(2,1)}, bf16[1,48,1280]{2,1,0:T(8,128)(2,1)S(1)}, u32[]{:S(2)}, u32[]{:S(2)}) collective-permute-start(bf16[1,48,1280]{2,1,0:T(8,128)(2,1)} %add_convert_fusion.21), channel_id=1, source_target_pairs={{0,16},{2,18},{4,20},{6,22},{8,24},{10,26},{12,28},{14,30},{16,0},... | collective-permute-start | bytes 368648 | tf_op jit(solution)/shard_map/ppermute | solution.py:601
  445.9 9.8 %collective-permute-start.42 = (bf16[2,48,1536]{2,1,0:T(8,128)(2,1)S(1)}, bf16[2,48,1536]{2,1,0:T(8,128)(2,1)S(1)}, u32[]{:S(2)}, u32[]{:S(2)}) collective-permute-start(bf16[2,48,1536]{2,1,0:T(8,128)(2,1)S(1)} %pad_maximum_fusion.18), channel_id=1, source_target_pairs={{0,8},{2,10},{4,12},{6,14},{8,0},{10,2},{12,4},{14,6},{16,24},{18,... | collective-permute-start | bytes 884744 | tf_op jit(solution)/shard_map/ppermute | solution.py:601
  455.7 13.9 %collective-permute-start.44 = (bf16[4,48,1536]{2,1,0:T(8,128)(2,1)S(1)}, bf16[4,48,1536]{2,1,0:T(8,128)(2,1)S(1)}, u32[]{:S(2)}, u32[]{:S(2)}) collective-permute-start(bf16[4,48,1536]{2,1,0:T(8,128)(2,1)S(1)} %pad_maximum_fusion.13), channel_id=1, source_target_pairs={{0,4},{2,6},{4,0},{6,2},{8,12},{10,14},{12,8},{14,10},{16,20},{18,... | collective-permute-start | bytes 1769480 | tf_op jit(solution)/shard_map/ppermute | solution.py:601
  456.2 7.3 %collective-permute-start.41 = (bf16[1,48,1280]{2,1,0:T(8,128)(2,1)S(1)}, bf16[1,48,1280]{2,1,0:T(8,128)(2,1)S(1)}, u32[]{:S(2)}, u32[]{:S(2)}) collective-permute-start(bf16[1,48,1280]{2,1,0:T(8,128)(2,1)S(1)} %add_convert_fusion.20), channel_id=1, source_target_pairs={{0,16},{2,18},{4,20},{6,22},{8,24},{10,26},{12,28},{14,30},{16,0},... | collective-permute-start | bytes 368648 | tf_op jit(solution)/shard_map/ppermute | solution.py:601
  463.5 6.3 %collective-permute-start.43 = (bf16[2,48,1280]{2,1,0:T(8,128)(2,1)S(1)}, bf16[2,48,1280]{2,1,0:T(8,128)(2,1)S(1)}, u32[]{:S(2)}, u32[]{:S(2)}) collective-permute-start(bf16[2,48,1280]{2,1,0:T(8,128)(2,1)S(1)} %pad_maximum_fusion.20), channel_id=1, source_target_pairs={{0,8},{2,10},{4,12},{6,14},{8,0},{10,2},{12,4},{14,6},{16,24},{18,... | collective-permute-start | bytes 737288 | tf_op jit(solution)/shard_map/ppermute | solution.py:601
  469.8 13.9 %collective-permute-start.46 = (bf16[8,48,1536]{2,1,0:T(8,128)(2,1)S(1)}, bf16[8,48,1536]{2,1,0:T(8,128)(2,1)S(1)}, u32[]{:S(2)}, u32[]{:S(2)}) collective-permute-start(bf16[8,48,1536]{2,1,0:T(8,128)(2,1)S(1)} %pad_maximum_fusion.4.mine_ref), channel_id=1, source_target_pairs={{0,2},{2,0},{4,6},{6,4},{8,10},{10,8},{12,14},{14,12},{16,18},{18,... | collective-permute-start | bytes 3538952 | tf_op jit(solution)/shard_map/ppermute | solution.py:601
  469.9 13.7 %collective-permute-start.45 = (bf16[4,48,1280]{2,1,0:T(8,128)(2,1)S(1)}, bf16[4,48,1280]{2,1,0:T(8,128)(2,1)S(1)}, u32[]{:S(2)}, u32[]{:S(2)}) collective-permute-start(bf16[4,48,1280]{2,1,0:T(8,128)(2,1)S(1)} %pad_maximum_fusion.15), channel_id=1, source_target_pairs={{0,4},{2,6},{4,0},{6,2},{8,12},{10,14},{12,8},{14,10},{16,20},{18,... | collective-permute-start | bytes 1474568 | tf_op jit(solution)/shard_map/ppermute | solution.py:601
  487.8 2.6 collective-permute-start.47
  (153 other events, 845.0 us)
Sparse Core Ops, SparseCore 0:
  47.3 40.1 all-gather.4
  90.4 44.1 all-gather.2

commit v4 on v3

--- a/solution.py
+++ b/solution.py
@@ -1072,7 +1072,7 @@
     agenda_steps = (
         send_halo, send_project, send_ffn, plan, norm_a, P_, gather_ffn, send_rest, self0, P_, mem0, R, keys0, P_,
         self1, R, R, take_memory, queries, keys1, cross0, cross1, ffn, gate_dw, down_dw, norm_m_grad, A, norm_m_back,
-        outs_dw, cross_b0, B, cross_b1, A, norm_c_back, mem_b0, part0, B, mem_dw0, mem_dw1, cross_dw, A, B, self_b1,
+        outs_dw, cross_b0, B, cross_b1, A, norm_c_back, B, mem_b0, part0, mem_dw0, mem_dw1, cross_dw, A, B, self_b1,
         E, A, B, self_b0, A, B, norm_a_grad, self_dw, E, A, B, take_partial, D, mem_b1, A, B, norm_a_back, E, D, A, B,
         E, D, A, E, D, B, E, D, E, D, E, D, E, D, D,
     )

time: 511 us -> 513 us (level)
  waiting for transfers between devices: 144 us -> 136 us
  starting transfers between devices: 43.4 us -> 50.2 us
    ppermute x36, waiting for transfers between devices: 102 us -> 94.3 us  [across(): return lax.ppermute(x, 'dp', [(i, i ^ mask) for i in range(self.n_dp)])]
    ppermute x36, starting transfers between devices: 24.4 us -> 30.8 us  [across(): return lax.ppermute(x, 'dp', [(i, i ^ mask) for i in range(self.n_dp)])]
  transfers between devices with their start and end apart: 50 -> 50, of which waited for: 26 -> 25; matrix products, arithmetic and copies ran while one was open for 21% -> 20% of each run, Pallas kernels for 20% -> 21%
where the time goes in v4:
time: 513 us; the launch traced here: 508 us
  Pallas kernels  161 us (31%)
  waiting for transfers between devices  136 us (27%)
  local copies, waits for them, and re-layouts  70.6 us (14%)
  starting transfers between devices  50.2 us (10%)
  matrix products  40.1 us (8%)
  other arithmetic  32.6 us (6%)
  between operations  17.4 us (3%)
    ppermute x36, waiting for transfers between devices, across(): return lax.ppermute(x, 'dp', [(i, i ^ mask) for i in range(self.n_dp)])  94.3 us
    pallas_call x4, Pallas kernels, attend_backward(): pl.pallas_call(functools.partial(backward_kernel, first_part=first_part,...  43.5 us
    ppermute x10, waiting for transfers between devices, across_tp(): return lax.ppermute(x, 'tp', [(0, 1), (1, 0)])  41.4 us
    dot_general x22, matrix products, contract(): lax.dot_general(a, b, (((i,), (j,)), ((), ())), preferred_element_type=F32)  40.1 us
    unnamed x339, local copies, waits for them, and re-layouts  35.5 us
    ppermute x36, starting transfers between devices, across(): return lax.ppermute(x, 'dp', [(i, i ^ mask) for i in range(self.n_dp)])  30.8 us
    pallas_call x4, Pallas kernels, attend_forward(): pl.pallas_call(functools.partial(forward_kernel, first_part=first_part, n...  28 us
    pallas_call x9, Pallas kernels, weight_grads(): pl.pallas_call(functools.partial(weight_kernel, n=len(rows), m=len(grads)...  26.4 us
  transfers between devices with their start and end apart: 50, of which 25 were waited for; matrix products, arithmetic and copies ran while one was open for 20% of the time, Pallas kernels for 21%

profile of v4, /device:TPU:0, one launch (start us, length us, event | category | flops | bytes accessed | tf_op | source)
XLA Modules:
  0.0 508.1 jit_solution(16110024865592689908)
XLA Ops:
  8.3 4.9 collective-permute-start
  32.1 4.2 collective-permute-done.2
  42.9 2.4 collective-permute-start.6
  47.5 4.4 attend_forward.4
  56.4 6.6 %collective-permute-done.6 = bf16[1,192,1920]{2,1,0:T(8,128)(2,1)} collective-permute-done((bf16[1,192,1920]{2,1,0:T(8,128)(2,1)}, bf16[1,192,1920]{2,1,0:T(8,128)(2,1)}, u32[]{:S(2)}, u32[]{:S(2)}) %collective-permute-start.6) | collective-permute-done | bytes 737312 | tf_op jit(solution)/shard_map/ppermute | solution.py:598
  64.5 3.3 convolution_convert_fusion.7.refs_0_
  67.8 3.3 convolution_convert_fusion.6.refs_1_
  75.7 4.4 attend_forward.5
  82.6 2.8 collective-permute-done.8.theirs_ref
  87.6 7.0 %collective-permute-done.9.refs_1_ = bf16[1024,768]{1,0:T(8,128)(2,1)} collective-permute-done((bf16[1024,768]{1,0:T(8,128)(2,1)}, bf16[1024,768]{1,0:T(8,128)(2,1)}, u32[]{:S(2)}, u32[]{:S(2)}) %collective-permute-start.9) | collective-permute-done | bytes 1572896 | tf_op jit(solution)/shard_map/ppermute | solution.py:598
  95.3 2.4 multiply_reduce_fusion.5
  100.5 2.4 convolution_convert_fusion.5.refs_0_
  103.0 2.7 convolution_convert_fusion.4.refs_1_
  105.7 2.7 convolution_convert_fusion.3.refs_2_
  108.4 2.7 convolution_convert_fusion.2.refs_3_
  111.1 9.4 %attend_forward.6 = (bf16[512,384]{1,0:T(8,128)(2,1)S(1)}, f32[4,3,256]{2,1,0:T(4,128)S(1)}) custom-call(s32[6,4,128]{2,1,0:T(4,128)S(1)} %copy-done.84, bf16[512,384]{1,0:T(8,128)(2,1)S(1)} %convolution_convert_fusion.15.q_ref, bf16[1024,384]{1,0:T(8,128)(2,1)S(1)} %copy-done.27, bf16[1024,384]{1,0:T(8,128)(2,1)S(1)} %copy-done.29, ...), custom_call_target="tpu_custom_call" | custom-call | flops 1048576 | bytes 1048576 | tf_op jit(solution)/shard_map/attend_forward/pallas_call | solution.py:258
  120.6 2.5 convolution_convert_fusion.1.refs_2_
  123.1 2.7 convolution_convert_fusion.refs_3_
  125.9 9.8 %attend_forward.7 = (bf16[512,384]{1,0:T(8,128)(2,1)S(1)}, f32[4,3,256]{2,1,0:T(4,128)S(1)}) custom-call(s32[6,4,128]{2,1,0:T(4,128)S(1)} %copy-done.84, bf16[512,384]{1,0:T(8,128)(2,1)S(1)} %convolution_convert_fusion.14.q_ref, bf16[1024,384]{1,0:T(8,128)(2,1)S(1)} %convolution_convert_fusion.5.refs_0_, ...), custom_call_target="tpu_custom_call" | custom-call | flops 1048576 | bytes 1048576 | tf_op jit(solution)/shard_map/attend_forward/pallas_call | solution.py:258
  139.1 5.3 %feed_forward.2 = (bf16[512,1024]{1,0:T(8,128)(2,1)S(1)}, bf16[512,2048]{1,0:T(8,128)(2,1)S(1)}) custom-call(bf16[512,768]{1,0:T(8,128)(2,1)S(1)} %get-tuple-element.364.normed_ref.refs_0_, bf16[512,768]{1,0:T(8,128)(2,1)S(1)} %get-tuple-element.198.full_ref.refs_0_.refs_10_, bf16[2,768,1024]{2,1,0:T(8,128)(2,1)} %refs_5_.3, bf16[2,768,1024]{2,1,0:T(8,128)(2,1)} %refs_5_.3, ...), custom_call_target="tpu_custom_call" | custom-call | flops 1048576 | bytes 1048576 | tf_op jit(solution)/shard_map/feed_forward/pallas_call | solution.py:514
  146.7 5.3 %feed_forward.3 = (bf16[512,1024]{1,0:T(8,128)(2,1)S(1)}, bf16[512,2048]{1,0:T(8,128)(2,1)S(1)}) custom-call(bf16[512,768]{1,0:T(8,128)(2,1)S(1)} %get-tuple-element.364.normed_ref.refs_0_, bf16[512,768]{1,0:T(8,128)(2,1)S(1)} %get-tuple-element.198.full_ref.refs_0_.refs_10_, bf16[768,2048]{1,0:T(8,128)(2,1)} %all-gather.3.cloned.1.call-done.gate_ref.up_ref.refs_6_.refs_7_, ...), custom_call_target="tpu_custom_call" | custom-call | flops 1048576 | bytes 1048576 | tf_op jit(solution)/shard_map/feed_forward/pallas_call | solution.py:514
  152.1 5.0 weight_grads.9
  162.0 2.6 weight_grads.10
  164.7 7.5 %norm_back.2 = (f32[512,768]{1,0:T(8,128)S(1)}, bf16[512,768]{1,0:T(8,128)(2,1)S(1)}, f32[1,768]{1,0:T(1,128)S(1)}, bf16[512,384]{1,0:T(8,128)(2,1)S(1)}, bf16[512,384]{1,0:T(8,128)(2,1)S(1)}) custom-call(bf16[512,2048]{1,0:T(8,128)(2,1)S(1)} %copy-done.12, bf16[512,2048]{1,0:T(8,128)(2,1)S(1)} %copy-done.12, ...), custom_call_target="tpu_custom_call" | custom-call | flops 1048576 | bytes 1048576 | tf_op jit(solution)/shard_map/norm_back/pallas_call | solution.py:438
  186.9 14.9 %attend_backward.4 = (bf16[512,384]{1,0:T(8,128)(2,1)S(1)}, bf16[2048,768]{1,0:T(8,128)(2,1)S(1)}) custom-call(s32[6,4,128]{2,1,0:T(4,128)S(1)} %copy-done.84, f32[4,3,256]{2,1,0:T(4,128)S(1)} %copy-done.100, bf16[512,384]{1,0:T(8,128)(2,1)S(1)} %copy-done.80, bf16[512,384]{1,0:T(8,128)(2,1)S(1)} %copy-done.21, bf16[512,384]{1,0:T(8,128)(2,1)S(1)} %copy-done.92, ...), custom_call_target="tpu_custom_call" | custom-call | flops 1048576 | bytes 1048576 | tf_op jit(solution)/shard_map/attend_backward/pallas_call | solution.py:298
  212.9 2.4 multiply_reduce_fusion
  215.4 14.7 %attend_backward.5 = (bf16[512,384]{1,0:T(8,128)(2,1)S(1)}, bf16[2048,768]{1,0:T(8,128)(2,1)S(1)}) custom-call(s32[6,4,128]{2,1,0:T(4,128)S(1)} %copy-done.84, f32[4,3,256]{2,1,0:T(4,128)S(1)} %copy-done.98, bf16[512,384]{1,0:T(8,128)(2,1)S(1)} %copy-done.78, bf16[512,384]{1,0:T(8,128)(2,1)S(1)} %copy-done.24, bf16[512,384]{1,0:T(8,128)(2,1)S(1)} %copy-done.90, ...), custom_call_target="tpu_custom_call" | custom-call | flops 1048576 | bytes 1048576 | tf_op jit(solution)/shard_map/attend_backward/pallas_call | solution.py:298
  230.2 2.7 slice.205
  233.1 11.4 %collective-permute-done.12 = bf16[8,48,2048]{2,1,0:T(8,128)(2,1)S(1)} collective-permute-done((bf16[8,48,2048]{2,1,0:T(8,128)(2,1)S(1)}, bf16[8,48,2048]{2,1,0:T(8,128)(2,1)S(1)}, u32[]{:S(2)}, u32[]{:S(2)}) %collective-permute-start.12) | collective-permute-done | bytes 1572896 | tf_op jit(solution)/shard_map/ppermute | solution.py:598
  245.0 3.7 norm_back.3
  248.7 7.1 %back.3 = bf16[1024,768]{1,0:T(8,128)(2,1)} custom-call(bf16[2048,768]{1,0:T(8,128)(2,1)S(1)} %get-tuple-element.263.refs_0_.refs_1_.refs_2_, bf16[2048,768]{1,0:T(8,128)(2,1)S(1)} %get-tuple-element.263.refs_0_.refs_1_.refs_2_, bf16[2048,768]{1,0:T(8,128)(2,1)S(1)} %get-tuple-element.264.refs_2_.refs_3_, ...), custom_call_target="tpu_custom_call" | custom-call | flops 1048576 | bytes 1048576 | tf_op jit(solution)/shard_map/back/pallas_call | solution.py:421
  255.8 10.4 %weight_grads.13 = (bf16[768,768]{1,0:T(8,128)(2,1)S(1)}, bf16[768,768]{1,0:T(8,128)(2,1)S(1)}) custom-call(bf16[1024,768]{1,0:T(8,128)(2,1)} %bitcast.24.refs_0_, bf16[1024,768]{1,0:T(8,128)(2,1)} %collective-permute-done.9.refs_1_, bf16[2048,768]{1,0:T(8,128)(2,1)S(1)} %get-tuple-element.263.refs_0_.refs_1_.refs_2_, ...), custom_call_target="tpu_custom_call" | custom-call | flops 1048576 | bytes 1048576 | tf_op jit(solution)/shard_map/weight_grads/pallas_call | solution.py:478
  277.4 10.0 %collective-permute-done.14 = bf16[4,48,1408]{2,1,0:T(8,128)(2,1)S(1)} collective-permute-done((bf16[4,48,1408]{2,1,0:T(8,128)(2,1)S(1)}, bf16[4,48,1408]{2,1,0:T(8,128)(2,1)S(1)}, u32[]{:S(2)}, u32[]{:S(2)}) %collective-permute-start.14) | collective-permute-done | bytes 540704 | tf_op jit(solution)/shard_map/ppermute | solution.py:598
  287.6 4.7 collective-permute-done.15
  296.7 6.9 %attend_backward.6.refs_3_.refs_4_.refs_5_.refs_2_ = bf16[768,1152]{1,0:T(8,128)(2,1)S(1)} custom-call(s32[6,4,128]{2,1,0:T(4,128)S(1)} %copy-done.84, f32[4,3,256]{2,1,0:T(4,128)S(1)} %copy-done.96, bf16[768,384]{1,0:T(8,128)(2,1)S(1)} %copy-done.58, bf16[512,384]{1,0:T(8,128)(2,1)S(1)} %copy-done.18, bf16[512,384]{1,0:T(8,128)(2,1)S(1)} %get-tuple-element.242.grad_ref, ...), custom_call_target="tpu_custom_call" | custom-call | flops 1048576 | bytes 1048576 | tf_op jit(solution)/shard_map/attend_backward/pallas_call | solution.py:298
  303.7 5.3 %collective-permute-done.17 = bf16[2,48,2048]{2,1,0:T(8,128)(2,1)S(1)} collective-permute-done((bf16[2,48,2048]{2,1,0:T(8,128)(2,1)S(1)}, bf16[2,48,2048]{2,1,0:T(8,128)(2,1)S(1)}, u32[]{:S(2)}, u32[]{:S(2)}) %collective-permute-start.17) | collective-permute-done | bytes 393248 | tf_op jit(solution)/shard_map/ppermute | solution.py:601
  311.9 3.2 collective-permute-start.19
  319.0 7.0 %attend_backward.7.refs_0_.refs_1_.refs_2_ = bf16[768,1152]{1,0:T(8,128)(2,1)S(1)} custom-call(s32[6,4,128]{2,1,0:T(4,128)S(1)} %copy-done.84, f32[4,3,256]{2,1,0:T(4,128)S(1)} %copy-done.94, bf16[768,384]{1,0:T(8,128)(2,1)S(1)} %copy-done.52, bf16[512,384]{1,0:T(8,128)(2,1)S(1)} %get-tuple-element.179.refs_0_.out_ref, ...), custom_call_target="tpu_custom_call" | custom-call | flops 1048576 | bytes 1048576 | tf_op jit(solution)/shard_map/attend_backward/pallas_call | solution.py:298
  326.1 2.9 collective-permute-done.20
  329.3 2.9 collective-permute-start.21
  332.2 6.7 %back.4 = f32[768,768]{1,0:T(8,128)S(1)} custom-call(bf16[768,1152]{1,0:T(8,128)(2,1)S(1)} %attend_backward.7.refs_0_.refs_1_.refs_2_, bf16[768,1152]{1,0:T(8,128)(2,1)S(1)} %attend_backward.7.refs_0_.refs_1_.refs_2_, bf16[768,1152]{1,0:T(8,128)(2,1)S(1)} %attend_backward.7.refs_0_.refs_1_.refs_2_, ...), custom_call_target="tpu_custom_call" | custom-call | flops 1048576 | bytes 1048576 | tf_op jit(solution)/shard_map/back/pallas_call | solution.py:421
  341.1 5.3 %weight_grads.17 = (bf16[768,1152]{1,0:T(8,128)(2,1)S(1)}, bf16[768,1152]{1,0:T(8,128)(2,1)S(1)}) custom-call(bf16[768,768]{1,0:T(8,128)(2,1)S(1)} %copy-done.14, bf16[768,1152]{1,0:T(8,128)(2,1)S(1)} %attend_backward.7.refs_0_.refs_1_.refs_2_, bf16[768,1152]{1,0:T(8,128)(2,1)S(1)} %attend_backward.6.refs_3_.refs_4_.refs_5_.refs_2_), custom_call_target="tpu_custom_call" | custom-call | flops 1048576 | bytes 1048576 | tf_op jit(solution)/shard_map/weight_grads/pallas_call | solution.py:478
  364.3 11.7 %collective-permute-done.24 = bf16[2,48,1408]{2,1,0:T(8,128)(2,1)S(1)} collective-permute-done((bf16[2,48,1408]{2,1,0:T(8,128)(2,1)S(1)}, bf16[2,48,1408]{2,1,0:T(8,128)(2,1)S(1)}, u32[]{:S(2)}, u32[]{:S(2)}) %collective-permute-start.24) | collective-permute-done | bytes 270368 | tf_op jit(solution)/shard_map/ppermute | solution.py:601
  379.9 2.7 collective-permute-start.29
  382.6 7.1 %back.5 = f32[1024,768]{1,0:T(8,128)} custom-call(bf16[2048,768]{1,0:T(8,128)(2,1)S(1)} %get-tuple-element.263.refs_0_.refs_1_.refs_2_, bf16[2048,768]{1,0:T(8,128)(2,1)S(1)} %get-tuple-element.263.refs_0_.refs_1_.refs_2_, bf16[2048,768]{1,0:T(8,128)(2,1)S(1)} %copy-done.1, bf16[2048,768]{1,0:T(8,128)(2,1)S(1)} %copy-done.1, bf16[2,768,384]{2,1,0:T(8,128)(2,1)} %refs_5_.5, ...), custom_call_target="tpu_custom_call" | custom-call | flops 1048576 | bytes 1048576 | tf_op jit(solution)/shard_map/back/pallas_call | solution.py:421
  389.7 2.2 collective-permute-start.34
  395.2 15.2 %collective-permute-done.34 = bf16[4,48,2048]{2,1,0:T(8,128)(2,1)S(1)} collective-permute-done((bf16[4,48,2048]{2,1,0:T(8,128)(2,1)S(1)}, bf16[4,48,2048]{2,1,0:T(8,128)(2,1)S(1)}, u32[]{:S(2)}, u32[]{:S(2)}) %collective-permute-start.34) | collective-permute-done | bytes 786464 | tf_op jit(solution)/shard_map/ppermute | solution.py:601
  414.9 7.0 %collective-permute-done.33 = bf16[4,48,1408]{2,1,0:T(8,128)(2,1)S(1)} collective-permute-done((bf16[4,48,1408]{2,1,0:T(8,128)(2,1)S(1)}, bf16[4,48,1408]{2,1,0:T(8,128)(2,1)S(1)}, u32[]{:S(2)}, u32[]{:S(2)}) %collective-permute-start.33) | collective-permute-done | bytes 540704 | tf_op jit(solution)/shard_map/ppermute | solution.py:601
  424.9 5.7 %collective-permute-done.31 = bf16[4,48,1280]{2,1,0:T(8,128)(2,1)S(1)} collective-permute-done((bf16[4,48,1280]{2,1,0:T(8,128)(2,1)S(1)}, bf16[4,48,1280]{2,1,0:T(8,128)(2,1)S(1)}, u32[]{:S(2)}, u32[]{:S(2)}) %collective-permute-start.31) | collective-permute-done | bytes 491552 | tf_op jit(solution)/shard_map/ppermute | solution.py:601
  431.1 2.6 collective-permute-done.36
  433.9 4.6 arrange.8
  439.7 3.5 arrange.9
  443.2 2.4 copy.27
  445.6 2.5 collective-permute-start.38
  448.6 4.9 collective-permute-done.38
  454.7 3.2 collective-permute-done.42
  460.1 2.6 collective-permute-start.41
  462.7 5.3 %collective-permute-done.41 = bf16[1,48,1280]{2,1,0:T(8,128)(2,1)S(1)} collective-permute-done((bf16[1,48,1280]{2,1,0:T(8,128)(2,1)S(1)}, bf16[1,48,1280]{2,1,0:T(8,128)(2,1)S(1)}, u32[]{:S(2)}, u32[]{:S(2)}) %collective-permute-start.41) | collective-permute-done | bytes 122912 | tf_op jit(solution)/shard_map/ppermute | solution.py:601
  468.1 4.9 collective-permute-done.44
  473.2 2.3 collective-permute-done.43
  476.0 11.4 %collective-permute-done.45 = bf16[4,48,1280]{2,1,0:T(8,128)(2,1)S(1)} collective-permute-done((bf16[4,48,1280]{2,1,0:T(8,128)(2,1)S(1)}, bf16[4,48,1280]{2,1,0:T(8,128)(2,1)S(1)}, u32[]{:S(2)}, u32[]{:S(2)}) %collective-permute-start.45) | collective-permute-done | bytes 491552 | tf_op jit(solution)/shard_map/ppermute | solution.py:601
  487.6 4.1 arrange.10
  491.7 2.6 collective-permute-done.47.theirs_ref
  494.3 3.9 arrange.11
  (573 shorter events, 150.0 us)
Async XLA Ops:
  7.2 139.6 %all-gather.5.cloned.1.call-start = ((), (), s32[]{:S(2)}) async-start(), calls=%async_computation.1 | async-start | bytes 1671168 | tf_op jit(solution)/shard_map/all_gather | solution.py:863
  8.3 22.1 %collective-permute-start = (bf16[256,768]{1,0:T(8,128)(2,1)S(1)}, bf16[256,768]{1,0:T(8,128)(2,1)S(1)}, u32[]{:S(2)}, u32[]{:S(2)}) collective-permute-start(bf16[256,768]{1,0:T(8,128)(2,1)S(1)} %slice_bitcast_fusion), channel_id=1, source_target_pairs={{0,1},{2,3},{4,5},{6,7},{8,9},{10,11},{12,13},{14,15},{16,17},{18,... | collective-permute-start | bytes 1179656 | tf_op jit(solution)/shard_map/ppermute | solution.py:844
  14.3 16.1 %copy-start.105 = (bf16[1,512,768]{2,1,0:T(8,128)(2,1)S(1)}, bf16[1,512,768]{2,1,0:T(8,128)(2,1)}, u32[]{:S(2)}) copy-start(bf16[1,512,768]{2,1,0:T(8,128)(2,1)} %param.14) | copy-start | bytes 2359300
  14.3 17.8 %collective-permute-start.1 = (bf16[1,192,1152]{2,1,0:T(8,128)(2,1)S(1)}, bf16[1,192,1152]{2,1,0:T(8,128)(2,1)}, u32[]{:S(2)}, u32[]{:S(2)}) collective-permute-start(bf16[1,192,1152]{2,1,0:T(8,128)(2,1)S(1)} %pad_maximum_fusion.16), channel_id=1, source_target_pairs={{0,1},{1,0},{2,3},{3,2},{4,5},{5,4},{6,7},{7,6},{8,9},{9,8},{10,11... | collective-permute-start | bytes 1327112 | tf_op jit(solution)/shard_map/ppermute | solution.py:598
  16.1 20.2 %collective-permute-start.2 = (bf16[48,2048]{1,0:T(8,128)(2,1)}, bf16[48,2048]{1,0:T(8,128)(2,1)S(1)}, u32[]{:S(2)}, u32[]{:S(2)}) collective-permute-start(bf16[48,2048]{1,0:T(8,128)(2,1)} %pad_maximum_fusion.21), channel_id=1, source_target_pairs={{0,1},{1,0},{2,3},{3,2},{4,5},{5,4},{6,7},{7,6},{8,9},{9,8},{10,11... | collective-permute-start | bytes 589832 | tf_op jit(solution)/shard_map/ppermute | solution.py:598
  19.6 17.8 %collective-permute-start.3 = (bf16[64,768]{1,0:T(8,128)(2,1)}, bf16[64,768]{1,0:T(8,128)(2,1)S(1)}, u32[]{:S(2)}, u32[]{:S(2)}) collective-permute-start(bf16[64,768]{1,0:T(8,128)(2,1)} %dynamic-slice_bitcast_fusion.7), channel_id=1, source_target_pairs={{0,1},{1,0},{2,3},{3,2},{4,5},{5,4},{6,7},{7,6},{8,9},{9,8},{10,11... | collective-permute-start | bytes 294920 | tf_op jit(solution)/shard_map/ppermute | solution.py:598
  31.1 43.8 %copy-start.13 = (bf16[768,768]{1,0:T(8,128)(2,1)}, bf16[768,768]{1,0:T(8,128)(2,1)S(1)}, u32[]{:S(2)}) copy-start(bf16[768,768]{1,0:T(8,128)(2,1)S(1)} %fusion.2.refs_0_) | copy-start | bytes 3538948
  41.4 11.7 %collective-permute-start.4 = (bf16[1,192,1152]{2,1,0:T(8,128)(2,1)}, bf16[1,192,1152]{2,1,0:T(8,128)(2,1)}, u32[]{:S(2)}, u32[]{:S(2)}) collective-permute-start(bf16[1,192,1152]{2,1,0:T(8,128)(2,1)} %collective-permute-done.1), channel_id=1, source_target_pairs={{0,4},{2,6},{4,0},{6,2},{8,12},{10,14},{12,8},{14,10},{16,20},{18,... | collective-permute-start | bytes 1327112 | tf_op jit(solution)/shard_map/ppermute | solution.py:601
  42.9 20.1 %collective-permute-start.6 = (bf16[1,192,1920]{2,1,0:T(8,128)(2,1)}, bf16[1,192,1920]{2,1,0:T(8,128)(2,1)}, u32[]{:S(2)}, u32[]{:S(2)}) collective-permute-start(bf16[1,192,1920]{2,1,0:T(8,128)(2,1)} %bitcast_dynamic-update-slice_fusion), channel_id=1, source_target_pairs={{0,1},{1,0},{2,3},{3,2},{4,5},{5,4},{6,7},{7,6},{8,9},{9,8},{10,11... | collective-permute-start | bytes 2211848 | tf_op jit(solution)/shard_map/ppermute | solution.py:598
  47.2 99.5 %all-gather.3.cloned.1.call-start = ((), (), s32[]{:S(2)}) async-start(), calls=%async_computation | async-start | bytes 3342336 | tf_op jit(solution)/shard_map/all_gather | solution.py:861
  54.1 17.0 %collective-permute-start.5 = (bf16[2,192,1152]{2,1,0:T(8,128)(2,1)S(1)}, bf16[2,192,1152]{2,1,0:T(8,128)(2,1)S(1)}, u32[]{:S(2)}, u32[]{:S(2)}) collective-permute-start(bf16[2,192,1152]{2,1,0:T(8,128)(2,1)S(1)} %constant_dynamic-update-slice_fusion.mine_ref), channel_id=1, source_target_pairs={{0,2},{2,0},{4,6},{6,4},{8,10},{10,8},{12,14},{14,12},{16,18},{18,... | collective-permute-start | bytes 2654216 | tf_op jit(solution)/shard_map/ppermute | solution.py:601
  54.3 40.4 %collective-permute-start.9 = (bf16[1024,768]{1,0:T(8,128)(2,1)}, bf16[1024,768]{1,0:T(8,128)(2,1)}, u32[]{:S(2)}, u32[]{:S(2)}) collective-permute-start(bf16[1024,768]{1,0:T(8,128)(2,1)} %bitcast.24.refs_0_), channel_id=1, source_target_pairs={{0,1},{1,0},{2,3},{3,2},{4,5},{5,4},{6,7},{7,6},{8,9},{9,8},{10,11... | collective-permute-start | bytes 4718600 | tf_op jit(solution)/shard_map/ppermute | solution.py:598
  63.0 18.8 %collective-permute-start.7 = (bf16[1,192,1920]{2,1,0:T(8,128)(2,1)}, bf16[1,192,1920]{2,1,0:T(8,128)(2,1)S(1)}, u32[]{:S(2)}, u32[]{:S(2)}) collective-permute-start(bf16[1,192,1920]{2,1,0:T(8,128)(2,1)} %collective-permute-done.6), channel_id=1, source_target_pairs={{0,4},{2,6},{4,0},{6,2},{8,12},{10,14},{12,8},{14,10},{16,20},{18,... | collective-permute-start | bytes 2211848 | tf_op jit(solution)/shard_map/ppermute | solution.py:601
  80.1 15.2 %copy-start.17 = (bf16[512,384]{1,0:T(8,128)(2,1)}, bf16[512,384]{1,0:T(8,128)(2,1)S(1)}, u32[]{:S(2)}) copy-start(bf16[512,384]{1,0:T(8,128)(2,1)S(1)} %get-tuple-element.180.refs_0_.out_ref) | copy-start | bytes 1179652
  81.9 3.5 collective-permute-start.8
  87.6 49.3 %copy-start.65 = (bf16[2,192,768]{2,1,0:T(8,128)(2,1)}, bf16[2,192,768]{2,1,0:T(8,128)(2,1)S(1)}, u32[]{:S(2)}) copy-start(bf16[2,192,768]{2,1,0:T(8,128)(2,1)S(1)} %get-tuple-element.177) | copy-start | bytes 1769476
  97.7 39.2 %copy-start.8 = (f32[512,768]{1,0:T(8,128)}, f32[512,768]{1,0:T(8,128)S(1)}, u32[]{:S(2)}) copy-start(f32[512,768]{1,0:T(8,128)S(1)} %get-tuple-element.300.refs_4_) | copy-start | bytes 4718596
  100.4 25.4 %copy-start.77 = (bf16[512,384]{1,0:T(8,128)(2,1)}, bf16[512,384]{1,0:T(8,128)(2,1)S(1)}, u32[]{:S(2)}) copy-start(bf16[512,384]{1,0:T(8,128)(2,1)S(1)} %convolution_convert_fusion.14.q_ref) | copy-start | bytes 1179652
  102.9 22.9 %copy-start.31 = (bf16[1024,384]{1,0:T(8,128)(2,1)}, bf16[1024,384]{1,0:T(8,128)(2,1)S(1)}, u32[]{:S(2)}) copy-start(bf16[1024,384]{1,0:T(8,128)(2,1)S(1)} %convolution_convert_fusion.5.refs_0_) | copy-start | bytes 2359300
  105.7 20.2 %copy-start.33 = (bf16[1024,384]{1,0:T(8,128)(2,1)}, bf16[1024,384]{1,0:T(8,128)(2,1)S(1)}, u32[]{:S(2)}) copy-start(bf16[1024,384]{1,0:T(8,128)(2,1)S(1)} %convolution_convert_fusion.4.refs_1_) | copy-start | bytes 2359300
  120.6 15.7 %copy-start.19 = (bf16[512,384]{1,0:T(8,128)(2,1)}, bf16[512,384]{1,0:T(8,128)(2,1)S(1)}, u32[]{:S(2)}) copy-start(bf16[512,384]{1,0:T(8,128)(2,1)S(1)} %get-tuple-element.186.refs_0_.out_ref) | copy-start | bytes 1179652
  138.7 25.9 %copy-start.6 = (f32[512,768]{1,0:T(8,128)}, f32[512,768]{1,0:T(8,128)S(1)}, u32[]{:S(2)}) copy-start(f32[512,768]{1,0:T(8,128)S(1)} %get-tuple-element.298.refs_8_) | copy-start | bytes 4718596
  176.8 26.4 %collective-permute-start.10 = (bf16[16,48,1408]{2,1,0:T(8,128)(2,1)}, bf16[16,48,1408]{2,1,0:T(8,128)(2,1)}, u32[]{:S(2)}, u32[]{:S(2)}) collective-permute-start(bf16[16,48,1408]{2,1,0:T(8,128)(2,1)} %maximum_maximum_fusion.1), channel_id=1, source_target_pairs={{0,2},{2,0},{4,6},{6,4},{8,10},{10,8},{12,14},{14,12},{16,18},{18,... | collective-permute-start | bytes 6488072 | tf_op jit(solution)/shard_map/ppermute | solution.py:601
  176.8 28.7 %collective-permute-start.11 = (bf16[16,48,2048]{2,1,0:T(8,128)(2,1)}, bf16[16,48,2048]{2,1,0:T(8,128)(2,1)}, u32[]{:S(2)}, u32[]{:S(2)}) collective-permute-start(bf16[16,48,2048]{2,1,0:T(8,128)(2,1)} %pad_maximum_fusion), channel_id=1, source_target_pairs={{0,2},{2,0},{4,6},{6,4},{8,10},{10,8},{12,14},{14,12},{16,18},{18,... | collective-permute-start | bytes 9437192 | tf_op jit(solution)/shard_map/ppermute | solution.py:601
  205.4 27.4 %collective-permute-start.13 = (bf16[8,48,1408]{2,1,0:T(8,128)(2,1)S(1)}, bf16[8,48,1408]{2,1,0:T(8,128)(2,1)S(1)}, u32[]{:S(2)}, u32[]{:S(2)}) collective-permute-start(bf16[8,48,1408]{2,1,0:T(8,128)(2,1)S(1)} %pad_maximum_fusion.5), channel_id=1, source_target_pairs={{0,4},{2,6},{4,0},{6,2},{8,12},{10,14},{12,8},{14,10},{16,20},{18,... | collective-permute-start | bytes 3244040 | tf_op jit(solution)/shard_map/ppermute | solution.py:601
  209.0 35.5 %collective-permute-start.12 = (bf16[8,48,2048]{2,1,0:T(8,128)(2,1)S(1)}, bf16[8,48,2048]{2,1,0:T(8,128)(2,1)S(1)}, u32[]{:S(2)}, u32[]{:S(2)}) collective-permute-start(bf16[8,48,2048]{2,1,0:T(8,128)(2,1)S(1)} %add_convert_fusion), channel_id=1, source_target_pairs={{0,1},{1,0},{2,3},{3,2},{4,5},{5,4},{6,7},{7,6},{8,9},{9,8},{10,11... | collective-permute-start | bytes 4718600 | tf_op jit(solution)/shard_map/ppermute | solution.py:598
  215.4 29.6 %copy-start.88 = (bf16[1,2,2,192,384]{4,3,2,1,0:T(8,128)(2,1)S(1)}, bf16[1,2,2,192,384]{4,3,2,1,0:T(8,128)(2,1)}, u32[]{:S(2)}) copy-start(bf16[1,2,2,192,384]{4,3,2,1,0:T(8,128)(2,1)} %copy-done.87) | copy-start | bytes 1769476
  230.1 25.7 %copy-start = (bf16[2048,768]{1,0:T(8,128)(2,1)}, bf16[2048,768]{1,0:T(8,128)(2,1)S(1)}, u32[]{:S(2)}) copy-start(bf16[2048,768]{1,0:T(8,128)(2,1)S(1)} %get-tuple-element.264.refs_2_.refs_3_) | copy-start | bytes 9437188
  269.7 39.5 %collective-permute-start.18 = (bf16[16,48,1536]{2,1,0:T(8,128)(2,1)S(1)}, bf16[16,48,1536]{2,1,0:T(8,128)(2,1)S(1)}, u32[]{:S(2)}, u32[]{:S(2)}) collective-permute-start(bf16[16,48,1536]{2,1,0:T(8,128)(2,1)S(1)} %maximum_maximum_fusion), channel_id=1, source_target_pairs={{0,2},{2,0},{4,6},{6,4},{8,10},{10,8},{12,14},{14,12},{16,18},{18,... | collective-permute-start | bytes 7077896 | tf_op jit(solution)/shard_map/ppermute | solution.py:601
  272.2 15.1 %collective-permute-start.14 = (bf16[4,48,1408]{2,1,0:T(8,128)(2,1)S(1)}, bf16[4,48,1408]{2,1,0:T(8,128)(2,1)S(1)}, u32[]{:S(2)}, u32[]{:S(2)}) collective-permute-start(bf16[4,48,1408]{2,1,0:T(8,128)(2,1)S(1)} %add_convert_fusion.6), channel_id=1, source_target_pairs={{0,1},{1,0},{2,3},{3,2},{4,5},{5,4},{6,7},{7,6},{8,9},{9,8},{10,11... | collective-permute-start | bytes 1622024 | tf_op jit(solution)/shard_map/ppermute | solution.py:598
  272.6 19.7 %collective-permute-start.15 = (bf16[4,48,2048]{2,1,0:T(8,128)(2,1)S(1)}, bf16[4,48,2048]{2,1,0:T(8,128)(2,1)S(1)}, u32[]{:S(2)}, u32[]{:S(2)}) collective-permute-start(bf16[4,48,2048]{2,1,0:T(8,128)(2,1)S(1)} %add_convert_fusion.2), channel_id=1, source_target_pairs={{0,4},{2,6},{4,0},{6,2},{8,12},{10,14},{12,8},{14,10},{16,20},{18,... | collective-permute-start | bytes 2359304 | tf_op jit(solution)/shard_map/ppermute | solution.py:601
  272.8 107.0 %collective-permute-start.27 = (bf16[1024,768]{1,0:T(8,128)(2,1)}, bf16[1024,768]{1,0:T(8,128)(2,1)}, u32[]{:S(2)}, u32[]{:S(2)}) collective-permute-start(bf16[1024,768]{1,0:T(8,128)(2,1)} %back.3), channel_id=1, source_target_pairs={{0,1},{1,0},{2,3},{3,2},{4,5},{5,4},{6,7},{7,6},{8,9},{9,8},{10,11... | collective-permute-start | bytes 4718600 | tf_op jit(solution)/shard_map/ppermute | solution.py:598
  292.6 11.1 %collective-permute-start.16 = (bf16[2,48,1408]{2,1,0:T(8,128)(2,1)S(1)}, bf16[2,48,1408]{2,1,0:T(8,128)(2,1)S(1)}, u32[]{:S(2)}, u32[]{:S(2)}) collective-permute-start(bf16[2,48,1408]{2,1,0:T(8,128)(2,1)S(1)} %add_convert_fusion.12), channel_id=1, source_target_pairs={{0,8},{2,10},{4,12},{6,14},{8,0},{10,2},{12,4},{14,6},{16,24},{18,... | collective-permute-start | bytes 811016 | tf_op jit(solution)/shard_map/ppermute | solution.py:601
  293.3 15.7 %collective-permute-start.17 = (bf16[2,48,2048]{2,1,0:T(8,128)(2,1)S(1)}, bf16[2,48,2048]{2,1,0:T(8,128)(2,1)S(1)}, u32[]{:S(2)}, u32[]{:S(2)}) collective-permute-start(bf16[2,48,2048]{2,1,0:T(8,128)(2,1)S(1)} %add_convert_fusion.10), channel_id=1, source_target_pairs={{0,8},{2,10},{4,12},{6,14},{8,0},{10,2},{12,4},{14,6},{16,24},{18,... | collective-permute-start | bytes 1179656 | tf_op jit(solution)/shard_map/ppermute | solution.py:601
  311.9 14.0 %collective-permute-start.19 = (bf16[1,48,1408]{2,1,0:T(8,128)(2,1)S(1)}, bf16[1,48,1408]{2,1,0:T(8,128)(2,1)S(1)}, u32[]{:S(2)}, u32[]{:S(2)}) collective-permute-start(bf16[1,48,1408]{2,1,0:T(8,128)(2,1)S(1)} %add_convert_fusion.19), channel_id=1, source_target_pairs={{0,16},{2,18},{4,20},{6,22},{8,24},{10,26},{12,28},{14,30},{16,0},... | collective-permute-start | bytes 405512 | tf_op jit(solution)/shard_map/ppermute | solution.py:601
  317.0 12.0 %collective-permute-start.20 = (bf16[1,48,2048]{2,1,0:T(8,128)(2,1)S(1)}, bf16[1,48,2048]{2,1,0:T(8,128)(2,1)S(1)}, u32[]{:S(2)}, u32[]{:S(2)}) collective-permute-start(bf16[1,48,2048]{2,1,0:T(8,128)(2,1)S(1)} %add_convert_fusion.15), channel_id=1, source_target_pairs={{0,16},{2,18},{4,20},{6,22},{8,24},{10,26},{12,28},{14,30},{16,0},... | collective-permute-start | bytes 589832 | tf_op jit(solution)/shard_map/ppermute | solution.py:601
  317.0 40.6 %collective-permute-start.23 = (bf16[8,48,1536]{2,1,0:T(8,128)(2,1)}, bf16[8,48,1536]{2,1,0:T(8,128)(2,1)}, u32[]{:S(2)}, u32[]{:S(2)}) collective-permute-start(bf16[8,48,1536]{2,1,0:T(8,128)(2,1)} %pad_maximum_fusion.3), channel_id=1, source_target_pairs={{0,4},{2,6},{4,0},{6,2},{8,12},{10,14},{12,8},{14,10},{16,20},{18,... | collective-permute-start | bytes 3538952 | tf_op jit(solution)/shard_map/ppermute | solution.py:601
  329.2 27.4 %collective-permute-start.22 = (bf16[1,48,2048]{2,1,0:T(8,128)(2,1)S(1)}, bf16[1,48,2048]{2,1,0:T(8,128)(2,1)}, u32[]{:S(2)}, u32[]{:S(2)}) collective-permute-start(bf16[1,48,2048]{2,1,0:T(8,128)(2,1)S(1)} %add_convert_fusion.14), channel_id=1, source_target_pairs={{0,16},{2,18},{4,20},{6,22},{8,24},{10,26},{12,28},{14,30},{16,0},... | collective-permute-start | bytes 589832 | tf_op jit(solution)/shard_map/ppermute | solution.py:601
  329.3 26.2 %collective-permute-start.21 = (bf16[1,48,1408]{2,1,0:T(8,128)(2,1)S(1)}, bf16[1,48,1408]{2,1,0:T(8,128)(2,1)}, u32[]{:S(2)}, u32[]{:S(2)}) collective-permute-start(bf16[1,48,1408]{2,1,0:T(8,128)(2,1)S(1)} %add_convert_fusion.18), channel_id=1, source_target_pairs={{0,16},{2,18},{4,20},{6,22},{8,24},{10,26},{12,28},{14,30},{16,0},... | collective-permute-start | bytes 405512 | tf_op jit(solution)/shard_map/ppermute | solution.py:601
  355.2 24.4 %collective-permute-start.26 = (bf16[16,48,1280]{2,1,0:T(8,128)(2,1)S(1)}, bf16[16,48,1280]{2,1,0:T(8,128)(2,1)S(1)}, u32[]{:S(2)}, u32[]{:S(2)}) collective-permute-start(bf16[16,48,1280]{2,1,0:T(8,128)(2,1)S(1)} %maximum_maximum_fusion.2), channel_id=1, source_target_pairs={{0,2},{2,0},{4,6},{6,4},{8,10},{10,8},{12,14},{14,12},{16,18},{18,... | collective-permute-start | bytes 5898248 | tf_op jit(solution)/shard_map/ppermute | solution.py:601
  358.9 19.3 %collective-permute-start.25 = (bf16[2,48,2048]{2,1,0:T(8,128)(2,1)S(1)}, bf16[2,48,2048]{2,1,0:T(8,128)(2,1)S(1)}, u32[]{:S(2)}, u32[]{:S(2)}) collective-permute-start(bf16[2,48,2048]{2,1,0:T(8,128)(2,1)S(1)} %pad_maximum_fusion.17), channel_id=1, source_target_pairs={{0,8},{2,10},{4,12},{6,14},{8,0},{10,2},{12,4},{14,6},{16,24},{18,... | collective-permute-start | bytes 1179656 | tf_op jit(solution)/shard_map/ppermute | solution.py:601
  359.4 16.6 %collective-permute-start.24 = (bf16[2,48,1408]{2,1,0:T(8,128)(2,1)S(1)}, bf16[2,48,1408]{2,1,0:T(8,128)(2,1)S(1)}, u32[]{:S(2)}, u32[]{:S(2)}) collective-permute-start(bf16[2,48,1408]{2,1,0:T(8,128)(2,1)S(1)} %pad_maximum_fusion.19), channel_id=1, source_target_pairs={{0,8},{2,10},{4,12},{6,14},{8,0},{10,2},{12,4},{14,6},{16,24},{18,... | collective-permute-start | bytes 811016 | tf_op jit(solution)/shard_map/ppermute | solution.py:601
  361.7 17.7 %collective-permute-start.30 = (bf16[4,48,1536]{2,1,0:T(8,128)(2,1)S(1)}, bf16[4,48,1536]{2,1,0:T(8,128)(2,1)S(1)}, u32[]{:S(2)}, u32[]{:S(2)}) collective-permute-start(bf16[4,48,1536]{2,1,0:T(8,128)(2,1)S(1)} %add_convert_fusion.3), channel_id=1, source_target_pairs={{0,1},{1,0},{2,3},{3,2},{4,5},{5,4},{6,7},{7,6},{8,9},{9,8},{10,11... | collective-permute-start | bytes 1769480 | tf_op jit(solution)/shard_map/ppermute | solution.py:598
  376.0 16.0 %collective-permute-start.28 = (bf16[256,768]{1,0:T(8,128)(2,1)S(1)}, bf16[256,768]{1,0:T(8,128)(2,1)S(1)}, u32[]{:S(2)}, u32[]{:S(2)}) collective-permute-start(bf16[256,768]{1,0:T(8,128)(2,1)S(1)} %copy-done.136), channel_id=1, source_target_pairs={{1,0},{3,2},{5,4},{7,6},{9,8},{11,10},{13,12},{15,14},{17,16},{19,... | collective-permute-start | bytes 1179656 | tf_op jit(solution)/shard_map/ppermute | solution.py:1022
  379.9 31.6 %collective-permute-start.29 = (bf16[8,48,1280]{2,1,0:T(8,128)(2,1)S(1)}, bf16[8,48,1280]{2,1,0:T(8,128)(2,1)S(1)}, u32[]{:S(2)}, u32[]{:S(2)}) collective-permute-start(bf16[8,48,1280]{2,1,0:T(8,128)(2,1)S(1)} %add_convert_fusion.1), channel_id=1, source_target_pairs={{0,1},{1,0},{2,3},{3,2},{4,5},{5,4},{6,7},{7,6},{8,9},{9,8},{10,11... | collective-permute-start | bytes 2949128 | tf_op jit(solution)/shard_map/ppermute | solution.py:598
  389.7 20.7 %collective-permute-start.34 = (bf16[4,48,2048]{2,1,0:T(8,128)(2,1)S(1)}, bf16[4,48,2048]{2,1,0:T(8,128)(2,1)S(1)}, u32[]{:S(2)}, u32[]{:S(2)}) collective-permute-start(bf16[4,48,2048]{2,1,0:T(8,128)(2,1)S(1)} %pad_maximum_fusion.8), channel_id=1, source_target_pairs={{0,4},{2,6},{4,0},{6,2},{8,12},{10,14},{12,8},{14,10},{16,20},{18,... | collective-permute-start | bytes 2359304 | tf_op jit(solution)/shard_map/ppermute | solution.py:601
  391.9 30.0 %collective-permute-start.33 = (bf16[4,48,1408]{2,1,0:T(8,128)(2,1)S(1)}, bf16[4,48,1408]{2,1,0:T(8,128)(2,1)S(1)}, u32[]{:S(2)}, u32[]{:S(2)}) collective-permute-start(bf16[4,48,1408]{2,1,0:T(8,128)(2,1)S(1)} %pad_maximum_fusion.14), channel_id=1, source_target_pairs={{0,4},{2,6},{4,0},{6,2},{8,12},{10,14},{12,8},{14,10},{16,20},{18,... | collective-permute-start | bytes 1622024 | tf_op jit(solution)/shard_map/ppermute | solution.py:601
  395.2 43.7 %copy-start.118 = (bf16[8,48,1280]{2,1,0:T(8,128)(2,1)}, bf16[8,48,1280]{2,1,0:T(8,128)(2,1)S(1)}, u32[]{:S(2)}) copy-start(bf16[8,48,1280]{2,1,0:T(8,128)(2,1)S(1)} %slice.218) | copy-start | bytes 2949124
  411.5 27.4 %copy-start.129 = (bf16[8,48,1280]{2,1,0:T(8,128)(2,1)}, bf16[8,48,1280]{2,1,0:T(8,128)(2,1)S(1)}, u32[]{:S(2)}) copy-start(bf16[8,48,1280]{2,1,0:T(8,128)(2,1)S(1)} %collective-permute-done.29) | copy-start | bytes 2949124
  411.7 22.2 %collective-permute-start.37 = (bf16[8,48,2048]{2,1,0:T(8,128)(2,1)S(1)}, bf16[8,48,2048]{2,1,0:T(8,128)(2,1)S(1)}, u32[]{:S(2)}, u32[]{:S(2)}) collective-permute-start(bf16[8,48,2048]{2,1,0:T(8,128)(2,1)S(1)} %pad_maximum_fusion.1.mine_ref), channel_id=1, source_target_pairs={{0,2},{2,0},{4,6},{6,4},{8,10},{10,8},{12,14},{14,12},{16,18},{18,... | collective-permute-start | bytes 4718600 | tf_op jit(solution)/shard_map/ppermute | solution.py:601
  412.4 10.7 %collective-permute-start.32 = (bf16[2,48,1536]{2,1,0:T(8,128)(2,1)S(1)}, bf16[2,48,1536]{2,1,0:T(8,128)(2,1)S(1)}, u32[]{:S(2)}, u32[]{:S(2)}) collective-permute-start(bf16[2,48,1536]{2,1,0:T(8,128)(2,1)S(1)} %add_convert_fusion.11), channel_id=1, source_target_pairs={{0,8},{2,10},{4,12},{6,14},{8,0},{10,2},{12,4},{14,6},{16,24},{18,... | collective-permute-start | bytes 884744 | tf_op jit(solution)/shard_map/ppermute | solution.py:601
  412.9 17.6 %collective-permute-start.31 = (bf16[4,48,1280]{2,1,0:T(8,128)(2,1)S(1)}, bf16[4,48,1280]{2,1,0:T(8,128)(2,1)S(1)}, u32[]{:S(2)}, u32[]{:S(2)}) collective-permute-start(bf16[4,48,1280]{2,1,0:T(8,128)(2,1)S(1)} %add_convert_fusion.9), channel_id=1, source_target_pairs={{0,4},{2,6},{4,0},{6,2},{8,12},{10,14},{12,8},{14,10},{16,20},{18,... | collective-permute-start | bytes 1474568 | tf_op jit(solution)/shard_map/ppermute | solution.py:601
  423.0 16.6 %collective-permute-start.40 = (bf16[8,48,1408]{2,1,0:T(8,128)(2,1)S(1)}, bf16[8,48,1408]{2,1,0:T(8,128)(2,1)S(1)}, u32[]{:S(2)}, u32[]{:S(2)}) collective-permute-start(bf16[8,48,1408]{2,1,0:T(8,128)(2,1)S(1)} %pad_maximum_fusion.6.mine_ref), channel_id=1, source_target_pairs={{0,2},{2,0},{4,6},{6,4},{8,10},{10,8},{12,14},{14,12},{16,18},{18,... | collective-permute-start | bytes 3244040 | tf_op jit(solution)/shard_map/ppermute | solution.py:601
  423.3 10.5 %collective-permute-start.36 = (bf16[1,48,1536]{2,1,0:T(8,128)(2,1)S(1)}, bf16[1,48,1536]{2,1,0:T(8,128)(2,1)S(1)}, u32[]{:S(2)}, u32[]{:S(2)}) collective-permute-start(bf16[1,48,1536]{2,1,0:T(8,128)(2,1)S(1)} %add_convert_fusion.17), channel_id=1, source_target_pairs={{0,16},{2,18},{4,20},{6,22},{8,24},{10,26},{12,28},{14,30},{16,0},... | collective-permute-start | bytes 442376 | tf_op jit(solution)/shard_map/ppermute | solution.py:601
  430.7 8.2 %collective-permute-start.35 = (bf16[2,48,1280]{2,1,0:T(8,128)(2,1)S(1)}, bf16[2,48,1280]{2,1,0:T(8,128)(2,1)S(1)}, u32[]{:S(2)}, u32[]{:S(2)}) collective-permute-start(bf16[2,48,1280]{2,1,0:T(8,128)(2,1)S(1)} %add_convert_fusion.13), channel_id=1, source_target_pairs={{0,8},{2,10},{4,12},{6,14},{8,0},{10,2},{12,4},{14,6},{16,24},{18,... | collective-permute-start | bytes 737288 | tf_op jit(solution)/shard_map/ppermute | solution.py:601
  438.5 9.6 %collective-permute-start.39 = (bf16[1,48,1536]{2,1,0:T(8,128)(2,1)S(1)}, bf16[1,48,1536]{2,1,0:T(8,128)(2,1)S(1)}, u32[]{:S(2)}, u32[]{:S(2)}) collective-permute-start(bf16[1,48,1536]{2,1,0:T(8,128)(2,1)S(1)} %add_convert_fusion.16), channel_id=1, source_target_pairs={{0,16},{2,18},{4,20},{6,22},{8,24},{10,26},{12,28},{14,30},{16,0},... | collective-permute-start | bytes 442376 | tf_op jit(solution)/shard_map/ppermute | solution.py:601
  445.6 7.9 %collective-permute-start.38 = (bf16[1,48,1280]{2,1,0:T(8,128)(2,1)}, bf16[1,48,1280]{2,1,0:T(8,128)(2,1)S(1)}, u32[]{:S(2)}, u32[]{:S(2)}) collective-permute-start(bf16[1,48,1280]{2,1,0:T(8,128)(2,1)} %add_convert_fusion.21), channel_id=1, source_target_pairs={{0,16},{2,18},{4,20},{6,22},{8,24},{10,26},{12,28},{14,30},{16,0},... | collective-permute-start | bytes 368648 | tf_op jit(solution)/shard_map/ppermute | solution.py:601
  448.1 9.8 %collective-permute-start.42 = (bf16[2,48,1536]{2,1,0:T(8,128)(2,1)S(1)}, bf16[2,48,1536]{2,1,0:T(8,128)(2,1)S(1)}, u32[]{:S(2)}, u32[]{:S(2)}) collective-permute-start(bf16[2,48,1536]{2,1,0:T(8,128)(2,1)S(1)} %pad_maximum_fusion.18), channel_id=1, source_target_pairs={{0,8},{2,10},{4,12},{6,14},{8,0},{10,2},{12,4},{14,6},{16,24},{18,... | collective-permute-start | bytes 884744 | tf_op jit(solution)/shard_map/ppermute | solution.py:601
  457.9 15.1 %collective-permute-start.44 = (bf16[4,48,1536]{2,1,0:T(8,128)(2,1)S(1)}, bf16[4,48,1536]{2,1,0:T(8,128)(2,1)S(1)}, u32[]{:S(2)}, u32[]{:S(2)}) collective-permute-start(bf16[4,48,1536]{2,1,0:T(8,128)(2,1)S(1)} %pad_maximum_fusion.13), channel_id=1, source_target_pairs={{0,4},{2,6},{4,0},{6,2},{8,12},{10,14},{12,8},{14,10},{16,20},{18,... | collective-permute-start | bytes 1769480 | tf_op jit(solution)/shard_map/ppermute | solution.py:601
  460.1 7.9 %collective-permute-start.41 = (bf16[1,48,1280]{2,1,0:T(8,128)(2,1)S(1)}, bf16[1,48,1280]{2,1,0:T(8,128)(2,1)S(1)}, u32[]{:S(2)}, u32[]{:S(2)}) collective-permute-start(bf16[1,48,1280]{2,1,0:T(8,128)(2,1)S(1)} %add_convert_fusion.20), channel_id=1, source_target_pairs={{0,16},{2,18},{4,20},{6,22},{8,24},{10,26},{12,28},{14,30},{16,0},... | collective-permute-start | bytes 368648 | tf_op jit(solution)/shard_map/ppermute | solution.py:601
  468.0 7.5 %collective-permute-start.43 = (bf16[2,48,1280]{2,1,0:T(8,128)(2,1)S(1)}, bf16[2,48,1280]{2,1,0:T(8,128)(2,1)S(1)}, u32[]{:S(2)}, u32[]{:S(2)}) collective-permute-start(bf16[2,48,1280]{2,1,0:T(8,128)(2,1)S(1)} %pad_maximum_fusion.20), channel_id=1, source_target_pairs={{0,8},{2,10},{4,12},{6,14},{8,0},{10,2},{12,4},{14,6},{16,24},{18,... | collective-permute-start | bytes 737288 | tf_op jit(solution)/shard_map/ppermute | solution.py:601
  473.1 14.4 %collective-permute-start.46 = (bf16[8,48,1536]{2,1,0:T(8,128)(2,1)S(1)}, bf16[8,48,1536]{2,1,0:T(8,128)(2,1)S(1)}, u32[]{:S(2)}, u32[]{:S(2)}) collective-permute-start(bf16[8,48,1536]{2,1,0:T(8,128)(2,1)S(1)} %pad_maximum_fusion.4.mine_ref), channel_id=1, source_target_pairs={{0,2},{2,0},{4,6},{6,4},{8,10},{10,8},{12,14},{14,12},{16,18},{18,... | collective-permute-start | bytes 3538952 | tf_op jit(solution)/shard_map/ppermute | solution.py:601
  475.6 11.9 %collective-permute-start.45 = (bf16[4,48,1280]{2,1,0:T(8,128)(2,1)S(1)}, bf16[4,48,1280]{2,1,0:T(8,128)(2,1)S(1)}, u32[]{:S(2)}, u32[]{:S(2)}) collective-permute-start(bf16[4,48,1280]{2,1,0:T(8,128)(2,1)S(1)} %pad_maximum_fusion.15), channel_id=1, source_target_pairs={{0,4},{2,6},{4,0},{6,2},{8,12},{10,14},{12,8},{14,10},{16,20},{18,... | collective-permute-start | bytes 1474568 | tf_op jit(solution)/shard_map/ppermute | solution.py:601
  491.7 2.6 collective-permute-start.47
  (153 other events, 849.9 us)
Sparse Core Ops, SparseCore 0:
  47.3 40.1 all-gather.4
  90.4 44.2 all-gather.2
